TPU v7x, 32 devices: a whole 2x2x4 slice. The times are simulated.
32 devices in a mesh: img: 2 (over x), rows: 16 (over z, y, core).
Axes of the slice: x: 2, y: 2, z: 4, core: 2. Of those that a mesh axis runs over, the one named last changes fastest.
Arguments:
- hidden_states: bfloat16 [3, 4096, 1024], P(None, ('img', 'rows')), parts along dimension 1, may hold values from -6 to 6
- cell_of: int32 [2048], replicated, may hold values from 0 to 2047, as said below
- proj_four_weight: bfloat16 [1024, 256], replicated, may hold values from -0.1875 to 0.1875
- proj_four_bias: float32 [256], replicated, may hold values from -3 to 3
- proj_two_weight: bfloat16 [1024, 512], replicated, may hold values from -0.1875 to 0.1875
- proj_two_bias: float32 [512], replicated, may hold values from -3 to 3
- proj_same_weight: bfloat16 [1024, 1024], replicated, may hold values from -0.1875 to 0.1875
- proj_same_bias: float32 [1024], replicated, may hold values from -3 to 3
- up4_weight: bfloat16 [256, 4096], replicated, may hold values from -0.375 to 0.375
- up4_bias: float32 [256], replicated, may hold values from -3 to 3
- up2_weight: bfloat16 [512, 2048], replicated, may hold values from -0.25 to 0.25
- up2_bias: float32 [512], replicated, may hold values from -3 to 3
- join_weight: bfloat16 [3, 3, 256, 256], replicated, may hold values from -0.125 to 0.125
Outputs:
- joined_four: bfloat16 [256, 256, 256], P(('img', 'rows')), parts along dimension 0
- upsampled_two: bfloat16 [128, 128, 512], P(('img', 'rows')), parts along dimension 0
- same_scale: bfloat16 [64, 64, 1024], P(('img', 'rows')), parts along dimension 0
There are 2 independent parts, one for each index of `img`. A program takes and returns all parts, laid end to end along the dimension named above; an argument that names none is the same for every part. Nothing has to cross between parts.
Inputs may be any that keep to these rules, and one draw needn't show every extreme that they name: `cell_of`: a permutation of the cells 0 to 2047; the sequence positions k * 128 to (k + 1) * 128 - 1 hold exactly 8 cells of every block of 128 consecutive cells.
All inputs are finite; a program needn't handle non-finite values.
Results may differ from a plain program's by a relative error of at most 0.0057.
Values may be sent and summed in bfloat16 or wider, within the bound.
No kernel may reach another device: no remote copies, remote signals or barrier semaphores. Data moves between devices by JAX's collectives and lax.ppermute only.
A program may use at most 64 MiB of HBM per device.

v0:
```python
import jax
import jax.numpy as jnp
from jax import lax
from jax.sharding import PartitionSpec as P

GRID_W = 64


def with_halo(cells, sides, width):
    for axis, dim in sides:
        count = lax.axis_size(axis)
        ends = count - 1
        head = lax.slice_in_dim(cells, 0, width, axis=dim)
        tail = lax.slice_in_dim(cells, cells.shape[dim] - width, cells.shape[dim], axis=dim)
        cells = jnp.concatenate(
            [
                lax.ppermute(tail, axis, [(i, (i + 1) % count) for i in range(ends)]),
                cells,
                lax.ppermute(head, axis, [((i + 1) % count, i) for i in range(ends)]),
            ],
            axis=dim,
        )
    return cells


def expand(proj, weight, bias_row, factor):
    height, columns, channels = proj.shape
    out_channels = weight.shape[1] // (factor * factor)
    flattened = jnp.dot(proj.reshape(-1, channels), weight, preferred_element_type=jnp.float32)
    flattened = flattened + jnp.tile(bias_row, factor * factor)[None, :]
    result = flattened.astype(jnp.bfloat16).reshape(height, columns, factor, factor, out_channels)
    return result.transpose(0, 2, 1, 3, 4).reshape(height * factor, columns * factor, out_channels)


def convolve(padded, weight, out_rows, out_cols):
    channels = padded.shape[2]
    total = jnp.zeros((out_rows, out_cols, weight.shape[3]), jnp.float32)
    for row_tap in range(3):
        for col_tap in range(3):
            window = padded[row_tap : row_tap + out_rows, col_tap : col_tap + out_cols]
            term = jnp.dot(
                window.reshape(-1, channels),
                weight[row_tap, col_tap],
                preferred_element_type=jnp.float32,
            )
            total = total + term.reshape(out_rows, out_cols, -1)
    return total.astype(jnp.bfloat16)


def project_one(tokens_block, weight, bias_row):
    projected = jnp.dot(tokens_block, weight, preferred_element_type=jnp.float32) + bias_row
    return projected.astype(jnp.bfloat16)


def body(
    hidden_states,
    cell_of,
    proj_four_weight,
    proj_four_bias,
    proj_two_weight,
    proj_two_bias,
    proj_same_weight,
    proj_same_bias,
    up4_weight,
    up4_bias,
    up2_weight,
    up2_bias,
    join_weight,
):
    tok_dev = hidden_states.shape[1]
    shards = lax.axis_size("rows")
    myself = lax.axis_index("rows")
    per_peer = tok_dev // shards
    my_cells = lax.dynamic_slice_in_dim(cell_of, myself * tok_dev, tok_dev)
    outgoing = jnp.argsort(my_cells // tok_dev, stable=True)
    table = cell_of.reshape(shards, tok_dev)
    foreign = (table // tok_dev != myself).astype(jnp.int32)
    picked = jnp.argsort(foreign, axis=1, stable=True)[:, :per_peer]
    arriving = jnp.take_along_axis(table, picked, axis=1).reshape(-1) - myself * tok_dev
    placing = jnp.argsort(arriving)
    pairs = (
        (proj_four_weight, proj_four_bias),
        (proj_two_weight, proj_two_bias),
        (proj_same_weight, proj_same_bias),
    )
    local_four = project_one(hidden_states[0][outgoing], pairs[0][0], pairs[0][1])
    local_two = project_one(hidden_states[1][outgoing], pairs[1][0], pairs[1][1])
    local_same = project_one(hidden_states[2][outgoing], pairs[2][0], pairs[2][1])
    arrived = (
        lax.all_to_all(local_four, "rows", split_axis=0, concat_axis=0, tiled=True),
        lax.all_to_all(local_two, "rows", split_axis=0, concat_axis=0, tiled=True),
        lax.all_to_all(local_same, "rows", split_axis=0, concat_axis=0, tiled=True),
    )
    tiles = [piece[placing] for piece in arrived]
    row_count = tok_dev // GRID_W
    upsampled_four = expand(tiles[0].reshape(row_count, GRID_W, -1), up4_weight, up4_bias, 4)
    rimmed = with_halo(upsampled_four, (("rows", 0),), 1)
    padded = jnp.pad(rimmed, ((0, 0), (1, 1), (0, 0)))
    joined_four = convolve(padded, join_weight, 4 * row_count, 4 * GRID_W)
    upsampled_two = expand(tiles[1].reshape(row_count, GRID_W, -1), up2_weight, up2_bias, 2)
    same_scale = tiles[2].reshape(row_count, GRID_W, -1)
    return (joined_four, upsampled_two, same_scale)


def solution(mesh):
    return jax.shard_map(
        body,
        mesh=mesh,
        in_specs=(
            P(None, ("img", "rows"), None),
            P(),
            P(),
            P(),
            P(),
            P(),
            P(),
            P(),
            P(),
            P(),
            P(),
            P(),
            P(),
        ),
        out_specs=(
            P(("img", "rows"), None, None),
            P(("img", "rows"), None, None),
            P(("img", "rows"), None, None),
        ),
        check_vma=False,
    )
```

profile of v0, /device:TPU:0, one launch (start us, length us, event | category | flops | bytes accessed | tf_op | source)
XLA Modules:
  0.0 89.7 jit_solution(3318098243743929334)
XLA Ops:
  8.1 2.5 %sort.51 = (s32[128]{0:T(128)}, s32[128]{0:T(128)S(1)}) sort(s32[128]{0:T(128)S(1)} %and_select_fusion, s32[128]{0:T(128)S(1)} %iota.15), dimensions={0}, to_apply=%region_0.1 | sort | flops 896 | bytes 2048 | tf_op jit(solution)/shard_map/jit(argsort)/sort | solution.py:75
  12.7 1.9 %fusion.21 = bf16[16,8,256]{2,1,0:T(8,128)(2,1)} fusion(bf16[128,1024]{1,0:T(8,128)(2,1)S(1)} %gather_fusion, bf16[1024,256]{1,0:T(8,128)(2,1)} %param.15, f32[256]{0:T(256)S(1)} %copy-done.9), kind=kOutput, calls=%fused_computation.36 | convolution fusion | flops 67174400 | bytes 852992 | tf_op jit(solution)/shard_map/dot_general | solution.py:51
  14.7 7.4 %all-to-all-start = ((bf16[16,8,256]{2,1,0:T(8,128)(2,1)}), bf16[16,8,256]{2,1,0:T(8,128)(2,1)S(1)}, u32[]{:S(2)}, u32[]{:S(2)}) async-start(bf16[16,8,256]{2,1,0:T(8,128)(2,1)} %fusion.21), calls=%async_computation | async-start | bytes 131072 | tf_op jit(solution)/shard_map/all_to_all | solution.py:90
  25.2 2.8 %fusion.17 = bf16[16,8,1024]{2,1,0:T(8,128)(2,1)} fusion(bf16[128,1024]{1,0:T(8,128)(2,1)S(1)} %gather_fusion.4, bf16[1024,1024]{1,0:T(8,128)(2,1)} %param.19, f32[1024]{0:T(1024)S(1)} %copy-done.6), kind=kOutput, calls=%fused_computation.30 | convolution fusion | flops 268697600 | bytes 2625536 | tf_op jit(solution)/shard_map/dot_general | solution.py:51
  30.0 1.2 %gather_fusion.6 = s32[128]{0:T(128)S(1)} fusion(s32[16,128]{1,0:T(8,128)S(1)} %bitcast.86, s32[128]{0:T(128)S(1)} %reshape.145), kind=kCustom, calls=%fused_computation.6 | custom fusion | bytes 2048 | tf_op jit(solution)/shard_map/jit(take_along_axis)/gather | solution.py:79
  31.5 2.5 %sort.53 = (s32[128]{0:T(128)}, s32[128]{0:T(128)S(1)}) sort(s32[128]{0:T(128)S(1)} %sub.25, s32[128]{0:T(128)S(1)} %iota.17), dimensions={0}, to_apply=%region_2.3 | sort | flops 896 | bytes 2048 | tf_op jit(solution)/shard_map/jit(argsort)/sort | solution.py:80
  34.0 6.0 %all-to-all-start.1 = ((bf16[16,8,512]{2,1,0:T(8,128)(2,1)}), bf16[16,8,512]{2,1,0:T(8,128)(2,1)S(1)}, u32[]{:S(2)}, u32[]{:S(2)}) async-start(bf16[16,8,512]{2,1,0:T(8,128)(2,1)} %fusion.19), calls=%async_computation.1 | async-start | bytes 262144 | tf_op jit(solution)/shard_map/all_to_all | solution.py:91
  41.4 1.6 %reshape.92 = bf16[2,64,4,4,256]{4,3,2,1,0:T(4,128)(2,1)} reshape(bf16[128,4096]{1,0:T(8,128)(2,1)S(1)} %fusion) | data formatting | bytes 2097152 | tf_op jit(solution)/shard_map/reshape | solution.py:31
  42.9 2.6 %copy.23 = bf16[2,4,64,4,256]{4,3,2,1,0:T(4,128)(2,1)} copy(bf16[2,4,64,4,256]{4,3,1,2,0:T(4,128)(2,1)} %bitcast.90) | data formatting | bytes 2097152 | tf_op jit(solution)/shard_map/transpose | solution.py:32
  45.5 1.3 %reshape.93 = bf16[8,256,256]{2,1,0:T(8,128)(2,1)S(1)} reshape(bf16[2,4,64,4,256]{4,3,2,1,0:T(4,128)(2,1)} %copy.23) | data formatting | bytes 2097152 | tf_op jit(solution)/shard_map/reshape | solution.py:32
  47.6 3.0 %collective-permute-start = (bf16[1,256,256]{2,1,0:T(8,128)(2,1)}, bf16[1,256,256]{2,1,0:T(8,128)(2,1)}, u32[]{:S(2)}, u32[]{:S(2)}) collective-permute-start(bf16[1,256,256]{2,1,0:T(8,128)(2,1)} %get-tuple-element.9), channel_id=1, source_target_pairs={{0,1},{1,2},{2,3},{3,4},{4,5},{5,6},{6,7},{7,8},{8,9},{9,10},{10,1... | collective-permute-start | bytes 393224 | tf_op jit(solution)/shard_map/ppermute | solution.py:17
  50.5 1.3 %collective-permute-start.1 = (bf16[1,256,256]{2,1,0:T(8,128)(2,1)}, bf16[1,256,256]{2,1,0:T(8,128)(2,1)}, u32[]{:S(2)}, u32[]{:S(2)}) collective-permute-start(bf16[1,256,256]{2,1,0:T(8,128)(2,1)} %get-tuple-element.10), channel_id=1, source_target_pairs={{1,0},{2,1},{3,2},{4,3},{5,4},{6,5},{7,6},{8,7},{9,8},{10,9},{11,1... | collective-permute-start | bytes 393224 | tf_op jit(solution)/shard_map/ppermute | solution.py:19
  51.8 2.7 %fusion.40 = f32[8,256,256]{2,1,0:T(8,128)} fusion(bf16[8,256,256]{2,1,0:T(8,128)(2,1)S(1)} %reshape.93, bf16[3,3,256,256]{3,2,1,0:T(8,128)(2,1)} %param.25), kind=kOutput, calls=%fused_computation.56 | convolution fusion | flops 268435456 | bytes 3276800 | tf_op jit(solution)/shard_map/dot_general | solution.py:41
  54.5 7.3 %all-to-all-start.2 = ((bf16[16,8,1024]{2,1,0:T(8,128)(2,1)}), bf16[16,8,1024]{2,1,0:T(8,128)(2,1)S(1)}, u32[]{:S(2)}, u32[]{:S(2)}) async-start(bf16[16,8,1024]{2,1,0:T(8,128)(2,1)} %fusion.17), calls=%async_computation.2 | async-start | bytes 524288 | tf_op jit(solution)/shard_map/all_to_all | solution.py:92
  61.8 1.5 %gather_fusion.3 = bf16[128,512]{1,0:T(8,128)(2,1)} fusion(bf16[128,512]{1,0:T(8,128)(2,1)S(1)} %bitcast.88, s32[1024]{0:T(1024)S(1)} %pad_clamp_fusion), kind=kCustom, calls=%fused_computation.3 | custom fusion | bytes 262656 | tf_op jit(solution)/shard_map/gather | solution.py:94
  63.3 2.9 %fusion.2 = bf16[128,2048]{1,0:T(8,128)(2,1)} fusion(bf16[128,512]{1,0:T(8,128)(2,1)} %gather_fusion.3, bf16[512,2048]{1,0:T(8,128)(2,1)} %param.23, f32[2048]{0:T(1024)S(1)} %bitcast.94), kind=kOutput, calls=%fused_computation.13 | convolution fusion | flops 268959744 | bytes 2760704 | tf_op jit(solution)/shard_map/dot_general | solution.py:29
  66.3 2.2 %reshape.94 = bf16[2,64,2,2,512]{4,3,2,1,0:T(2,128)(2,1)} reshape(bf16[128,2048]{1,0:T(8,128)(2,1)} %fusion.2) | data formatting | bytes 1048576 | tf_op jit(solution)/shard_map/reshape | solution.py:31
  68.5 2.2 %copy.24 = bf16[2,2,64,2,512]{4,3,2,1,0:T(2,128)(2,1)} copy(bf16[2,2,64,2,512]{4,3,1,2,0:T(2,128)(2,1)} %bitcast.91) | data formatting | bytes 1048576 | tf_op jit(solution)/shard_map/transpose | solution.py:32
  70.7 2.0 %reshape.95 = bf16[4,128,512]{2,1,0:T(8,128)(2,1)} reshape(bf16[2,2,64,2,512]{4,3,2,1,0:T(2,128)(2,1)} %copy.24) | data formatting | bytes 1048576 | tf_op jit(solution)/shard_map/reshape | solution.py:32
  72.7 1.4 %fusion.7 = bf16[10,258,256]{2,1,0:T(8,128)(2,1)S(1)} fusion(bf16[1,256,256]{2,1,0:T(8,128)(2,1)} %collective-permute-done.1, bf16[8,256,256]{2,1,0:T(8,128)(2,1)S(1)} %reshape.93, bf16[1,256,256]{2,1,0:T(8,128)(2,1)} %collective-permute-done), kind=kLoop, calls=%fused_computation.19 | loop fusion | flops 7925760 | bytes 2631680 | tf_op jit(solution)/shard_map/concatenate | solution.py:15
  76.3 1.3 %fusion.9 = f32[8,256,256]{2,1,0:T(8,128)S(1)} fusion(bf16[8,256,256]{2,1,0:T(8,128)(2,1)S(1)} %reshape.93, bf16[1,256,256]{2,1,0:T(8,128)(2,1)} %collective-permute-done, bf16[3,3,256,256]{3,2,1,0:T(8,128)(2,1)S(1)} %copy-done.3), kind=kOutput, calls=%fused_computation.22 | convolution fusion | flops 270794752 | bytes 3407872 | tf_op jit(solution)/shard_map/dot_general | solution.py:41
  77.7 1.5 %fusion.13 = f32[8,256,256]{2,1,0:T(8,128)S(1)} fusion(bf16[1,256,256]{2,1,0:T(8,128)(2,1)} %collective-permute-done.1, bf16[8,256,256]{2,1,0:T(8,128)(2,1)S(1)} %reshape.93, bf16[3,3,256,256]{3,2,1,0:T(8,128)(2,1)S(1)} %copy-done.3), kind=kOutput, calls=%fused_computation.26 | convolution fusion | flops 270794752 | bytes 3407872 | tf_op jit(solution)/shard_map/dot_general | solution.py:41
  79.3 2.0 %add_convert_fusion = bf16[8,256,256]{2,1,0:T(8,128)(2,1)} fusion(f32[8,256,256]{2,1,0:T(8,128)S(1)} %fusion.13, f32[8,256,256]{2,1,0:T(8,128)S(1)} %fusion.26, f32[8,256,256]{2,1,0:T(8,128)S(1)} %fusion.28, f32[8,256,256]{2,1,0:T(8,128)S(1)} %copy-done.2, f32[8,256,256]{2,1,0:T(8,128)S(1)} %fusion.30, f32[8,256,256]{2,1,0:T(8,128)S(1)} %fusion.32, ...), kind=kOutput, calls=%fused_computation.14 | convolution fusion | flops 273154048 | bytes 19005440 | tf_op jit(solution)/shard_map/dot_general | solution.py:41
  81.3 1.6 %gather_fusion.5 = bf16[128,1024]{1,0:T(8,128)(2,1)} fusion(bf16[128,1024]{1,0:T(8,128)(2,1)S(1)} %bitcast.87, s32[1024]{0:T(1024)S(1)} %pad_clamp_fusion), kind=kCustom, calls=%fused_computation.5 | custom fusion | bytes 524800 | tf_op jit(solution)/shard_map/gather | solution.py:94
  (64 shorter events, 12.5 us)
Async XLA Ops:
  7.2 33.7 %copy-start = (bf16[256,4096]{1,0:T(8,128)(2,1)S(1)}, bf16[256,4096]{1,0:T(8,128)(2,1)}, u32[]{:S(2)}) copy-start(bf16[256,4096]{1,0:T(8,128)(2,1)} %param.21) | copy-start | bytes 6291460
  7.2 5.5 %copy-start.9 = (f32[256]{0:T(256)S(1)}, f32[256]{0:T(256)}, u32[]{:S(2)}) copy-start(f32[256]{0:T(256)} %param.16) | copy-start | bytes 3076
  10.7 11.5 %copy-start.1 = (s32[2048]{0:T(1024)S(1)}, s32[2048]{0:T(1024)}, u32[]{:S(2)}) copy-start(s32[2048]{0:T(1024)} %param.14) | copy-start | bytes 24580
  10.7 12.7 %copy-start.10 = (f32[256]{0:T(256)S(1)}, f32[256]{0:T(256)}, u32[]{:S(2)}) copy-start(f32[256]{0:T(256)} %param.22) | copy-start | bytes 3076
  12.7 11.5 %copy-start.8 = (f32[512]{0:T(512)S(1)}, f32[512]{0:T(512)}, u32[]{:S(2)}) copy-start(f32[512]{0:T(512)} %param.24) | copy-start | bytes 6148
  14.7 19.4 %all-to-all-start = ((bf16[16,8,256]{2,1,0:T(8,128)(2,1)}), bf16[16,8,256]{2,1,0:T(8,128)(2,1)S(1)}, u32[]{:S(2)}, u32[]{:S(2)}) async-start(bf16[16,8,256]{2,1,0:T(8,128)(2,1)} %fusion.21), calls=%async_computation | async-start | bytes 131072 | tf_op jit(solution)/shard_map/all_to_all | solution.py:90
  22.1 7.0 %sort.55.cloned.1.call-start = ((), (), s32[]{:S(2)}) async-start(), calls=%async_computation.3 | async-start | bytes 49184 | tf_op jit(solution)/shard_map/jit(argsort)/sort | solution.py:78
  23.4 1.8 %copy-start.6 = (f32[1024]{0:T(1024)S(1)}, f32[1024]{0:T(1024)}, u32[]{:S(2)}) copy-start(f32[1024]{0:T(1024)} %param.20) | copy-start | bytes 12292
  24.3 3.7 %copy-start.7 = (f32[512]{0:T(512)S(1)}, f32[512]{0:T(512)}, u32[]{:S(2)}) copy-start(f32[512]{0:T(512)} %param.18) | copy-start | bytes 6148
  25.2 2.9 %copy-start.4 = (bf16[1024,512]{1,0:T(8,128)(2,1)S(1)}, bf16[1024,512]{1,0:T(8,128)(2,1)}, u32[]{:S(2)}) copy-start(bf16[1024,512]{1,0:T(8,128)(2,1)} %param.17) | copy-start | bytes 3145732
  30.0 1.3 %copy-start.5 = (s32[16,128]{1,0:T(8,128)S(1)}, s32[16,128]{1,0:T(8,128)}, u32[]{:S(2)}) copy-start(s32[16,128]{1,0:T(8,128)} %get-tuple-element.7) | copy-start | bytes 24580
  34.0 20.5 %all-to-all-start.1 = ((bf16[16,8,512]{2,1,0:T(8,128)(2,1)}), bf16[16,8,512]{2,1,0:T(8,128)(2,1)S(1)}, u32[]{:S(2)}, u32[]{:S(2)}) async-start(bf16[16,8,512]{2,1,0:T(8,128)(2,1)} %fusion.19), calls=%async_computation.1 | async-start | bytes 262144 | tf_op jit(solution)/shard_map/all_to_all | solution.py:91
  47.6 25.1 %collective-permute-start = (bf16[1,256,256]{2,1,0:T(8,128)(2,1)}, bf16[1,256,256]{2,1,0:T(8,128)(2,1)}, u32[]{:S(2)}, u32[]{:S(2)}) collective-permute-start(bf16[1,256,256]{2,1,0:T(8,128)(2,1)} %get-tuple-element.9), channel_id=1, source_target_pairs={{0,1},{1,2},{2,3},{3,4},{4,5},{5,6},{6,7},{7,8},{8,9},{9,10},{10,1... | collective-permute-start | bytes 393224 | tf_op jit(solution)/shard_map/ppermute | solution.py:17
  50.5 22.2 %collective-permute-start.1 = (bf16[1,256,256]{2,1,0:T(8,128)(2,1)}, bf16[1,256,256]{2,1,0:T(8,128)(2,1)}, u32[]{:S(2)}, u32[]{:S(2)}) collective-permute-start(bf16[1,256,256]{2,1,0:T(8,128)(2,1)} %get-tuple-element.10), channel_id=1, source_target_pairs={{1,0},{2,1},{3,2},{4,3},{5,4},{6,5},{7,6},{8,7},{9,8},{10,9},{11,1... | collective-permute-start | bytes 393224 | tf_op jit(solution)/shard_map/ppermute | solution.py:19
  54.5 26.8 %all-to-all-start.2 = ((bf16[16,8,1024]{2,1,0:T(8,128)(2,1)}), bf16[16,8,1024]{2,1,0:T(8,128)(2,1)S(1)}, u32[]{:S(2)}, u32[]{:S(2)}) async-start(bf16[16,8,1024]{2,1,0:T(8,128)(2,1)} %fusion.17), calls=%async_computation.2 | async-start | bytes 524288 | tf_op jit(solution)/shard_map/all_to_all | solution.py:92
  72.7 1.4 %copy-start.3 = (bf16[3,3,256,256]{3,2,1,0:T(8,128)(2,1)S(1)}, bf16[3,3,256,256]{3,2,1,0:T(8,128)(2,1)}, u32[]{:S(2)}) copy-start(bf16[3,3,256,256]{3,2,1,0:T(8,128)(2,1)} %param.25) | copy-start | bytes 3538948
  77.7 1.7 %copy-start.2 = (f32[8,256,256]{2,1,0:T(8,128)S(1)}, f32[8,256,256]{2,1,0:T(8,128)}, u32[]{:S(2)}) copy-start(f32[8,256,256]{2,1,0:T(8,128)} %fusion.40) | copy-start | bytes 6291460
Sparse Core Ops, SparseCore 0:
  25.1 2.0 sort.57.cloned.1.call-done
  (1 shorter events, 0.0 us)
where the time goes:
time: 90.6 us; the launch traced here: 89.7 us
  starting transfers between devices  25 us (28%)
  local copies, waits for them, and re-layouts  22.9 us (25%)
  matrix products  18.8 us (21%)
  between operations  14.3 us (16%)
  other arithmetic  8.72 us (10%)
    dot_general x9, matrix products, convolve(): jnp.dot(window.reshape(-1, channels), weight[row_tap, col_tap], preferred...  9.71 us
    all_to_all x1, starting transfers between devices, body(): lax.all_to_all(local_four, 'rows', split_axis=0, concat_axis=0, tiled=True)  7.41 us
    all_to_all x1, starting transfers between devices, body(): lax.all_to_all(local_same, 'rows', split_axis=0, concat_axis=0, tiled=True)  7.32 us
    all_to_all x1, starting transfers between devices, body(): lax.all_to_all(local_two, 'rows', split_axis=0, concat_axis=0, tiled=True)  6.02 us
    dot_general x3, matrix products, project_one(): jnp.dot(tokens_block, weight, preferred_element_type=jnp.float32) + bias_row  5.74 us
    transpose x2, local copies, waits for them, and re-layouts, expand(): result.transpose(0, 2, 1, 3, 4)  4.75 us
    gather x3, local copies, waits for them, and re-layouts, body(): tiles = [piece[placing] for piece in arrived]  3.91 us
    reshape x2, local copies, waits for them, and re-layouts, expand(): flattened.astype(jnp.bfloat16)  3.8 us
  transfers between devices with their start and end apart: 5, of which 0 were waited for; matrix products, arithmetic and copies ran while one was open for 46% of the time, Pallas kernels for 0%

commit v1 on v0

v1 whole, which is shorter than its diff:
```python
import functools

import jax
import jax.numpy as jnp
from jax import lax
from jax.experimental import pallas as pl
from jax.experimental.pallas import tpu as pltpu
from jax.sharding import PartitionSpec as P

GRID_W = 64
F32 = jnp.float32
BF16 = jnp.bfloat16
ANY = pl.BlockSpec(memory_space=pl.ANY)
VMEM = pl.BlockSpec(memory_space=pltpu.VMEM)


def in_hbm(x):
    return pltpu.with_memory_space_constraint(x, pltpu.HBM)


def one_hot(mask):
    return jnp.where(mask, 1.0, 0.0).astype(BF16)


def iota(shape, dim):
    return lax.broadcasted_iota(jnp.int32, shape, dim)


def matmul(left, right):
    return jnp.dot(left, right, preferred_element_type=F32)


def column(row, size):
    same = iota((size, size), 0) == iota((size, size), 1)
    return jnp.sum(jnp.where(same, jnp.broadcast_to(row, (size, size)), 0.0), axis=1, keepdims=True)


def landing(table, block, tok_dev, per_peer):
    shards = table.shape[0]
    start = block * tok_dev
    inside = jnp.logical_and(table >= start, table < start + tok_dev)
    before = one_hot(iota((tok_dev, tok_dev), 0) < iota((tok_dev, tok_dev), 1))
    rank = matmul(one_hot(inside), before)
    place = (table - start).astype(F32)
    lane = iota((shards, tok_dev), 1)
    spread = jnp.zeros((shards, tok_dev), F32)
    for k in range(per_peer):
        hit = jnp.logical_and(inside, rank == float(k))
        found = jnp.sum(jnp.where(hit, place, 0.0), axis=1, keepdims=True)
        spread = spread + jnp.where(lax.rem(lane, per_peer) == k, found, 0.0)
    own = lax.div(lane, per_peer) == iota((shards, tok_dev), 0)
    return jnp.sum(jnp.where(own, spread, 0.0), axis=0, keepdims=True).astype(jnp.int32)


def project_kernel(
    hidden, table_hbm, w4, b4, w2, b2, ws, bs, four_v, rest_v, places_v,
    hidden_v, table_v, w4_v, w2_v, ws_v, b4_v, b2_v, bs_v, sems,
):
    copies = [
        pltpu.make_async_copy(src, dst, sems.at[i])
        for i, (src, dst) in enumerate(
            (
                (table_hbm, table_v),
                (hidden.at[0], hidden_v.at[0]),
                (b4, b4_v),
                (w4, w4_v),
                (hidden.at[1], hidden_v.at[1]),
                (b2, b2_v),
                (w2, w2_v),
                (hidden.at[2], hidden_v.at[2]),
                (bs, bs_v),
                (ws, ws_v),
            )
        )
    ]
    for copy in copies:
        copy.start()
    shards, tok_dev = table_v.shape
    per_peer = tok_dev // shards
    me = lax.axis_index("rows")
    copies[0].wait()
    table = table_v[...]
    mine = table_v[pl.ds(me, 1), :]
    block_row = lax.div(mine, tok_dev)
    block_col = column(block_row.astype(F32), tok_dev).astype(jnp.int32)
    square = (tok_dev, tok_dev)
    earlier = jnp.logical_and(block_col == jnp.broadcast_to(block_row, square), iota(square, 0) < iota(square, 1))
    within = jnp.sum(jnp.where(earlier, 1.0, 0.0), axis=0, keepdims=True).astype(jnp.int32)
    slot = block_row * per_peer + within
    order = one_hot(iota(square, 0) == slot)
    order_above = one_hot(iota(square, 0) == slot + per_peer)
    order_below = one_hot(iota(square, 0) == slot - per_peer)

    own = landing(table, me, tok_dev, per_peer)
    above = landing(table, me - 1, tok_dev, per_peer)
    below = landing(table, me + 1, tok_dev, per_peer)
    cell = iota(square, 0)
    col = lax.rem(cell, GRID_W)
    edge = (GRID_W, tok_dev)
    edge_col = iota(edge, 0)
    last = edge_col + (tok_dev - GRID_W)
    places_v[0:tok_dev] = one_hot(cell == own)
    places_v[tok_dev : 2 * tok_dev] = one_hot(jnp.logical_and(cell == own + 1, col != 0))
    places_v[2 * tok_dev : 3 * tok_dev] = one_hot(jnp.logical_and(cell == own - 1, col != GRID_W - 1))
    base = 3 * tok_dev
    for source, target in ((above, last), (below, edge_col)):
        places_v[base : base + GRID_W] = one_hot(target == source)
        places_v[base + GRID_W : base + 2 * GRID_W] = one_hot(jnp.logical_and(target == source + 1, edge_col != 0))
        places_v[base + 2 * GRID_W : base + 3 * GRID_W] = one_hot(
            jnp.logical_and(target == source - 1, edge_col != GRID_W - 1)
        )
        base += 3 * GRID_W

    for copy in copies[1:4]:
        copy.wait()
    c4 = w4_v.shape[1]
    four = (matmul(hidden_v[0], w4_v[...]) + b4_v[...]).astype(BF16)
    four_v[:, 0:c4] = matmul(order, four).astype(BF16)
    four_v[:, c4 : 2 * c4] = matmul(order_above, four).astype(BF16)
    four_v[:, 2 * c4 : 3 * c4] = matmul(order_below, four).astype(BF16)
    for copy in copies[4:7]:
        copy.wait()
    c2 = w2_v.shape[1]
    two = (matmul(hidden_v[1], w2_v[...]) + b2_v[...]).astype(BF16)
    rest_v[:, 0:c2] = matmul(order, two).astype(BF16)
    for copy in copies[7:10]:
        copy.wait()
    same = (matmul(hidden_v[2], ws_v[...]) + bs_v[...]).astype(BF16)
    rest_v[:, c2:] = matmul(order, same).astype(BF16)


def fetch_kernel(w4, b4, wj, w2, b2, w4_v, b4_v, wj_v, w2_v, b2_v, sems):
    pairs = ((w4, w4_v), (b4, b4_v), (wj, wj_v), (w2, w2_v), (b2, b2_v))
    copies = [pltpu.make_async_copy(src, dst, sems.at[i]) for i, (src, dst) in enumerate(pairs)]
    for copy in copies:
        copy.start()
    for copy in copies:
        copy.wait()


def four_kernel(arrived, places, w4, b4, wj, joined, tiles_v, wide_v, acc_v, out_v, sems):
    tok_dev, c4 = arrived.shape[0], arrived.shape[1] // 3
    row_count = tok_dev // GRID_W
    me = lax.axis_index("rows")
    top = jnp.where(me > 0, 1.0, 0.0)
    bottom = jnp.where(me < lax.axis_size("rows") - 1, 1.0, 0.0)
    bias = b4[...]
    feat = c4

    base = 3 * tok_dev
    tiles_v[0:base] = matmul(places[0:base], arrived[:, 0:c4]).astype(BF16)
    tiles_v[base : base + 3 * GRID_W] = matmul(places[base : base + 3 * GRID_W], arrived[:, c4 : 2 * c4]).astype(BF16)
    base += 3 * GRID_W
    tiles_v[base : base + 3 * GRID_W] = matmul(places[base : base + 3 * GRID_W], arrived[:, 2 * c4 :]).astype(BF16)

    left = jnp.where(iota((GRID_W, 1), 0) == 0, 0.0, 1.0)
    right = jnp.where(iota((GRID_W, 1), 0) == GRID_W - 1, 0.0, 1.0)

    def fill(first, stride, rows, tap, to, scale):
        size = rows * GRID_W
        for b in range(4):
            part = matmul(tiles_v[first : first + size], w4[:, (tap * 4 + b) * feat : (tap * 4 + b + 1) * feat]) + bias
            if scale is not None:
                part = part * scale
            for i in range(rows):
                wide_v[pl.ds(to(i) * GRID_W, GRID_W), (b + 1) * feat : (b + 2) * feat] = part[
                    i * GRID_W : (i + 1) * GRID_W
                ].astype(BF16)
        for b, shift, edge, block in ((3, 1, left, 0), (0, 2, right, 5)):
            start = first + shift * stride
            part = matmul(tiles_v[start : start + size], w4[:, (tap * 4 + b) * feat : (tap * 4 + b + 1) * feat]) + bias
            if scale is not None:
                part = part * scale
            for i in range(rows):
                wide_v[pl.ds(to(i) * GRID_W, GRID_W), block * feat : (block + 1) * feat] = (
                    part[i * GRID_W : (i + 1) * GRID_W] * edge
                ).astype(BF16)

    for tap in range(4):
        fill(0, tok_dev, row_count, tap, lambda i, tap=tap: 4 * i + tap + 1, None)
    fill(3 * tok_dev, GRID_W, 1, 3, lambda i: 0, top)
    fill(3 * tok_dev + 3 * GRID_W, GRID_W, 1, 0, lambda i: 4 * row_count + 1, bottom)

    copies = []
    for chunk in range(row_count):
        for b in range(4):
            total = None
            for row_tap in range(3):
                term = matmul(
                    wide_v[(4 * chunk + row_tap) * GRID_W : (4 * chunk + row_tap + 4) * GRID_W, b * feat : (b + 3) * feat],
                    wj[row_tap],
                )
                total = term if total is None else total + term
            for r in range(4):
                for block in range(feat // 128):
                    acc_v[4 * chunk + r, block, pl.ds(b, GRID_W, 4), :] = total[
                        r * GRID_W : (r + 1) * GRID_W, block * 128 : (block + 1) * 128
                    ]
        for r in range(4 * chunk, 4 * chunk + 4):
            for block in range(feat // 128):
                out_v[r, :, block * 128 : (block + 1) * 128] = acc_v[r, block].astype(BF16)
        copy = pltpu.make_async_copy(
            out_v.at[pl.ds(4 * chunk, 4)], joined.at[pl.ds(4 * chunk, 4)], sems.at[chunk]
        )
        copy.start()
        copies.append(copy)
    for copy in copies:
        copy.wait()


def rest_kernel(arrived, places, w2, b2, up_two, same, acc_v, out_v, same_v, sems):
    tok_dev = arrived.shape[0]
    c2 = w2.shape[0]
    row_count = tok_dev // GRID_W
    place = places[0:tok_dev]
    same_v[...] = matmul(place, arrived[:, c2:]).astype(BF16)
    out_same = pltpu.make_async_copy(same_v, same, sems.at[0])
    out_same.start()
    tile = matmul(place, arrived[:, 0:c2]).astype(BF16)
    bias = b2[...]
    copies = []
    for a in range(2):
        for b in range(2):
            part = matmul(tile, w2[:, (a * 2 + b) * c2 : (a * 2 + b + 1) * c2]) + bias
            for i in range(row_count):
                for block in range(c2 // 128):
                    acc_v[2 * i + a, block, pl.ds(b, GRID_W, 2), :] = part[
                        i * GRID_W : (i + 1) * GRID_W, block * 128 : (block + 1) * 128
                    ]
        for i in range(row_count):
            r = 2 * i + a
            for block in range(c2 // 128):
                out_v[r, :, block * 128 : (block + 1) * 128] = acc_v[r, block].astype(BF16)
            copy = pltpu.make_async_copy(out_v.at[r], up_two.at[r], sems.at[1 + r])
            copy.start()
            copies.append(copy)
    out_same.wait()
    for copy in copies:
        copy.wait()


def body(
    hidden_states,
    cell_of,
    proj_four_weight,
    proj_four_bias,
    proj_two_weight,
    proj_two_bias,
    proj_same_weight,
    proj_same_bias,
    up4_weight,
    up4_bias,
    up2_weight,
    up2_bias,
    join_weight,
):
    hooks, tok_dev, hid = hidden_states.shape
    shards = lax.axis_size("rows")
    per_peer = tok_dev // shards
    row_count = tok_dev // GRID_W
    c4, c2, cs = proj_four_weight.shape[1], proj_two_weight.shape[1], proj_same_weight.shape[1]
    feat = join_weight.shape[3]
    table = cell_of.reshape(shards, tok_dev)
    place_rows = 3 * tok_dev + 6 * GRID_W
    shape = jax.ShapeDtypeStruct

    send_four, send_rest, places = pl.pallas_call(
        project_kernel,
        out_shape=(
            pltpu.VMEM((tok_dev, 3 * c4), BF16),
            pltpu.VMEM((tok_dev, c2 + cs), BF16),
            pltpu.VMEM((place_rows, tok_dev), BF16),
        ),
        in_specs=[ANY] * 8,
        out_specs=(VMEM, VMEM, VMEM),
        scratch_shapes=[
            pltpu.VMEM(hidden_states.shape, BF16),
            pltpu.VMEM(table.shape, jnp.int32),
            pltpu.VMEM((hid, c4), BF16),
            pltpu.VMEM((hid, c2), BF16),
            pltpu.VMEM((hid, cs), BF16),
            pltpu.VMEM((1, c4), F32),
            pltpu.VMEM((1, c2), F32),
            pltpu.VMEM((1, cs), F32),
            pltpu.SemaphoreType.DMA((10,)),
        ],
        cost_estimate=pl.CostEstimate(flops=2 * tok_dev * hid * (c4 + c2 + cs), bytes_accessed=5 << 20, transcendentals=0),
        name="project",
        compiler_params=pltpu.CompilerParams(vmem_limit_bytes=12 << 20),
    )(
        in_hbm(hidden_states),
        in_hbm(table),
        in_hbm(proj_four_weight),
        in_hbm(proj_four_bias.reshape(1, -1)),
        in_hbm(proj_two_weight),
        in_hbm(proj_two_bias.reshape(1, -1)),
        in_hbm(proj_same_weight),
        in_hbm(proj_same_bias.reshape(1, -1)),
    )
    exchange = functools.partial(lax.all_to_all, axis_name="rows", split_axis=0, concat_axis=0, tiled=True)
    four = exchange(send_four.reshape(shards, per_peer, 3 * c4)).reshape(tok_dev, 3 * c4)
    rest = exchange(send_rest.reshape(shards, per_peer, c2 + cs)).reshape(tok_dev, c2 + cs)

    weights = (
        up4_weight,
        up4_bias.reshape(1, -1),
        join_weight.reshape(3, 3 * c4, feat),
        up2_weight,
        up2_bias.reshape(1, -1),
    )
    w4, b4, wj, w2, b2 = pl.pallas_call(
        fetch_kernel,
        out_shape=tuple(pltpu.VMEM(w.shape, w.dtype) for w in weights),
        in_specs=[ANY] * 5,
        out_specs=(VMEM,) * 5,
        scratch_shapes=[pltpu.SemaphoreType.DMA((5,))],
        cost_estimate=pl.CostEstimate(flops=1 << 30, bytes_accessed=6 << 20, transcendentals=0),
        name="fetch",
        compiler_params=pltpu.CompilerParams(vmem_limit_bytes=8 << 20),
    )(*(in_hbm(w) for w in weights))

    out_rows = 4 * row_count
    joined = pl.pallas_call(
        four_kernel,
        out_shape=shape((out_rows, 4 * GRID_W, feat), BF16),
        in_specs=[VMEM] * 5,
        out_specs=ANY,
        scratch_shapes=[
            pltpu.VMEM((place_rows, c4), BF16),
            pltpu.VMEM(((out_rows + 2) * GRID_W, 6 * c4), BF16),
            pltpu.VMEM((out_rows, feat // 128, 4 * GRID_W, 128), F32),
            pltpu.VMEM((out_rows, 4 * GRID_W, feat), BF16),
            pltpu.SemaphoreType.DMA((row_count,)),
        ],
        compiler_params=pltpu.CompilerParams(vmem_limit_bytes=24 << 20),
        cost_estimate=pl.CostEstimate(flops=4 << 30, bytes_accessed=4 << 20, transcendentals=0),
        name="join",
    )(four, places, w4, b4, wj)

    upsampled_two, same_scale = pl.pallas_call(
        rest_kernel,
        out_shape=(shape((2 * row_count, 2 * GRID_W, c2), BF16), shape((tok_dev, cs), BF16)),
        in_specs=[VMEM] * 4,
        out_specs=(ANY, ANY),
        scratch_shapes=[
            pltpu.VMEM((2 * row_count, c2 // 128, 2 * GRID_W, 128), F32),
            pltpu.VMEM((2 * row_count, 2 * GRID_W, c2), BF16),
            pltpu.VMEM((tok_dev, cs), BF16),
            pltpu.SemaphoreType.DMA((1 + 2 * row_count,)),
        ],
        compiler_params=pltpu.CompilerParams(vmem_limit_bytes=16 << 20),
        cost_estimate=pl.CostEstimate(flops=1 << 28, bytes_accessed=4 << 20, transcendentals=0),
        name="rest",
    )(rest, places, w2, b2)
    return (joined, upsampled_two, same_scale.reshape(row_count, GRID_W, cs))


def solution(mesh):
    return jax.shard_map(
        body,
        mesh=mesh,
        in_specs=(P(None, ("img", "rows"), None),) + (P(),) * 12,
        out_specs=(P(("img", "rows"), None, None),) * 3,
        check_vma=False,
    )
```

time: 90.6 us -> 38 us (0.42)
  local copies, waits for them, and re-layouts: 22.9 us -> 0 us
  starting transfers between devices: 25 us -> 3.55 us
  matrix products: 18.8 us -> 0 us
  blocking collectives: 0 us -> 16.2 us
  between operations: 14.3 us -> 0.67 us
  Pallas kernels: 0 us -> 12.3 us
  other arithmetic: 8.72 us -> 0 us
  waiting for transfers between devices: 0.01 us -> 5.09 us
    dot_general x14 -> x0, matrix products: 18.8 us -> none  [the longest x9 9.71 us: convolve(): jnp.dot(window.reshape(-1, channels), weight[row_tap, col_tap], preferred...]
    all_to_all x3 -> x1, starting transfers between devices: 20.8 us -> 3.55 us  [body(): exchange(send_rest.reshape(shards, per_peer, c2 + cs))]
    all_to_all x0 -> x1, blocking collectives: none -> 16.2 us  [body(): exchange(send_four.reshape(shards, per_peer, 3 * c4))]
    pallas_call x0 -> x4, Pallas kernels: none -> 12.3 us  [the longest x1 4.37 us: body(): pl.pallas_call(four_kernel, out_shape=shape((out_rows, 4 * GRID_W, feat),...]
    gather x11 -> x0, local copies, waits for them, and re-layouts: 8.06 us -> none  [the longest x3 3.91 us: body(): tiles = [piece[placing] for piece in arrived]]
    reshape x4 -> x0, local copies, waits for them, and re-layouts: 7.17 us -> none  [the longest x2 3.8 us: expand(): flattened.astype(jnp.bfloat16)]
    all_to_all x3 -> x1, waiting for transfers between devices: 0.01 us -> 5.09 us  [body(): exchange(send_rest.reshape(shards, per_peer, c2 + cs))]
    sort x2 -> x0, other arithmetic: 5.06 us -> none  [the longest x1 2.54 us: body(): outgoing = jnp.argsort(my_cells // tok_dev, stable=True)]
  transfers between devices with their start and end apart: 5 -> 1, of which waited for: 0 -> 1; matrix products, arithmetic and copies ran while one was open for 46% -> 0% of each run, Pallas kernels for 0% -> 19%
where the time goes in v1:
time: 38 us; the launch traced here: 37.7 us
  blocking collectives  16.2 us (43%)
  Pallas kernels  12.3 us (32%)
  waiting for transfers between devices  5.09 us (13%)
  starting transfers between devices  3.55 us (9%)
  between operations  0.67 us (2%)
    all_to_all x1, blocking collectives, body(): exchange(send_four.reshape(shards, per_peer, 3 * c4))  16.2 us
    all_to_all x1, waiting for transfers between devices, body(): exchange(send_rest.reshape(shards, per_peer, c2 + cs))  5.09 us
    pallas_call x1, Pallas kernels, body(): pl.pallas_call(four_kernel, out_shape=shape((out_rows, 4 * GRID_W, feat),...  4.37 us
    pallas_call x1, Pallas kernels, body(): pl.pallas_call(project_kernel, out_shape=(pltpu.VMEM((tok_dev, 3 * c4), B...  3.82 us
    all_to_all x1, starting transfers between devices, body(): exchange(send_rest.reshape(shards, per_peer, c2 + cs))  3.55 us
    pallas_call x1, Pallas kernels, body(): pl.pallas_call(fetch_kernel, out_shape=tuple((pltpu.VMEM(w.shape, w.dtype...  2.65 us
    pallas_call x1, Pallas kernels, body(): pl.pallas_call(rest_kernel, out_shape=(shape((2 * row_count, 2 * GRID_W,...  1.42 us
  transfers between devices with their start and end apart: 1, of which 1 were waited for; matrix products, arithmetic and copies ran while one was open for 0% of the time, Pallas kernels for 19%

profile of v1, /device:TPU:0, one launch (start us, length us, event | category | flops | bytes accessed | tf_op | source)
XLA Modules:
  0.0 37.7 jit_solution(17680773122886966082)
XLA Ops:
  0.6 3.8 %project.1 = (bf16[128,768]{1,0:T(8,128)(2,1)S(1)}, bf16[128,1536]{1,0:T(8,128)(2,1)}, bf16[768,128]{1,0:T(8,128)(2,1)S(1)}) custom-call(bf16[3,128,1024]{2,1,0:T(8,128)(2,1)} %hidden.1, s32[16,128]{1,0:T(8,128)} %bitcast.16, bf16[1024,256]{1,0:T(8,128)(2,1)} %w4.2, f32[1,256]{1,0:T(1,128)} %bitcast.20, bf16[1024,512]{1,0:T(8,128)(2,1)} %w2.2, ...), custom_call_target="tpu_custom_call" | custom-call | flops 469762048 | bytes 5242880 | tf_op jit(solution)/shard_map/project/pallas_call | solution.py:267
  4.5 16.2 %all_to_all.10 = bf16[16,8,768]{2,1,0:T(8,128)(2,1)S(1)} all-to-all(bf16[16,8,768]{2,1,0:T(8,128)(2,1)S(1)} %bitcast.14), channel_id=1, replica_groups=mesh['img'=2,'rows'=16] {'rows'}, dimensions={0} | all-to-all | bytes 393216 | tf_op jit(solution)/shard_map/all_to_all | solution.py:301
  20.6 3.6 %all-to-all-start.1 = ((bf16[16,8,1536]{2,1,0:T(8,128)(2,1)}), bf16[16,8,1536]{2,1,0:T(8,128)(2,1)S(1)}, u32[]{:S(2)}, u32[]{:S(2)}) async-start(bf16[16,8,1536]{2,1,0:T(8,128)(2,1)} %bitcast.9), calls=%async_computation.1 | async-start | bytes 786432 | tf_op jit(solution)/shard_map/all_to_all | solution.py:302
  24.2 2.6 %fetch.1 = (bf16[256,4096]{1,0:T(8,128)(2,1)S(1)}, f32[1,256]{1,0:T(1,128)S(1)}, bf16[3,768,256]{2,1,0:T(8,128)(2,1)S(1)}, bf16[512,2048]{1,0:T(8,128)(2,1)S(1)}, f32[1,512]{1,0:T(1,128)S(1)}) custom-call(bf16[256,4096]{1,0:T(8,128)(2,1)} %w4.3, f32[1,256]{1,0:T(1,128)} %bitcast.21, bf16[3,768,256]{2,1,0:T(8,128)(2,1)} %bitcast.15, bf16[512,2048]{1,0:T(8,128)(2,1)} %w2.3, ...), custom_call_target="tpu_custom_call" | custom-call | flops 1073741824 | bytes 6291456 | tf_op jit(solution)/shard_map/fetch/pallas_call | solution.py:311
  26.9 4.4 %join.1 = bf16[8,256,256]{2,1,0:T(8,128)(2,1)} custom-call(bf16[128,768]{1,0:T(8,128)(2,1)S(1)} %bitcast.13, bf16[768,128]{1,0:T(8,128)(2,1)S(1)} %get-tuple-element.14.places, bf16[256,4096]{1,0:T(8,128)(2,1)S(1)} %get-tuple-element.15.w4, f32[1,256]{1,0:T(1,128)S(1)} %get-tuple-element.16.b4, bf16[3,768,256]{2,1,0:T(8,128)(2,1)S(1)} %get-tuple-element.17.wj), custom_call_target="tpu_custom_call" | custom-call | flops 4294967296 | bytes 4194304 | tf_op jit(solution)/shard_map/join/pallas_call | solution.py:323
  31.2 5.1 %all-to-all-done.1 = bf16[16,8,1536]{2,1,0:T(8,128)(2,1)S(1)} async-done(((bf16[16,8,1536]{2,1,0:T(8,128)(2,1)}), bf16[16,8,1536]{2,1,0:T(8,128)(2,1)S(1)}, u32[]{:S(2)}, u32[]{:S(2)}) %all-to-all-start.1) | async-done | bytes 393248 | tf_op jit(solution)/shard_map/all_to_all | solution.py:302
  36.3 1.4 %rest.1 = (bf16[4,128,512]{2,1,0:T(8,128)(2,1)}, bf16[128,1024]{1,0:T(8,128)(2,1)}) custom-call(bf16[128,1536]{1,0:T(8,128)(2,1)S(1)} %bitcast.12, bf16[768,128]{1,0:T(8,128)(2,1)S(1)} %get-tuple-element.14.places, bf16[512,2048]{1,0:T(8,128)(2,1)S(1)} %get-tuple-element.19.w2, f32[1,512]{1,0:T(1,128)S(1)} %get-tuple-element.20.b2), custom_call_target="tpu_custom_call" | custom-call | flops 268435456 | bytes 4194304 | tf_op jit(solution)/shard_map/rest/pallas_call | solution.py:340
Async XLA Ops:
  20.6 15.7 %all-to-all-start.1 = ((bf16[16,8,1536]{2,1,0:T(8,128)(2,1)}), bf16[16,8,1536]{2,1,0:T(8,128)(2,1)S(1)}, u32[]{:S(2)}, u32[]{:S(2)}) async-start(bf16[16,8,1536]{2,1,0:T(8,128)(2,1)} %bitcast.9), calls=%async_computation.1 | async-start | bytes 786432 | tf_op jit(solution)/shard_map/all_to_all | solution.py:302

commit v2 on v1

v2 whole, which is shorter than its diff:
```python
import functools

import jax
import jax.numpy as jnp
from jax import lax
from jax.experimental import pallas as pl
from jax.experimental.pallas import tpu as pltpu
from jax.sharding import PartitionSpec as P

GRID_W = 64
CHUNK = 256
F32 = jnp.float32
BF16 = jnp.bfloat16
ANY = pl.BlockSpec(memory_space=pl.ANY)
VMEM = pl.BlockSpec(memory_space=pltpu.VMEM)


def in_hbm(x):
    return pltpu.with_memory_space_constraint(x, pltpu.HBM)


def one_hot(mask):
    return jnp.where(mask, 1.0, 0.0).astype(BF16)


def iota(shape, dim):
    return lax.broadcasted_iota(jnp.int32, shape, dim)


def matmul(left, right):
    return jnp.dot(left, right, preferred_element_type=F32)


def column(row, size):
    same = iota((size, size), 0) == iota((size, size), 1)
    return jnp.sum(jnp.where(same, jnp.broadcast_to(row, (size, size)), 0.0), axis=1, keepdims=True)


def landing(table, block, tok_dev, per_peer):
    shards = table.shape[0]
    start = block * tok_dev
    inside = jnp.logical_and(table >= start, table < start + tok_dev)
    before = one_hot(iota((tok_dev, tok_dev), 0) < iota((tok_dev, tok_dev), 1))
    rank = matmul(one_hot(inside), before)
    place = (table - start).astype(F32)
    lane = iota((shards, tok_dev), 1)
    spread = jnp.zeros((shards, tok_dev), F32)
    for k in range(per_peer):
        hit = jnp.logical_and(inside, rank == float(k))
        found = jnp.sum(jnp.where(hit, place, 0.0), axis=1, keepdims=True)
        spread = spread + jnp.where(lax.rem(lane, per_peer) == k, found, 0.0)
    own = lax.div(lane, per_peer) == iota((shards, tok_dev), 0)
    return jnp.sum(jnp.where(own, spread, 0.0), axis=0, keepdims=True).astype(jnp.int32)


def project_kernel(
    hidden, table_hbm, w4, b4, w2, b2, ws, bs, send, places_v,
    hidden_v, table_v, w4_v, w2_v, ws_v, b4_v, b2_v, bs_v, send_v, sems, out_sems,
):
    chunks = ws.shape[1] // CHUNK
    pairs = [
        (table_hbm, table_v),
        (hidden.at[0], hidden_v.at[0]),
        (b4, b4_v),
        (w4, w4_v),
        (hidden.at[1], hidden_v.at[1]),
        (b2, b2_v),
        (w2, w2_v),
        (hidden.at[2], hidden_v.at[2]),
        (bs, bs_v),
    ] + [(ws.at[:, pl.ds(i * CHUNK, CHUNK)], ws_v.at[i]) for i in range(chunks)]
    copies = [pltpu.make_async_copy(src, dst, sems.at[i]) for i, (src, dst) in enumerate(pairs)]
    for copy in copies:
        copy.start()
    shards, tok_dev = table_v.shape
    per_peer = tok_dev // shards
    me = lax.axis_index("rows")
    copies[0].wait()
    table = table_v[...]
    mine = table_v[pl.ds(me, 1), :]
    block_row = lax.div(mine, tok_dev)
    block_col = column(block_row.astype(F32), tok_dev).astype(jnp.int32)
    square = (tok_dev, tok_dev)
    earlier = jnp.logical_and(block_col == jnp.broadcast_to(block_row, square), iota(square, 0) < iota(square, 1))
    within = jnp.sum(jnp.where(earlier, 1.0, 0.0), axis=0, keepdims=True).astype(jnp.int32)
    slot = block_row * per_peer + within
    order = one_hot(iota(square, 0) == slot)
    order_above = one_hot(iota(square, 0) == slot + per_peer)
    order_below = one_hot(iota(square, 0) == slot - per_peer)

    own = landing(table, me, tok_dev, per_peer)
    above = landing(table, me - 1, tok_dev, per_peer)
    below = landing(table, me + 1, tok_dev, per_peer)
    cell = iota(square, 0)
    col = lax.rem(cell, GRID_W)
    edge = (GRID_W, tok_dev)
    edge_col = iota(edge, 0)
    last = edge_col + (tok_dev - GRID_W)
    places_v[0:tok_dev] = one_hot(cell == own)
    places_v[tok_dev : 2 * tok_dev] = one_hot(jnp.logical_and(cell == own + 1, col != 0))
    places_v[2 * tok_dev : 3 * tok_dev] = one_hot(jnp.logical_and(cell == own - 1, col != GRID_W - 1))
    base = 3 * tok_dev
    for source, target in ((above, last), (below, edge_col)):
        places_v[base : base + GRID_W] = one_hot(target == source)
        places_v[base + GRID_W : base + 2 * GRID_W] = one_hot(jnp.logical_and(target == source + 1, edge_col != 0))
        places_v[base + 2 * GRID_W : base + 3 * GRID_W] = one_hot(
            jnp.logical_and(target == source - 1, edge_col != GRID_W - 1)
        )
        base += 3 * GRID_W

    for copy in copies[1:4]:
        copy.wait()
    c4 = w4_v.shape[1]
    four = (matmul(hidden_v[0], w4_v[...]) + b4_v[...]).astype(BF16)
    send_v[:, 0:c4] = matmul(order, four).astype(BF16)
    send_v[:, c4 : 2 * c4] = matmul(order_above, four).astype(BF16)
    send_v[:, 2 * c4 : 3 * c4] = matmul(order_below, four).astype(BF16)
    for copy in copies[4:7]:
        copy.wait()
    c2 = w2_v.shape[1]
    two = (matmul(hidden_v[1], w2_v[...]) + b2_v[...]).astype(BF16)
    send_v[:, 3 * c4 : 3 * c4 + c2] = matmul(order, two).astype(BF16)
    done = 3 * c4 + c2
    outs = [(0, done)] + [(done + i * CHUNK, CHUNK) for i in range(chunks)]
    stores = [
        pltpu.make_async_copy(send_v.at[:, pl.ds(at, size)], send.at[:, pl.ds(at, size)], out_sems.at[i])
        for i, (at, size) in enumerate(outs)
    ]
    stores[0].start()
    for copy in copies[7:9]:
        copy.wait()
    for i in range(chunks):
        copies[9 + i].wait()
        same = (matmul(hidden_v[2], ws_v[i]) + bs_v[:, i * CHUNK : (i + 1) * CHUNK]).astype(BF16)
        send_v[:, done + i * CHUNK : done + (i + 1) * CHUNK] = matmul(order, same).astype(BF16)
        stores[1 + i].start()
    for store in stores:
        store.wait()


def fetch_kernel(w4, b4, b2, w4_v, b4_v, b2_v, sems):
    pairs = ((w4, w4_v), (b4, b4_v), (b2, b2_v))
    copies = [pltpu.make_async_copy(src, dst, sems.at[i]) for i, (src, dst) in enumerate(pairs)]
    for copy in copies:
        copy.start()
    for copy in copies:
        copy.wait()


def finish_kernel(
    arrived, places, w4, b4, b2, wj_hbm, w2_hbm, joined, up_two, same,
    wj, w2, tiles_v, wide_v, acc_v, out_v, acc_two_v, two_v, same_v, weight_sems, sems, rest_sems,
):
    weights = [
        pltpu.make_async_copy(src, dst, weight_sems.at[i]) for i, (src, dst) in enumerate(((wj_hbm, wj), (w2_hbm, w2)))
    ]
    for copy in weights:
        copy.start()
    tok_dev, c4 = arrived.shape[0], w4.shape[0]
    c2 = w2.shape[0]
    row_count = tok_dev // GRID_W
    place = places[0:tok_dev]
    same_v[...] = matmul(place, arrived[:, 3 * c4 + c2 :]).astype(BF16)
    stores = [pltpu.make_async_copy(same_v, same, rest_sems.at[0])]
    stores[0].start()
    widen(arrived, places, w4, b4, tiles_v, wide_v)
    weights[0].wait()
    for chunk in range(row_count):
        stores.append(convolve(chunk, wide_v, wj, joined, acc_v, out_v, sems))
        if chunk == 0:
            weights[1].wait()
            stores += expand_two(arrived, place, w2, b2, 3 * c4, up_two, acc_two_v, two_v, rest_sems)
    for store in stores:
        store.wait()


def widen(arrived, places, w4, b4, tiles_v, wide_v):
    tok_dev, c4 = arrived.shape[0], w4.shape[0]
    row_count = tok_dev // GRID_W
    me = lax.axis_index("rows")
    top = jnp.where(me > 0, 1.0, 0.0)
    bottom = jnp.where(me < lax.axis_size("rows") - 1, 1.0, 0.0)
    bias = b4[...]
    feat = c4

    base = 3 * tok_dev
    tiles_v[0:base] = matmul(places[0:base], arrived[:, 0:c4]).astype(BF16)
    tiles_v[base : base + 3 * GRID_W] = matmul(places[base : base + 3 * GRID_W], arrived[:, c4 : 2 * c4]).astype(BF16)
    base += 3 * GRID_W
    tiles_v[base : base + 3 * GRID_W] = matmul(places[base : base + 3 * GRID_W], arrived[:, 2 * c4 : 3 * c4]).astype(BF16)

    left = jnp.where(iota((GRID_W, 1), 0) == 0, 0.0, 1.0)
    right = jnp.where(iota((GRID_W, 1), 0) == GRID_W - 1, 0.0, 1.0)

    def fill(first, stride, rows, tap, to, scale):
        size = rows * GRID_W
        for b in range(4):
            part = matmul(tiles_v[first : first + size], w4[:, (tap * 4 + b) * feat : (tap * 4 + b + 1) * feat]) + bias
            if scale is not None:
                part = part * scale
            for i in range(rows):
                wide_v[pl.ds(to(i) * GRID_W, GRID_W), (b + 1) * feat : (b + 2) * feat] = part[
                    i * GRID_W : (i + 1) * GRID_W
                ].astype(BF16)
        for b, shift, edge, block in ((3, 1, left, 0), (0, 2, right, 5)):
            start = first + shift * stride
            part = matmul(tiles_v[start : start + size], w4[:, (tap * 4 + b) * feat : (tap * 4 + b + 1) * feat]) + bias
            if scale is not None:
                part = part * scale
            for i in range(rows):
                wide_v[pl.ds(to(i) * GRID_W, GRID_W), block * feat : (block + 1) * feat] = (
                    part[i * GRID_W : (i + 1) * GRID_W] * edge
                ).astype(BF16)

    for tap in range(4):
        fill(0, tok_dev, row_count, tap, lambda i, tap=tap: 4 * i + tap + 1, None)
    fill(3 * tok_dev, GRID_W, 1, 3, lambda i: 0, top)
    fill(3 * tok_dev + 3 * GRID_W, GRID_W, 1, 0, lambda i: 4 * row_count + 1, bottom)


def convolve(chunk, wide_v, wj, joined, acc_v, out_v, sems):
    feat = wj.shape[2]
    for b in range(4):
        total = None
        for row_tap in range(3):
            first = (4 * chunk + row_tap) * GRID_W
            term = matmul(wide_v[first : first + 4 * GRID_W, b * feat : (b + 3) * feat], wj[row_tap])
            total = term if total is None else total + term
        for r in range(4):
            for block in range(feat // 128):
                acc_v[4 * chunk + r, block, pl.ds(b, GRID_W, 4), :] = total[
                    r * GRID_W : (r + 1) * GRID_W, block * 128 : (block + 1) * 128
                ]
    for r in range(4 * chunk, 4 * chunk + 4):
        for block in range(feat // 128):
            out_v[r, :, block * 128 : (block + 1) * 128] = acc_v[r, block].astype(BF16)
    rows = pl.ds(4 * chunk, 4)
    store = pltpu.make_async_copy(out_v.at[rows], joined.at[rows], sems.at[chunk])
    store.start()
    return store


def expand_two(arrived, place, w2, b2, at, up_two, acc_v, out_v, sems):
    c2 = w2.shape[0]
    row_count = arrived.shape[0] // GRID_W
    tile = matmul(place, arrived[:, at : at + c2]).astype(BF16)
    bias = b2[...]
    stores = []
    for a in range(2):
        for b in range(2):
            part = matmul(tile, w2[:, (a * 2 + b) * c2 : (a * 2 + b + 1) * c2]) + bias
            for i in range(row_count):
                for block in range(c2 // 128):
                    acc_v[2 * i + a, block, pl.ds(b, GRID_W, 2), :] = part[
                        i * GRID_W : (i + 1) * GRID_W, block * 128 : (block + 1) * 128
                    ]
        for i in range(row_count):
            r = 2 * i + a
            for block in range(c2 // 128):
                out_v[r, :, block * 128 : (block + 1) * 128] = acc_v[r, block].astype(BF16)
            store = pltpu.make_async_copy(out_v.at[r], up_two.at[r], sems.at[1 + r])
            store.start()
            stores.append(store)
    return stores


def body(
    hidden_states,
    cell_of,
    proj_four_weight,
    proj_four_bias,
    proj_two_weight,
    proj_two_bias,
    proj_same_weight,
    proj_same_bias,
    up4_weight,
    up4_bias,
    up2_weight,
    up2_bias,
    join_weight,
):
    hooks, tok_dev, hid = hidden_states.shape
    shards = lax.axis_size("rows")
    per_peer = tok_dev // shards
    row_count = tok_dev // GRID_W
    c4, c2, cs = proj_four_weight.shape[1], proj_two_weight.shape[1], proj_same_weight.shape[1]
    feat = join_weight.shape[3]
    table = cell_of.reshape(shards, tok_dev)
    place_rows = 3 * tok_dev + 6 * GRID_W
    shape = jax.ShapeDtypeStruct

    total = 3 * c4 + c2 + cs
    biases = [bias.reshape(1, -1) for bias in (proj_four_bias, proj_two_bias, proj_same_bias)]
    inputs = (
        hidden_states,
        table,
        proj_four_weight,
        biases[0],
        proj_two_weight,
        biases[1],
        proj_same_weight,
        biases[2],
    )
    send, places = pl.pallas_call(
        project_kernel,
        out_shape=(pltpu.HBM((tok_dev, total), BF16), pltpu.VMEM((place_rows, tok_dev), BF16)),
        in_specs=[ANY] * 8,
        out_specs=(ANY, VMEM),
        scratch_shapes=[
            pltpu.VMEM(hidden_states.shape, BF16),
            pltpu.VMEM(table.shape, jnp.int32),
            pltpu.VMEM((hid, c4), BF16),
            pltpu.VMEM((hid, c2), BF16),
            pltpu.VMEM((cs // CHUNK, hid, CHUNK), BF16),
            pltpu.VMEM((1, c4), F32),
            pltpu.VMEM((1, c2), F32),
            pltpu.VMEM((1, cs), F32),
            pltpu.VMEM((tok_dev, total), BF16),
            pltpu.SemaphoreType.DMA((9 + cs // CHUNK,)),
            pltpu.SemaphoreType.DMA((1 + cs // CHUNK,)),
        ],
        compiler_params=pltpu.CompilerParams(vmem_limit_bytes=12 << 20),
        cost_estimate=pl.CostEstimate(flops=2 * tok_dev * hid * (c4 + c2 + cs), bytes_accessed=5 << 20, transcendentals=0),
        name="project",
    )(*(in_hbm(x) for x in inputs))
    arrived = lax.all_to_all(
        send.reshape(shards, per_peer, total), "rows", split_axis=0, concat_axis=0, tiled=True
    ).reshape(tok_dev, total)

    weights = (up4_weight, up4_bias.reshape(1, -1), up2_bias.reshape(1, -1))
    w4, b4, b2 = pl.pallas_call(
        fetch_kernel,
        out_shape=tuple(pltpu.VMEM(w.shape, w.dtype) for w in weights),
        in_specs=[ANY] * 3,
        out_specs=(VMEM,) * 3,
        scratch_shapes=[pltpu.SemaphoreType.DMA((3,))],
        cost_estimate=pl.CostEstimate(flops=1 << 30, bytes_accessed=2 << 20, transcendentals=0),
        name="fetch",
        compiler_params=pltpu.CompilerParams(vmem_limit_bytes=4 << 20),
    )(*(in_hbm(w) for w in weights))

    out_rows = 4 * row_count
    joined, upsampled_two, same_scale = pl.pallas_call(
        finish_kernel,
        out_shape=(
            shape((out_rows, 4 * GRID_W, feat), BF16),
            shape((2 * row_count, 2 * GRID_W, c2), BF16),
            shape((tok_dev, cs), BF16),
        ),
        in_specs=[VMEM] * 5 + [ANY] * 2,
        out_specs=(ANY, ANY, ANY),
        scratch_shapes=[
            pltpu.VMEM((3, 3 * c4, feat), BF16),
            pltpu.VMEM(up2_weight.shape, BF16),
            pltpu.VMEM((place_rows, c4), BF16),
            pltpu.VMEM(((out_rows + 2) * GRID_W, 6 * c4), BF16),
            pltpu.VMEM((out_rows, feat // 128, 4 * GRID_W, 128), F32),
            pltpu.VMEM((out_rows, 4 * GRID_W, feat), BF16),
            pltpu.VMEM((2 * row_count, c2 // 128, 2 * GRID_W, 128), F32),
            pltpu.VMEM((2 * row_count, 2 * GRID_W, c2), BF16),
            pltpu.VMEM((tok_dev, cs), BF16),
            pltpu.SemaphoreType.DMA((2,)),
            pltpu.SemaphoreType.DMA((row_count,)),
            pltpu.SemaphoreType.DMA((1 + 2 * row_count,)),
        ],
        compiler_params=pltpu.CompilerParams(vmem_limit_bytes=24 << 20),
        cost_estimate=pl.CostEstimate(flops=4 << 30, bytes_accessed=4 << 20, transcendentals=0),
        name="finish",
    )(arrived, places, w4, b4, b2, in_hbm(join_weight.reshape(3, 3 * c4, feat)), in_hbm(up2_weight))
    return (joined, upsampled_two, same_scale.reshape(row_count, GRID_W, cs))


def solution(mesh):
    return jax.shard_map(
        body,
        mesh=mesh,
        in_specs=(P(None, ("img", "rows"), None),) + (P(),) * 12,
        out_specs=(P(("img", "rows"), None, None),) * 3,
        check_vma=False,
    )
```

time: 38 us -> 34.2 us (0.900)
  blocking collectives: 16.2 us -> 0 us
  waiting for transfers between devices: 5.09 us -> 13.7 us
  starting transfers between devices: 3.55 us -> 7.43 us
    all_to_all x1 -> x0, blocking collectives: 16.2 us -> none  [body(): exchange(send_four.reshape(shards, per_peer, 3 * c4))]
    all_to_all x1, waiting for transfers between devices: 5.09 us -> 13.7 us  [body(): lax.all_to_all(send.reshape(shards, per_peer, total), 'rows', split_axis=...]
    all_to_all x1, starting transfers between devices: 3.55 us -> 7.43 us  [body(): lax.all_to_all(send.reshape(shards, per_peer, total), 'rows', split_axis=...]
    pallas_call x1, Pallas kernels: 2.65 us -> 1.62 us  [body(): pl.pallas_call(fetch_kernel, out_shape=tuple((pltpu.VMEM(w.shape, w.dtype...]
    pallas_call x3 -> x2, Pallas kernels: 9.61 us -> 10.5 us  [the longest x1 5.83 us: body(): pl.pallas_call(finish_kernel, out_shape=(shape((out_rows, 4 * GRID_W, fea...]
  transfers between devices with their start and end apart: 1 -> 1, of which waited for: 1 -> 1; matrix products, arithmetic and copies ran while one was open for 0% -> 0% of each run, Pallas kernels for 19% -> 5%
where the time goes in v2:
time: 34.2 us; the launch traced here: 34 us
  waiting for transfers between devices  13.7 us (40%)
  Pallas kernels  12.1 us (35%)
  starting transfers between devices  7.43 us (22%)
  between operations  0.66 us (2%)
    all_to_all x1, waiting for transfers between devices, body(): lax.all_to_all(send.reshape(shards, per_peer, total), 'rows', split_axis=...  13.7 us
    all_to_all x1, starting transfers between devices, body(): lax.all_to_all(send.reshape(shards, per_peer, total), 'rows', split_axis=...  7.43 us
    pallas_call x1, Pallas kernels, body(): pl.pallas_call(finish_kernel, out_shape=(shape((out_rows, 4 * GRID_W, fea...  5.83 us
    pallas_call x1, Pallas kernels, body(): pl.pallas_call(project_kernel, out_shape=(pltpu.HBM((tok_dev, total), BF1...  4.69 us
    pallas_call x1, Pallas kernels, body(): pl.pallas_call(fetch_kernel, out_shape=tuple((pltpu.VMEM(w.shape, w.dtype...  1.62 us
  transfers between devices with their start and end apart: 1, of which 1 were waited for; matrix products, arithmetic and copies ran while one was open for 0% of the time, Pallas kernels for 5%

profile of v2, /device:TPU:0, one launch (start us, length us, event | category | flops | bytes accessed | tf_op | source)
XLA Modules:
  0.0 34.0 jit_solution(1601822579585179647)
XLA Ops:
  0.6 4.7 %project.1 = (bf16[128,2304]{1,0:T(8,128)(2,1)}, bf16[768,128]{1,0:T(8,128)(2,1)S(1)}) custom-call(bf16[3,128,1024]{2,1,0:T(8,128)(2,1)} %hidden.1, s32[16,128]{1,0:T(8,128)} %bitcast.12, bf16[1024,256]{1,0:T(8,128)(2,1)} %w4.2, f32[1,256]{1,0:T(1,128)} %bitcast.15, bf16[1024,512]{1,0:T(8,128)(2,1)} %w2.1, f32[1,512]{1,0:T(1,128)} %bitcast.14, ...), custom_call_target="tpu_custom_call" | custom-call | flops 469762048 | bytes 5242880 | tf_op jit(solution)/shard_map/project/pallas_call | solution.py:304
  5.3 7.4 %all-to-all-start = ((bf16[16,8,2304]{2,1,0:T(8,128)(2,1)}), bf16[16,8,2304]{2,1,0:T(8,128)(2,1)S(1)}, u32[]{:S(2)}, u32[]{:S(2)}) async-start(bf16[16,8,2304]{2,1,0:T(8,128)(2,1)} %bitcast.11), calls=%async_computation | async-start | bytes 1179648 | tf_op jit(solution)/shard_map/all_to_all | solution.py:326
  12.8 1.6 %fetch.1 = (bf16[256,4096]{1,0:T(8,128)(2,1)S(1)}, f32[1,256]{1,0:T(1,128)S(1)}, f32[1,512]{1,0:T(1,128)S(1)}) custom-call(bf16[256,4096]{1,0:T(8,128)(2,1)} %w4.3, f32[1,256]{1,0:T(1,128)} %bitcast.18, f32[1,512]{1,0:T(1,128)} %bitcast.17), custom_call_target="tpu_custom_call" | custom-call | flops 1073741824 | bytes 2097152 | tf_op jit(solution)/shard_map/fetch/pallas_call | solution.py:331
  14.4 13.7 %all-to-all-done = bf16[16,8,2304]{2,1,0:T(8,128)(2,1)S(1)} async-done(((bf16[16,8,2304]{2,1,0:T(8,128)(2,1)}), bf16[16,8,2304]{2,1,0:T(8,128)(2,1)S(1)}, u32[]{:S(2)}, u32[]{:S(2)}) %all-to-all-start) | async-done | bytes 589856 | tf_op jit(solution)/shard_map/all_to_all | solution.py:326
  28.1 5.8 %finish.1 = (bf16[8,256,256]{2,1,0:T(8,128)(2,1)}, bf16[4,128,512]{2,1,0:T(8,128)(2,1)}, bf16[128,1024]{1,0:T(8,128)(2,1)}) custom-call(bf16[128,2304]{1,0:T(8,128)(2,1)S(1)} %bitcast.10, bf16[768,128]{1,0:T(8,128)(2,1)S(1)} %get-tuple-element.12.places, bf16[256,4096]{1,0:T(8,128)(2,1)S(1)} %get-tuple-element.13.w4, f32[1,256]{1,0:T(1,128)S(1)} %get-tuple-element.14.b4, ...), custom_call_target="tpu_custom_call" | custom-call | flops 4294967296 | bytes 4194304 | tf_op jit(solution)/shard_map/finish/pallas_call | solution.py:343
Async XLA Ops:
  5.3 22.8 %all-to-all-start = ((bf16[16,8,2304]{2,1,0:T(8,128)(2,1)}), bf16[16,8,2304]{2,1,0:T(8,128)(2,1)S(1)}, u32[]{:S(2)}, u32[]{:S(2)}) async-start(bf16[16,8,2304]{2,1,0:T(8,128)(2,1)} %bitcast.11), calls=%async_computation | async-start | bytes 1179648 | tf_op jit(solution)/shard_map/all_to_all | solution.py:326

commit v3 on v2

--- a/solution.py
+++ b/solution.py
@@ -7,6 +7,7 @@
 from jax.experimental.pallas import tpu as pltpu
 from jax.sharding import PartitionSpec as P
 
+
 GRID_W = 64
 CHUNK = 256
 F32 = jnp.float32
@@ -36,7 +37,11 @@
     return jnp.sum(jnp.where(same, jnp.broadcast_to(row, (size, size)), 0.0), axis=1, keepdims=True)
 
 
-def landing(table, block, tok_dev, per_peer):
+def low_part(shards):
+    return 1 << ((shards.bit_length()) // 2)
+
+
+def landing(table, block, tok_dev, per_peer, flip=0):
     shards = table.shape[0]
     start = block * tok_dev
     inside = jnp.logical_and(table >= start, table < start + tok_dev)
@@ -49,29 +54,33 @@
         hit = jnp.logical_and(inside, rank == float(k))
         found = jnp.sum(jnp.where(hit, place, 0.0), axis=1, keepdims=True)
         spread = spread + jnp.where(lax.rem(lane, per_peer) == k, found, 0.0)
-    own = lax.div(lane, per_peer) == iota((shards, tok_dev), 0)
+    own = lax.div(lane, per_peer) == jnp.bitwise_xor(iota((shards, tok_dev), 0), flip)
     return jnp.sum(jnp.where(own, spread, 0.0), axis=0, keepdims=True).astype(jnp.int32)
 
 
-def project_kernel(
-    hidden, table_hbm, w4, b4, w2, b2, ws, bs, send, places_v,
-    hidden_v, table_v, w4_v, w2_v, ws_v, b4_v, b2_v, bs_v, send_v, sems, out_sems,
-):
-    chunks = ws.shape[1] // CHUNK
-    pairs = [
-        (table_hbm, table_v),
-        (hidden.at[0], hidden_v.at[0]),
-        (b4, b4_v),
-        (w4, w4_v),
-        (hidden.at[1], hidden_v.at[1]),
-        (b2, b2_v),
-        (w2, w2_v),
-        (hidden.at[2], hidden_v.at[2]),
-        (bs, bs_v),
-    ] + [(ws.at[:, pl.ds(i * CHUNK, CHUNK)], ws_v.at[i]) for i in range(chunks)]
+def start_all(pairs, sems):
     copies = [pltpu.make_async_copy(src, dst, sems.at[i]) for i, (src, dst) in enumerate(pairs)]
     for copy in copies:
         copy.start()
+    return copies
+
+
+def project_kernel(
+    hidden, table_hbm, w4, b4, w2, b2, send, places_v, order_v,
+    hidden_v, table_v, w4_v, w2_v, b4_v, b2_v, send_v, sems, out_sems,
+):
+    copies = start_all(
+        [
+            (table_hbm, table_v),
+            (hidden.at[0], hidden_v.at[0]),
+            (b4, b4_v),
+            (w4, w4_v),
+            (hidden.at[1], hidden_v.at[1]),
+            (b2, b2_v),
+            (w2, w2_v),
+        ],
+        sems,
+    )
     shards, tok_dev = table_v.shape
     per_peer = tok_dev // shards
     me = lax.axis_index("rows")
@@ -87,6 +96,11 @@
     order = one_hot(iota(square, 0) == slot)
     order_above = one_hot(iota(square, 0) == slot + per_peer)
     order_below = one_hot(iota(square, 0) == slot - per_peer)
+
+    low = low_part(shards)
+    apart = jnp.bitwise_xor(block_row, me)
+    turn = lax.rem(apart, low) * (shards // low) + lax.div(apart, low)
+    order_v[...] = one_hot(iota(square, 0) == turn * per_peer + within)
 
     own = landing(table, me, tok_dev, per_peer)
     above = landing(table, me - 1, tok_dev, per_peer)
@@ -108,6 +122,8 @@
         )
         base += 3 * GRID_W
 
+    places_v[base : base + tok_dev] = one_hot(cell == landing(table, me, tok_dev, per_peer, me))
+
     for copy in copies[1:4]:
         copy.wait()
     c4 = w4_v.shape[1]
@@ -115,61 +131,70 @@
     send_v[:, 0:c4] = matmul(order, four).astype(BF16)
     send_v[:, c4 : 2 * c4] = matmul(order_above, four).astype(BF16)
     send_v[:, 2 * c4 : 3 * c4] = matmul(order_below, four).astype(BF16)
+    cuts = (slice(0, 3 * c4), slice(3 * c4, send_v.shape[1]))
+    stores = [
+        pltpu.make_async_copy(send_v.at[:, cut], send.at[:, cut], out_sems.at[i]) for i, cut in enumerate(cuts)
+    ]
+    stores[0].start()
     for copy in copies[4:7]:
         copy.wait()
-    c2 = w2_v.shape[1]
     two = (matmul(hidden_v[1], w2_v[...]) + b2_v[...]).astype(BF16)
-    send_v[:, 3 * c4 : 3 * c4 + c2] = matmul(order, two).astype(BF16)
-    done = 3 * c4 + c2
-    outs = [(0, done)] + [(done + i * CHUNK, CHUNK) for i in range(chunks)]
-    stores = [
-        pltpu.make_async_copy(send_v.at[:, pl.ds(at, size)], send.at[:, pl.ds(at, size)], out_sems.at[i])
-        for i, (at, size) in enumerate(outs)
-    ]
-    stores[0].start()
-    for copy in copies[7:9]:
-        copy.wait()
-    for i in range(chunks):
-        copies[9 + i].wait()
-        same = (matmul(hidden_v[2], ws_v[i]) + bs_v[:, i * CHUNK : (i + 1) * CHUNK]).astype(BF16)
-        send_v[:, done + i * CHUNK : done + (i + 1) * CHUNK] = matmul(order, same).astype(BF16)
-        stores[1 + i].start()
+    send_v[:, 3 * c4 :] = matmul(order, two).astype(BF16)
+    stores[1].start()
     for store in stores:
         store.wait()
 
 
+def same_kernel(hidden, ws, bs, order, *refs):
+    count = len(refs) - 4
+    outs, (hidden_v, ws_v, bs_v, sems) = refs[:count], refs[count:]
+    chunks = ws.shape[1] // CHUNK
+    copies = start_all(
+        [(hidden.at[2], hidden_v), (bs, bs_v)]
+        + [(ws.at[:, pl.ds(i * CHUNK, CHUNK)], ws_v.at[i]) for i in range(chunks)],
+        sems,
+    )
+    copies[0].wait()
+    copies[1].wait()
+    rows = outs[0].shape[0]
+    for i in range(chunks):
+        cut = slice(i * CHUNK, (i + 1) * CHUNK)
+        copies[2 + i].wait()
+        same = (matmul(hidden_v[...], ws_v[i]) + bs_v[:, cut]).astype(BF16)
+        sent = matmul(order[...], same).astype(BF16)
+        for k, out in enumerate(outs):
+            out[:, cut] = sent[k * rows : (k + 1) * rows]
+
+
+def turn_kernel(low_count, *refs):
+    lows, highs = refs[:low_count], refs[low_count:]
+    rows = lows[0].shape[0] // len(highs)
+    for h, high in enumerate(highs):
+        for k, low in enumerate(lows):
+            high[k * rows : (k + 1) * rows] = low[h * rows : (h + 1) * rows]
+
+
 def fetch_kernel(w4, b4, b2, w4_v, b4_v, b2_v, sems):
-    pairs = ((w4, w4_v), (b4, b4_v), (b2, b2_v))
-    copies = [pltpu.make_async_copy(src, dst, sems.at[i]) for i, (src, dst) in enumerate(pairs)]
-    for copy in copies:
-        copy.start()
-    for copy in copies:
+    for copy in start_all([(w4, w4_v), (b4, b4_v), (b2, b2_v)], sems):
         copy.wait()
 
 
 def finish_kernel(
-    arrived, places, w4, b4, b2, wj_hbm, w2_hbm, joined, up_two, same,
-    wj, w2, tiles_v, wide_v, acc_v, out_v, acc_two_v, two_v, same_v, weight_sems, sems, rest_sems,
+    arrived, places, w4, b4, b2, wj_hbm, w2_hbm, joined, up_two,
+    wj, w2, tiles_v, wide_v, acc_v, out_v, acc_two_v, two_v, weight_sems, sems, two_sems,
 ):
-    weights = [
-        pltpu.make_async_copy(src, dst, weight_sems.at[i]) for i, (src, dst) in enumerate(((wj_hbm, wj), (w2_hbm, w2)))
-    ]
-    for copy in weights:
-        copy.start()
+    weights = start_all([(wj_hbm, wj), (w2_hbm, w2)], weight_sems)
     tok_dev, c4 = arrived.shape[0], w4.shape[0]
-    c2 = w2.shape[0]
     row_count = tok_dev // GRID_W
     place = places[0:tok_dev]
-    same_v[...] = matmul(place, arrived[:, 3 * c4 + c2 :]).astype(BF16)
-    stores = [pltpu.make_async_copy(same_v, same, rest_sems.at[0])]
-    stores[0].start()
+    stores = []
     widen(arrived, places, w4, b4, tiles_v, wide_v)
     weights[0].wait()
     for chunk in range(row_count):
         stores.append(convolve(chunk, wide_v, wj, joined, acc_v, out_v, sems))
         if chunk == 0:
             weights[1].wait()
-            stores += expand_two(arrived, place, w2, b2, 3 * c4, up_two, acc_two_v, two_v, rest_sems)
+            stores += expand_two(arrived, place, w2, b2, 3 * c4, up_two, acc_two_v, two_v, two_sems)
     for store in stores:
         store.wait()
 
@@ -258,10 +283,19 @@
             r = 2 * i + a
             for block in range(c2 // 128):
                 out_v[r, :, block * 128 : (block + 1) * 128] = acc_v[r, block].astype(BF16)
-            store = pltpu.make_async_copy(out_v.at[r], up_two.at[r], sems.at[1 + r])
+            store = pltpu.make_async_copy(out_v.at[r], up_two.at[r], sems.at[r])
             store.start()
             stores.append(store)
     return stores
+
+
+def place_kernel(places, *refs):
+    arrived, same, rows_v = refs[:-2], refs[-2], refs[-1]
+    rows = arrived[0].shape[0]
+    for h, piece in enumerate(arrived):
+        rows_v[h * rows : (h + 1) * rows] = piece[...]
+    tok_dev = rows_v.shape[0]
+    same[...] = matmul(places[places.shape[0] - tok_dev :], rows_v[...]).astype(BF16)
 
 
 def body(
@@ -279,53 +313,78 @@
     up2_bias,
     join_weight,
 ):
-    hooks, tok_dev, hid = hidden_states.shape
+    _, tok_dev, hid = hidden_states.shape
     shards = lax.axis_size("rows")
     per_peer = tok_dev // shards
     row_count = tok_dev // GRID_W
     c4, c2, cs = proj_four_weight.shape[1], proj_two_weight.shape[1], proj_same_weight.shape[1]
     feat = join_weight.shape[3]
     table = cell_of.reshape(shards, tok_dev)
-    place_rows = 3 * tok_dev + 6 * GRID_W
+    place_rows = 4 * tok_dev + 6 * GRID_W
     shape = jax.ShapeDtypeStruct
 
-    total = 3 * c4 + c2 + cs
+    total = 3 * c4 + c2
+    low = low_part(shards)
+    high = shards // low
     biases = [bias.reshape(1, -1) for bias in (proj_four_bias, proj_two_bias, proj_same_bias)]
-    inputs = (
-        hidden_states,
-        table,
-        proj_four_weight,
-        biases[0],
-        proj_two_weight,
-        biases[1],
-        proj_same_weight,
-        biases[2],
-    )
-    send, places = pl.pallas_call(
+    inputs = (hidden_states, table, proj_four_weight, biases[0], proj_two_weight, biases[1])
+    send, places, order = pl.pallas_call(
         project_kernel,
-        out_shape=(pltpu.HBM((tok_dev, total), BF16), pltpu.VMEM((place_rows, tok_dev), BF16)),
-        in_specs=[ANY] * 8,
-        out_specs=(ANY, VMEM),
+        out_shape=(
+            pltpu.HBM((tok_dev, total), BF16),
+            pltpu.VMEM((place_rows, tok_dev), BF16),
+            pltpu.VMEM((tok_dev, tok_dev), BF16),
+        ),
+        in_specs=[ANY] * 6,
+        out_specs=(ANY, VMEM, VMEM),
         scratch_shapes=[
-            pltpu.VMEM(hidden_states.shape, BF16),
+            pltpu.VMEM((2, tok_dev, hid), BF16),
             pltpu.VMEM(table.shape, jnp.int32),
             pltpu.VMEM((hid, c4), BF16),
             pltpu.VMEM((hid, c2), BF16),
-            pltpu.VMEM((cs // CHUNK, hid, CHUNK), BF16),
             pltpu.VMEM((1, c4), F32),
             pltpu.VMEM((1, c2), F32),
-            pltpu.VMEM((1, cs), F32),
             pltpu.VMEM((tok_dev, total), BF16),
-            pltpu.SemaphoreType.DMA((9 + cs // CHUNK,)),
-            pltpu.SemaphoreType.DMA((1 + cs // CHUNK,)),
+            pltpu.SemaphoreType.DMA((7,)),
+            pltpu.SemaphoreType.DMA((2,)),
         ],
-        compiler_params=pltpu.CompilerParams(vmem_limit_bytes=12 << 20),
-        cost_estimate=pl.CostEstimate(flops=2 * tok_dev * hid * (c4 + c2 + cs), bytes_accessed=5 << 20, transcendentals=0),
+        compiler_params=pltpu.CompilerParams(vmem_limit_bytes=8 << 20),
+        cost_estimate=pl.CostEstimate(flops=2 * tok_dev * hid * (c4 + c2), bytes_accessed=2 << 20, transcendentals=0),
         name="project",
     )(*(in_hbm(x) for x in inputs))
     arrived = lax.all_to_all(
         send.reshape(shards, per_peer, total), "rows", split_axis=0, concat_axis=0, tiled=True
     ).reshape(tok_dev, total)
+    sent = pl.pallas_call(
+        same_kernel,
+        out_shape=(shape((high * per_peer, cs), BF16),) * low,
+        in_specs=[ANY, ANY, ANY, VMEM],
+        out_specs=(VMEM,) * low,
+        scratch_shapes=[
+            pltpu.VMEM((tok_dev, hid), BF16),
+            pltpu.VMEM((cs // CHUNK, hid, CHUNK), BF16),
+            pltpu.VMEM((1, cs), F32),
+            pltpu.SemaphoreType.DMA((2 + cs // CHUNK,)),
+        ],
+        compiler_params=pltpu.CompilerParams(vmem_limit_bytes=8 << 20),
+        cost_estimate=pl.CostEstimate(flops=2 * tok_dev * hid * cs, bytes_accessed=3 << 20, transcendentals=0),
+        name="same",
+    )(in_hbm(hidden_states), in_hbm(proj_same_weight), in_hbm(biases[2]), order)
+
+    def swap(piece, step):
+        return lax.ppermute(piece, "rows", [(i, i ^ step) for i in range(shards)])
+
+    crossed = [sent[0]] + [swap(sent[k], k) for k in range(1, low)]
+    turned = pl.pallas_call(
+        functools.partial(turn_kernel, low),
+        out_shape=(shape((low * per_peer, cs), BF16),) * high,
+        in_specs=[VMEM] * low,
+        out_specs=(VMEM,) * high,
+        compiler_params=pltpu.CompilerParams(vmem_limit_bytes=4 << 20),
+        cost_estimate=pl.CostEstimate(flops=1 << 26, bytes_accessed=1 << 20, transcendentals=0),
+        name="turn",
+    )(*crossed)
+    landed = [turned[0]] + [swap(turned[h], h * low) for h in range(1, high)]
 
     weights = (up4_weight, up4_bias.reshape(1, -1), up2_bias.reshape(1, -1))
     w4, b4, b2 = pl.pallas_call(
@@ -335,20 +394,19 @@
         out_specs=(VMEM,) * 3,
         scratch_shapes=[pltpu.SemaphoreType.DMA((3,))],
         cost_estimate=pl.CostEstimate(flops=1 << 30, bytes_accessed=2 << 20, transcendentals=0),
+        compiler_params=pltpu.CompilerParams(vmem_limit_bytes=4 << 20),
         name="fetch",
-        compiler_params=pltpu.CompilerParams(vmem_limit_bytes=4 << 20),
     )(*(in_hbm(w) for w in weights))
 
     out_rows = 4 * row_count
-    joined, upsampled_two, same_scale = pl.pallas_call(
+    joined, upsampled_two = pl.pallas_call(
         finish_kernel,
         out_shape=(
             shape((out_rows, 4 * GRID_W, feat), BF16),
             shape((2 * row_count, 2 * GRID_W, c2), BF16),
-            shape((tok_dev, cs), BF16),
         ),
         in_specs=[VMEM] * 5 + [ANY] * 2,
-        out_specs=(ANY, ANY, ANY),
+        out_specs=(ANY, ANY),
         scratch_shapes=[
             pltpu.VMEM((3, 3 * c4, feat), BF16),
             pltpu.VMEM(up2_weight.shape, BF16),
@@ -358,15 +416,24 @@
             pltpu.VMEM((out_rows, 4 * GRID_W, feat), BF16),
             pltpu.VMEM((2 * row_count, c2 // 128, 2 * GRID_W, 128), F32),
             pltpu.VMEM((2 * row_count, 2 * GRID_W, c2), BF16),
-            pltpu.VMEM((tok_dev, cs), BF16),
             pltpu.SemaphoreType.DMA((2,)),
             pltpu.SemaphoreType.DMA((row_count,)),
-            pltpu.SemaphoreType.DMA((1 + 2 * row_count,)),
+            pltpu.SemaphoreType.DMA((2 * row_count,)),
         ],
         compiler_params=pltpu.CompilerParams(vmem_limit_bytes=24 << 20),
         cost_estimate=pl.CostEstimate(flops=4 << 30, bytes_accessed=4 << 20, transcendentals=0),
         name="finish",
     )(arrived, places, w4, b4, b2, in_hbm(join_weight.reshape(3, 3 * c4, feat)), in_hbm(up2_weight))
+    same_scale = pl.pallas_call(
+        place_kernel,
+        out_shape=shape((tok_dev, cs), BF16),
+        in_specs=[VMEM] * (1 + high),
+        out_specs=VMEM,
+        scratch_shapes=[pltpu.VMEM((tok_dev, cs), BF16)],
+        compiler_params=pltpu.CompilerParams(vmem_limit_bytes=4 << 20),
+        cost_estimate=pl.CostEstimate(flops=1 << 26, bytes_accessed=1 << 20, transcendentals=0),
+        name="place",
+    )(places, *landed)
     return (joined, upsampled_two, same_scale.reshape(row_count, GRID_W, cs))
 
 

time: 34.2 us -> 37.9 us (1.11)
  starting transfers between devices: 7.43 us -> 14.2 us
  waiting for transfers between devices: 13.7 us -> 8.77 us
  Pallas kernels: 12.1 us -> 14 us
    all_to_all x1, waiting for transfers between devices: 13.7 us -> 0.01 us  [body(): lax.all_to_all(send.reshape(shards, per_peer, total), 'rows', split_axis=...]
    ppermute x0 -> x6, waiting for transfers between devices: none -> 8.77 us  [swap(): return lax.ppermute(piece, 'rows', [(i, i ^ step) for i in range(shards)])]
    ppermute x0 -> x6, starting transfers between devices: none -> 6.76 us  [swap(): return lax.ppermute(piece, 'rows', [(i, i ^ step) for i in range(shards)])]
    pallas_call x0 -> x3, Pallas kernels: none -> 3.88 us  [the longest x1 2.94 us: body(): pl.pallas_call(same_kernel, out_shape=(shape((high * per_peer, cs), BF16)...]
    pallas_call x1, Pallas kernels: 4.69 us -> 2.89 us  [body(): pl.pallas_call(project_kernel, out_shape=(pltpu.HBM((tok_dev, total), BF1...]
  transfers between devices with their start and end apart: 1 -> 7, of which waited for: 1 -> 3; matrix products, arithmetic and copies ran while one was open for 0% -> 0% of each run, Pallas kernels for 5% -> 15%
where the time goes in v3:
time: 37.9 us; the launch traced here: 37.7 us
  starting transfers between devices  14.2 us (37%)
  Pallas kernels  14 us (37%)
  waiting for transfers between devices  8.77 us (23%)
  between operations  0.68 us (2%)
    ppermute x6, waiting for transfers between devices, swap(): return lax.ppermute(piece, 'rows', [(i, i ^ step) for i in range(shards)])  8.77 us
    all_to_all x1, starting transfers between devices, body(): lax.all_to_all(send.reshape(shards, per_peer, total), 'rows', split_axis=...  7.43 us
    ppermute x6, starting transfers between devices, swap(): return lax.ppermute(piece, 'rows', [(i, i ^ step) for i in range(shards)])  6.76 us
    pallas_call x1, Pallas kernels, body(): pl.pallas_call(finish_kernel, out_shape=(shape((out_rows, 4 * GRID_W, fea...  5.63 us
    pallas_call x1, Pallas kernels, body(): pl.pallas_call(same_kernel, out_shape=(shape((high * per_peer, cs), BF16)...  2.94 us
    pallas_call x1, Pallas kernels, body(): pl.pallas_call(project_kernel, out_shape=(pltpu.HBM((tok_dev, total), BF1...  2.89 us
    pallas_call x1, Pallas kernels, body(): pl.pallas_call(fetch_kernel, out_shape=tuple((pltpu.VMEM(w.shape, w.dtype...  1.62 us
    pallas_call x1, Pallas kernels, body(): pl.pallas_call(place_kernel, out_shape=shape((tok_dev, cs), BF16), in_spe...  0.92 us
  transfers between devices with their start and end apart: 7, of which 3 were waited for; matrix products, arithmetic and copies ran while one was open for 0% of the time, Pallas kernels for 15%

profile of v3, /device:TPU:0, one launch (start us, length us, event | category | flops | bytes accessed | tf_op | source)
XLA Modules:
  0.0 37.7 jit_solution(17851374988319654937)
XLA Ops:
  0.6 2.9 %project.1 = (bf16[128,1280]{1,0:T(8,128)(2,1)}, bf16[896,128]{1,0:T(8,128)(2,1)S(1)}, bf16[128,128]{1,0:T(8,128)(2,1)S(1)}) custom-call(bf16[3,128,1024]{2,1,0:T(8,128)(2,1)} %hidden.3, s32[16,128]{1,0:T(8,128)} %bitcast.13, bf16[1024,256]{1,0:T(8,128)(2,1)} %w4.2, f32[1,256]{1,0:T(1,128)} %bitcast.16, bf16[1024,512]{1,0:T(8,128)(2,1)} %w2.1, f32[1,512]{1,0:T(1,128)} %bitcast.15), custom_call_target="tpu_custom_call" | custom-call | flops 201326592 | bytes 2097152 | tf_op jit(solution)/shard_map/project/pallas_call | solution.py:331
  3.5 7.4 %all-to-all-start = ((bf16[16,8,1280]{2,1,0:T(8,128)(2,1)}), bf16[16,8,1280]{2,1,0:T(8,128)(2,1)S(1)}, u32[]{:S(2)}, u32[]{:S(2)}) async-start(bf16[16,8,1280]{2,1,0:T(8,128)(2,1)} %bitcast.11), calls=%async_computation | async-start | bytes 655360 | tf_op jit(solution)/shard_map/all_to_all | solution.py:355
  11.0 2.9 %same.1 = (bf16[32,1024]{1,0:T(8,128)(2,1)S(1)}, bf16[32,1024]{1,0:T(8,128)(2,1)S(1)}, bf16[32,1024]{1,0:T(8,128)(2,1)S(1)}, bf16[32,1024]{1,0:T(8,128)(2,1)S(1)}) custom-call(bf16[3,128,1024]{2,1,0:T(8,128)(2,1)} %hidden.3, bf16[1024,1024]{1,0:T(8,128)(2,1)} %ws.1, f32[1,1024]{1,0:T(1,128)} %bitcast.14, bf16[128,128]{1,0:T(8,128)(2,1)S(1)} %get-tuple-element.26.order), custom_call_target="tpu_custom_call" | custom-call | flops 268435456 | bytes 3145728 | tf_op jit(solution)/shard_map/same/pallas_call | solution.py:358
  13.9 0.5 %collective-permute-start = (bf16[32,1024]{1,0:T(8,128)(2,1)S(1)}, bf16[32,1024]{1,0:T(8,128)(2,1)S(1)}, u32[]{:S(2)}, u32[]{:S(2)}) collective-permute-start(bf16[32,1024]{1,0:T(8,128)(2,1)S(1)} %get-tuple-element.28), channel_id=1, source_target_pairs={{0,1},{1,0},{2,3},{3,2},{4,5},{5,4},{6,7},{7,6},{8,9},{9,8},{10,11... | collective-permute-start | bytes 196616 | tf_op jit(solution)/shard_map/ppermute | solution.py:375
  14.4 1.6 %collective-permute-start.1 = (bf16[32,1024]{1,0:T(8,128)(2,1)S(1)}, bf16[32,1024]{1,0:T(8,128)(2,1)S(1)}, u32[]{:S(2)}, u32[]{:S(2)}) collective-permute-start(bf16[32,1024]{1,0:T(8,128)(2,1)S(1)} %get-tuple-element.29), channel_id=1, source_target_pairs={{0,2},{1,3},{2,0},{3,1},{4,6},{5,7},{6,4},{7,5},{8,10},{9,11},{10,... | collective-permute-start | bytes 196616 | tf_op jit(solution)/shard_map/ppermute | solution.py:375
  16.0 0.0 collective-permute-start.2
  16.0 0.0 collective-permute-done.refs_1_
  16.0 3.4 %collective-permute-done.1.refs_2_ = bf16[32,1024]{1,0:T(8,128)(2,1)S(1)} collective-permute-done((bf16[32,1024]{1,0:T(8,128)(2,1)S(1)}, bf16[32,1024]{1,0:T(8,128)(2,1)S(1)}, u32[]{:S(2)}, u32[]{:S(2)}) %collective-permute-start.1) | collective-permute-done | bytes 65568 | tf_op jit(solution)/shard_map/ppermute | solution.py:375
  19.4 1.3 %collective-permute-done.2.refs_3_ = bf16[32,1024]{1,0:T(8,128)(2,1)S(1)} collective-permute-done((bf16[32,1024]{1,0:T(8,128)(2,1)S(1)}, bf16[32,1024]{1,0:T(8,128)(2,1)S(1)}, u32[]{:S(2)}, u32[]{:S(2)}) %collective-permute-start.2) | collective-permute-done | bytes 65568 | tf_op jit(solution)/shard_map/ppermute | solution.py:375
  20.7 2.0 %collective-permute-start.3 = (bf16[32,1024]{1,0:T(8,128)(2,1)S(1)}, bf16[32,1024]{1,0:T(8,128)(2,1)S(1)}, u32[]{:S(2)}, u32[]{:S(2)}) collective-permute-start(bf16[32,1024]{1,0:T(8,128)(2,1)S(1)} %get-tuple-element.32), channel_id=1, source_target_pairs={{0,4},{1,5},{2,6},{3,7},{4,0},{5,1},{6,2},{7,3},{8,12},{9,13},{10,... | collective-permute-start | bytes 196616 | tf_op jit(solution)/shard_map/ppermute | solution.py:375
  22.7 2.1 %collective-permute-start.4 = (bf16[32,1024]{1,0:T(8,128)(2,1)S(1)}, bf16[32,1024]{1,0:T(8,128)(2,1)S(1)}, u32[]{:S(2)}, u32[]{:S(2)}) collective-permute-start(bf16[32,1024]{1,0:T(8,128)(2,1)S(1)} %get-tuple-element.33), channel_id=1, source_target_pairs={{0,8},{1,9},{2,10},{3,11},{4,12},{5,13},{6,14},{7,15},{8,0},{9,1},... | collective-permute-start | bytes 196616 | tf_op jit(solution)/shard_map/ppermute | solution.py:375
  24.8 0.6 %collective-permute-start.5 = (bf16[32,1024]{1,0:T(8,128)(2,1)S(1)}, bf16[32,1024]{1,0:T(8,128)(2,1)S(1)}, u32[]{:S(2)}, u32[]{:S(2)}) collective-permute-start(bf16[32,1024]{1,0:T(8,128)(2,1)S(1)} %get-tuple-element.34), channel_id=1, source_target_pairs={{0,12},{1,13},{2,14},{3,15},{4,8},{5,9},{6,10},{7,11},{8,4},{9,5},... | collective-permute-start | bytes 196616 | tf_op jit(solution)/shard_map/ppermute | solution.py:375
  25.4 1.6 %fetch.1 = (bf16[256,4096]{1,0:T(8,128)(2,1)S(1)}, f32[1,256]{1,0:T(1,128)S(1)}, f32[1,512]{1,0:T(1,128)S(1)}) custom-call(bf16[256,4096]{1,0:T(8,128)(2,1)} %w4.3, f32[1,256]{1,0:T(1,128)} %bitcast.19, f32[1,512]{1,0:T(1,128)} %bitcast.18), custom_call_target="tpu_custom_call" | custom-call | flops 1073741824 | bytes 2097152 | tf_op jit(solution)/shard_map/fetch/pallas_call | solution.py:390
  27.0 0.0 collective-permute-done.3.refs_1_
  27.0 4.1 %collective-permute-done.4.refs_2_ = bf16[32,1024]{1,0:T(8,128)(2,1)S(1)} collective-permute-done((bf16[32,1024]{1,0:T(8,128)(2,1)S(1)}, bf16[32,1024]{1,0:T(8,128)(2,1)S(1)}, u32[]{:S(2)}, u32[]{:S(2)}) %collective-permute-start.4) | collective-permute-done | bytes 65568 | tf_op jit(solution)/shard_map/ppermute | solution.py:375
  31.1 0.0 collective-permute-done.5.refs_3_
  31.1 0.9 %place.1 = bf16[128,1024]{1,0:T(8,128)(2,1)} custom-call(bf16[896,128]{1,0:T(8,128)(2,1)S(1)} %get-tuple-element.20.places, bf16[32,1024]{1,0:T(8,128)(2,1)S(1)} %get-tuple-element.31.refs_0_, bf16[32,1024]{1,0:T(8,128)(2,1)S(1)} %collective-permute-done.3.refs_1_, bf16[32,1024]{1,0:T(8,128)(2,1)S(1)} %collective-permute-done.4.refs_2_, ...), custom_call_target="tpu_custom_call" | custom-call | flops 67108864 | bytes 1048576 | tf_op jit(solution)/shard_map/place/pallas_call | solution.py:427
  32.0 0.0 all-to-all-done
  32.0 5.6 %finish.1 = (bf16[8,256,256]{2,1,0:T(8,128)(2,1)}, bf16[4,128,512]{2,1,0:T(8,128)(2,1)}) custom-call(bf16[128,1280]{1,0:T(8,128)(2,1)S(1)} %bitcast.10, bf16[896,128]{1,0:T(8,128)(2,1)S(1)} %get-tuple-element.20.places, bf16[256,4096]{1,0:T(8,128)(2,1)S(1)} %get-tuple-element.21.w4, f32[1,256]{1,0:T(1,128)S(1)} %get-tuple-element.22.b4, ...), custom_call_target="tpu_custom_call" | custom-call | flops 4294967296 | bytes 4194304 | tf_op jit(solution)/shard_map/finish/pallas_call | solution.py:402
  (1 shorter events, 0.0 us)
Async XLA Ops:
  3.5 28.5 %all-to-all-start = ((bf16[16,8,1280]{2,1,0:T(8,128)(2,1)}), bf16[16,8,1280]{2,1,0:T(8,128)(2,1)S(1)}, u32[]{:S(2)}, u32[]{:S(2)}) async-start(bf16[16,8,1280]{2,1,0:T(8,128)(2,1)} %bitcast.11), calls=%async_computation | async-start | bytes 655360 | tf_op jit(solution)/shard_map/all_to_all | solution.py:355
  13.9 2.1 %collective-permute-start = (bf16[32,1024]{1,0:T(8,128)(2,1)S(1)}, bf16[32,1024]{1,0:T(8,128)(2,1)S(1)}, u32[]{:S(2)}, u32[]{:S(2)}) collective-permute-start(bf16[32,1024]{1,0:T(8,128)(2,1)S(1)} %get-tuple-element.28), channel_id=1, source_target_pairs={{0,1},{1,0},{2,3},{3,2},{4,5},{5,4},{6,7},{7,6},{8,9},{9,8},{10,11... | collective-permute-start | bytes 196616 | tf_op jit(solution)/shard_map/ppermute | solution.py:375
  14.4 5.0 %collective-permute-start.1 = (bf16[32,1024]{1,0:T(8,128)(2,1)S(1)}, bf16[32,1024]{1,0:T(8,128)(2,1)S(1)}, u32[]{:S(2)}, u32[]{:S(2)}) collective-permute-start(bf16[32,1024]{1,0:T(8,128)(2,1)S(1)} %get-tuple-element.29), channel_id=1, source_target_pairs={{0,2},{1,3},{2,0},{3,1},{4,6},{5,7},{6,4},{7,5},{8,10},{9,11},{10,... | collective-permute-start | bytes 196616 | tf_op jit(solution)/shard_map/ppermute | solution.py:375
  16.0 4.7 %collective-permute-start.2 = (bf16[32,1024]{1,0:T(8,128)(2,1)S(1)}, bf16[32,1024]{1,0:T(8,128)(2,1)S(1)}, u32[]{:S(2)}, u32[]{:S(2)}) collective-permute-start(bf16[32,1024]{1,0:T(8,128)(2,1)S(1)} %get-tuple-element.30), channel_id=1, source_target_pairs={{0,3},{1,2},{2,1},{3,0},{4,7},{5,6},{6,5},{7,4},{8,11},{9,10},{10,... | collective-permute-start | bytes 196616 | tf_op jit(solution)/shard_map/ppermute | solution.py:375
  20.7 6.3 %collective-permute-start.3 = (bf16[32,1024]{1,0:T(8,128)(2,1)S(1)}, bf16[32,1024]{1,0:T(8,128)(2,1)S(1)}, u32[]{:S(2)}, u32[]{:S(2)}) collective-permute-start(bf16[32,1024]{1,0:T(8,128)(2,1)S(1)} %get-tuple-element.32), channel_id=1, source_target_pairs={{0,4},{1,5},{2,6},{3,7},{4,0},{5,1},{6,2},{7,3},{8,12},{9,13},{10,... | collective-permute-start | bytes 196616 | tf_op jit(solution)/shard_map/ppermute | solution.py:375
  22.7 8.4 %collective-permute-start.4 = (bf16[32,1024]{1,0:T(8,128)(2,1)S(1)}, bf16[32,1024]{1,0:T(8,128)(2,1)S(1)}, u32[]{:S(2)}, u32[]{:S(2)}) collective-permute-start(bf16[32,1024]{1,0:T(8,128)(2,1)S(1)} %get-tuple-element.33), channel_id=1, source_target_pairs={{0,8},{1,9},{2,10},{3,11},{4,12},{5,13},{6,14},{7,15},{8,0},{9,1},... | collective-permute-start | bytes 196616 | tf_op jit(solution)/shard_map/ppermute | solution.py:375
  24.8 6.3 %collective-permute-start.5 = (bf16[32,1024]{1,0:T(8,128)(2,1)S(1)}, bf16[32,1024]{1,0:T(8,128)(2,1)S(1)}, u32[]{:S(2)}, u32[]{:S(2)}) collective-permute-start(bf16[32,1024]{1,0:T(8,128)(2,1)S(1)} %get-tuple-element.34), channel_id=1, source_target_pairs={{0,12},{1,13},{2,14},{3,15},{4,8},{5,9},{6,10},{7,11},{8,4},{9,5},... | collective-permute-start | bytes 196616 | tf_op jit(solution)/shard_map/ppermute | solution.py:375

commit v4 on v2

--- a/solution.py
+++ b/solution.py
@@ -7,6 +7,7 @@
 from jax.experimental.pallas import tpu as pltpu
 from jax.sharding import PartitionSpec as P
 
+
 GRID_W = 64
 CHUNK = 256
 F32 = jnp.float32
@@ -36,7 +37,11 @@
     return jnp.sum(jnp.where(same, jnp.broadcast_to(row, (size, size)), 0.0), axis=1, keepdims=True)
 
 
-def landing(table, block, tok_dev, per_peer):
+def low_part(shards):
+    return 1 << ((shards.bit_length()) // 2)
+
+
+def landing(table, block, tok_dev, per_peer, flip=0):
     shards = table.shape[0]
     start = block * tok_dev
     inside = jnp.logical_and(table >= start, table < start + tok_dev)
@@ -49,29 +54,36 @@
         hit = jnp.logical_and(inside, rank == float(k))
         found = jnp.sum(jnp.where(hit, place, 0.0), axis=1, keepdims=True)
         spread = spread + jnp.where(lax.rem(lane, per_peer) == k, found, 0.0)
-    own = lax.div(lane, per_peer) == iota((shards, tok_dev), 0)
+    own = lax.div(lane, per_peer) == jnp.bitwise_xor(iota((shards, tok_dev), 0), flip)
     return jnp.sum(jnp.where(own, spread, 0.0), axis=0, keepdims=True).astype(jnp.int32)
 
 
-def project_kernel(
-    hidden, table_hbm, w4, b4, w2, b2, ws, bs, send, places_v,
-    hidden_v, table_v, w4_v, w2_v, ws_v, b4_v, b2_v, bs_v, send_v, sems, out_sems,
-):
-    chunks = ws.shape[1] // CHUNK
-    pairs = [
-        (table_hbm, table_v),
-        (hidden.at[0], hidden_v.at[0]),
-        (b4, b4_v),
-        (w4, w4_v),
-        (hidden.at[1], hidden_v.at[1]),
-        (b2, b2_v),
-        (w2, w2_v),
-        (hidden.at[2], hidden_v.at[2]),
-        (bs, bs_v),
-    ] + [(ws.at[:, pl.ds(i * CHUNK, CHUNK)], ws_v.at[i]) for i in range(chunks)]
+def start_all(pairs, sems):
     copies = [pltpu.make_async_copy(src, dst, sems.at[i]) for i, (src, dst) in enumerate(pairs)]
     for copy in copies:
         copy.start()
+    return copies
+
+
+def project_kernel(low, hidden, table_hbm, w4, b4, w2, b2, ws, bs, send, places_v, *refs):
+    sent = refs[:low]
+    hidden_v, table_v, w4_v, w2_v, ws_v, b4_v, b2_v, bs_v, send_v, sems, out_sem = refs[low:]
+    chunks = ws.shape[1] // CHUNK
+    copies = start_all(
+        [
+            (table_hbm, table_v),
+            (hidden.at[0], hidden_v.at[0]),
+            (b4, b4_v),
+            (w4, w4_v),
+            (hidden.at[1], hidden_v.at[1]),
+            (b2, b2_v),
+            (w2, w2_v),
+            (hidden.at[2], hidden_v.at[2]),
+            (bs, bs_v),
+        ]
+        + [(ws.at[:, pl.ds(i * CHUNK, CHUNK)], ws_v.at[i]) for i in range(chunks)],
+        sems,
+    )
     shards, tok_dev = table_v.shape
     per_peer = tok_dev // shards
     me = lax.axis_index("rows")
@@ -87,6 +99,10 @@
     order = one_hot(iota(square, 0) == slot)
     order_above = one_hot(iota(square, 0) == slot + per_peer)
     order_below = one_hot(iota(square, 0) == slot - per_peer)
+
+    apart = jnp.bitwise_xor(block_row, me)
+    turn = lax.rem(apart, low) * (shards // low) + lax.div(apart, low)
+    order_turn = one_hot(iota(square, 0) == turn * per_peer + within)
 
     own = landing(table, me, tok_dev, per_peer)
     above = landing(table, me - 1, tok_dev, per_peer)
@@ -108,6 +124,8 @@
         )
         base += 3 * GRID_W
 
+    places_v[base : base + tok_dev] = one_hot(cell == landing(table, me, tok_dev, per_peer, me))
+
     for copy in copies[1:4]:
         copy.wait()
     c4 = w4_v.shape[1]
@@ -115,61 +133,52 @@
     send_v[:, 0:c4] = matmul(order, four).astype(BF16)
     send_v[:, c4 : 2 * c4] = matmul(order_above, four).astype(BF16)
     send_v[:, 2 * c4 : 3 * c4] = matmul(order_below, four).astype(BF16)
+    store = pltpu.make_async_copy(send_v, send, out_sem)
+    store.start()
+    c2 = w2_v.shape[1]
     for copy in copies[4:7]:
         copy.wait()
-    c2 = w2_v.shape[1]
-    two = (matmul(hidden_v[1], w2_v[...]) + b2_v[...]).astype(BF16)
-    send_v[:, 3 * c4 : 3 * c4 + c2] = matmul(order, two).astype(BF16)
-    done = 3 * c4 + c2
-    outs = [(0, done)] + [(done + i * CHUNK, CHUNK) for i in range(chunks)]
-    stores = [
-        pltpu.make_async_copy(send_v.at[:, pl.ds(at, size)], send.at[:, pl.ds(at, size)], out_sems.at[i])
-        for i, (at, size) in enumerate(outs)
-    ]
-    stores[0].start()
+    hand_out(order_turn, matmul(hidden_v[1], w2_v[...]) + b2_v[...], sent, 0)
     for copy in copies[7:9]:
         copy.wait()
     for i in range(chunks):
         copies[9 + i].wait()
-        same = (matmul(hidden_v[2], ws_v[i]) + bs_v[:, i * CHUNK : (i + 1) * CHUNK]).astype(BF16)
-        send_v[:, done + i * CHUNK : done + (i + 1) * CHUNK] = matmul(order, same).astype(BF16)
-        stores[1 + i].start()
-    for store in stores:
-        store.wait()
+        same = matmul(hidden_v[2], ws_v[i]) + bs_v[:, i * CHUNK : (i + 1) * CHUNK]
+        hand_out(order_turn, same, sent, c2 + i * CHUNK)
+    store.wait()
+
+
+def hand_out(order, projected, sent, at):
+    moved = matmul(order, projected.astype(BF16)).astype(BF16)
+    rows = sent[0].shape[0]
+    for k, out in enumerate(sent):
+        out[:, at : at + moved.shape[1]] = moved[k * rows : (k + 1) * rows]
+
+
+def turn_kernel(low_count, *refs):
+    lows, highs = refs[:low_count], refs[low_count:]
+    rows = lows[0].shape[0] // len(highs)
+    for h, high in enumerate(highs):
+        for k, low in enumerate(lows):
+            high[k * rows : (k + 1) * rows] = low[h * rows : (h + 1) * rows]
 
 
 def fetch_kernel(w4, b4, b2, w4_v, b4_v, b2_v, sems):
-    pairs = ((w4, w4_v), (b4, b4_v), (b2, b2_v))
-    copies = [pltpu.make_async_copy(src, dst, sems.at[i]) for i, (src, dst) in enumerate(pairs)]
-    for copy in copies:
-        copy.start()
-    for copy in copies:
+    for copy in start_all([(w4, w4_v), (b4, b4_v), (b2, b2_v)], sems):
         copy.wait()
 
 
-def finish_kernel(
-    arrived, places, w4, b4, b2, wj_hbm, w2_hbm, joined, up_two, same,
-    wj, w2, tiles_v, wide_v, acc_v, out_v, acc_two_v, two_v, same_v, weight_sems, sems, rest_sems,
+def join_kernel(
+    arrived, places, w4, b4, wj_hbm, w2_hbm, joined, w2,
+    wj, tiles_v, wide_v, acc_v, out_v, weight_sems, sems,
 ):
-    weights = [
-        pltpu.make_async_copy(src, dst, weight_sems.at[i]) for i, (src, dst) in enumerate(((wj_hbm, wj), (w2_hbm, w2)))
-    ]
-    for copy in weights:
-        copy.start()
-    tok_dev, c4 = arrived.shape[0], w4.shape[0]
-    c2 = w2.shape[0]
-    row_count = tok_dev // GRID_W
-    place = places[0:tok_dev]
-    same_v[...] = matmul(place, arrived[:, 3 * c4 + c2 :]).astype(BF16)
-    stores = [pltpu.make_async_copy(same_v, same, rest_sems.at[0])]
-    stores[0].start()
+    weights = start_all([(wj_hbm, wj), (w2_hbm, w2)], weight_sems)
     widen(arrived, places, w4, b4, tiles_v, wide_v)
     weights[0].wait()
-    for chunk in range(row_count):
-        stores.append(convolve(chunk, wide_v, wj, joined, acc_v, out_v, sems))
-        if chunk == 0:
-            weights[1].wait()
-            stores += expand_two(arrived, place, w2, b2, 3 * c4, up_two, acc_two_v, two_v, rest_sems)
+    stores = [
+        convolve(chunk, wide_v, wj, joined, acc_v, out_v, sems) for chunk in range(arrived.shape[0] // GRID_W)
+    ]
+    weights[1].wait()
     for store in stores:
         store.wait()
 
@@ -240,12 +249,20 @@
     return store
 
 
-def expand_two(arrived, place, w2, b2, at, up_two, acc_v, out_v, sems):
+def rest_kernel(places, w2, b2, *refs):
+    arrived, (up_two, same, rows_v, acc_v, out_v, same_v, sems, same_sem) = refs[:-8], refs[-8:]
+    rows = arrived[0].shape[0]
+    for h, piece in enumerate(arrived):
+        rows_v[h * rows : (h + 1) * rows] = piece[...]
+    tok_dev = rows_v.shape[0]
     c2 = w2.shape[0]
-    row_count = arrived.shape[0] // GRID_W
-    tile = matmul(place, arrived[:, at : at + c2]).astype(BF16)
+    row_count = tok_dev // GRID_W
+    place = places[places.shape[0] - tok_dev :]
+    same_v[...] = matmul(place, rows_v[:, c2:]).astype(BF16)
+    stores = [pltpu.make_async_copy(same_v, same, same_sem)]
+    stores[0].start()
+    tile = matmul(place, rows_v[:, 0:c2]).astype(BF16)
     bias = b2[...]
-    stores = []
     for a in range(2):
         for b in range(2):
             part = matmul(tile, w2[:, (a * 2 + b) * c2 : (a * 2 + b + 1) * c2]) + bias
@@ -258,10 +275,11 @@
             r = 2 * i + a
             for block in range(c2 // 128):
                 out_v[r, :, block * 128 : (block + 1) * 128] = acc_v[r, block].astype(BF16)
-            store = pltpu.make_async_copy(out_v.at[r], up_two.at[r], sems.at[1 + r])
+            store = pltpu.make_async_copy(out_v.at[r], up_two.at[r], sems.at[r])
             store.start()
             stores.append(store)
-    return stores
+    for store in stores:
+        store.wait()
 
 
 def body(
@@ -279,17 +297,18 @@
     up2_bias,
     join_weight,
 ):
-    hooks, tok_dev, hid = hidden_states.shape
+    _, tok_dev, hid = hidden_states.shape
     shards = lax.axis_size("rows")
     per_peer = tok_dev // shards
     row_count = tok_dev // GRID_W
     c4, c2, cs = proj_four_weight.shape[1], proj_two_weight.shape[1], proj_same_weight.shape[1]
     feat = join_weight.shape[3]
     table = cell_of.reshape(shards, tok_dev)
-    place_rows = 3 * tok_dev + 6 * GRID_W
+    place_rows = 4 * tok_dev + 6 * GRID_W
     shape = jax.ShapeDtypeStruct
 
-    total = 3 * c4 + c2 + cs
+    low = low_part(shards)
+    high = shards // low
     biases = [bias.reshape(1, -1) for bias in (proj_four_bias, proj_two_bias, proj_same_bias)]
     inputs = (
         hidden_states,
@@ -301,11 +320,12 @@
         proj_same_weight,
         biases[2],
     )
-    send, places = pl.pallas_call(
-        project_kernel,
-        out_shape=(pltpu.HBM((tok_dev, total), BF16), pltpu.VMEM((place_rows, tok_dev), BF16)),
+    send, places, *sent = pl.pallas_call(
+        functools.partial(project_kernel, low),
+        out_shape=(pltpu.HBM((tok_dev, 3 * c4), BF16), pltpu.VMEM((place_rows, tok_dev), BF16))
+        + (pltpu.VMEM((high * per_peer, c2 + cs), BF16),) * low,
         in_specs=[ANY] * 8,
-        out_specs=(ANY, VMEM),
+        out_specs=(ANY,) + (VMEM,) * (1 + low),
         scratch_shapes=[
             pltpu.VMEM(hidden_states.shape, BF16),
             pltpu.VMEM(table.shape, jnp.int32),
@@ -315,17 +335,32 @@
             pltpu.VMEM((1, c4), F32),
             pltpu.VMEM((1, c2), F32),
             pltpu.VMEM((1, cs), F32),
-            pltpu.VMEM((tok_dev, total), BF16),
+            pltpu.VMEM((tok_dev, 3 * c4), BF16),
             pltpu.SemaphoreType.DMA((9 + cs // CHUNK,)),
-            pltpu.SemaphoreType.DMA((1 + cs // CHUNK,)),
+            pltpu.SemaphoreType.DMA,
         ],
-        compiler_params=pltpu.CompilerParams(vmem_limit_bytes=12 << 20),
+        compiler_params=pltpu.CompilerParams(vmem_limit_bytes=10 << 20),
         cost_estimate=pl.CostEstimate(flops=2 * tok_dev * hid * (c4 + c2 + cs), bytes_accessed=5 << 20, transcendentals=0),
         name="project",
     )(*(in_hbm(x) for x in inputs))
+
+    def swap(piece, step):
+        return lax.ppermute(piece, "rows", [(i, i ^ step) for i in range(shards)])
+
+    crossed = [sent[0]] + [swap(sent[k], k) for k in range(1, low)]
     arrived = lax.all_to_all(
-        send.reshape(shards, per_peer, total), "rows", split_axis=0, concat_axis=0, tiled=True
-    ).reshape(tok_dev, total)
+        send.reshape(shards, per_peer, 3 * c4), "rows", split_axis=0, concat_axis=0, tiled=True
+    ).reshape(tok_dev, 3 * c4)
+    turned = pl.pallas_call(
+        functools.partial(turn_kernel, low),
+        out_shape=(shape((low * per_peer, c2 + cs), BF16),) * high,
+        in_specs=[VMEM] * low,
+        out_specs=(VMEM,) * high,
+        compiler_params=pltpu.CompilerParams(vmem_limit_bytes=4 << 20),
+        cost_estimate=pl.CostEstimate(flops=1 << 26, bytes_accessed=1 << 20, transcendentals=0),
+        name="turn",
+    )(*crossed)
+    landed = [turned[0]] + [swap(turned[h], h * low) for h in range(1, high)]
 
     weights = (up4_weight, up4_bias.reshape(1, -1), up2_bias.reshape(1, -1))
     w4, b4, b2 = pl.pallas_call(
@@ -335,38 +370,49 @@
         out_specs=(VMEM,) * 3,
         scratch_shapes=[pltpu.SemaphoreType.DMA((3,))],
         cost_estimate=pl.CostEstimate(flops=1 << 30, bytes_accessed=2 << 20, transcendentals=0),
+        compiler_params=pltpu.CompilerParams(vmem_limit_bytes=4 << 20),
         name="fetch",
-        compiler_params=pltpu.CompilerParams(vmem_limit_bytes=4 << 20),
     )(*(in_hbm(w) for w in weights))
 
     out_rows = 4 * row_count
-    joined, upsampled_two, same_scale = pl.pallas_call(
-        finish_kernel,
+    joined, w2 = pl.pallas_call(
+        join_kernel,
         out_shape=(
             shape((out_rows, 4 * GRID_W, feat), BF16),
-            shape((2 * row_count, 2 * GRID_W, c2), BF16),
-            shape((tok_dev, cs), BF16),
+            pltpu.VMEM(up2_weight.shape, BF16),
         ),
-        in_specs=[VMEM] * 5 + [ANY] * 2,
-        out_specs=(ANY, ANY, ANY),
+        in_specs=[VMEM] * 4 + [ANY] * 2,
+        out_specs=(ANY, VMEM),
         scratch_shapes=[
             pltpu.VMEM((3, 3 * c4, feat), BF16),
-            pltpu.VMEM(up2_weight.shape, BF16),
             pltpu.VMEM((place_rows, c4), BF16),
             pltpu.VMEM(((out_rows + 2) * GRID_W, 6 * c4), BF16),
             pltpu.VMEM((out_rows, feat // 128, 4 * GRID_W, 128), F32),
             pltpu.VMEM((out_rows, 4 * GRID_W, feat), BF16),
+            pltpu.SemaphoreType.DMA((2,)),
+            pltpu.SemaphoreType.DMA((row_count,)),
+        ],
+        compiler_params=pltpu.CompilerParams(vmem_limit_bytes=20 << 20),
+        cost_estimate=pl.CostEstimate(flops=4 << 30, bytes_accessed=4 << 20, transcendentals=0),
+        name="join",
+    )(arrived, places, w4, b4, in_hbm(join_weight.reshape(3, 3 * c4, feat)), in_hbm(up2_weight))
+    upsampled_two, same_scale = pl.pallas_call(
+        rest_kernel,
+        out_shape=(shape((2 * row_count, 2 * GRID_W, c2), BF16), shape((tok_dev, cs), BF16)),
+        in_specs=[VMEM] * (3 + high),
+        out_specs=(ANY, ANY),
+        scratch_shapes=[
+            pltpu.VMEM((tok_dev, c2 + cs), BF16),
             pltpu.VMEM((2 * row_count, c2 // 128, 2 * GRID_W, 128), F32),
             pltpu.VMEM((2 * row_count, 2 * GRID_W, c2), BF16),
             pltpu.VMEM((tok_dev, cs), BF16),
-            pltpu.SemaphoreType.DMA((2,)),
-            pltpu.SemaphoreType.DMA((row_count,)),
-            pltpu.SemaphoreType.DMA((1 + 2 * row_count,)),
+            pltpu.SemaphoreType.DMA((2 * row_count,)),
+            pltpu.SemaphoreType.DMA,
         ],
-        compiler_params=pltpu.CompilerParams(vmem_limit_bytes=24 << 20),
-        cost_estimate=pl.CostEstimate(flops=4 << 30, bytes_accessed=4 << 20, transcendentals=0),
-        name="finish",
-    )(arrived, places, w4, b4, b2, in_hbm(join_weight.reshape(3, 3 * c4, feat)), in_hbm(up2_weight))
+        compiler_params=pltpu.CompilerParams(vmem_limit_bytes=8 << 20),
+        cost_estimate=pl.CostEstimate(flops=1 << 30, bytes_accessed=4 << 20, transcendentals=0),
+        name="rest",
+    )(places, w2, b2, *landed)
     return (joined, upsampled_two, same_scale.reshape(row_count, GRID_W, cs))
 
 

time: 34.2 us -> 35.4 us (1.035)
  starting transfers between devices: 7.43 us -> 14 us
  waiting for transfers between devices: 13.7 us -> 8.41 us
    all_to_all x1, waiting for transfers between devices: 13.7 us -> 0.01 us  [body(): lax.all_to_all(send.reshape(shards, per_peer, 3 * c4), 'rows', split_axis...]
    ppermute x0 -> x6, waiting for transfers between devices: none -> 8.41 us  [swap(): return lax.ppermute(piece, 'rows', [(i, i ^ step) for i in range(shards)])]
    ppermute x0 -> x6, starting transfers between devices: none -> 6.56 us  [swap(): return lax.ppermute(piece, 'rows', [(i, i ^ step) for i in range(shards)])]
    pallas_call x2 -> x4, Pallas kernels: 10.5 us -> 10.4 us  [the longest x1 4.86 us: body(): pl.pallas_call(join_kernel, out_shape=(shape((out_rows, 4 * GRID_W, feat)...]
  transfers between devices with their start and end apart: 1 -> 7, of which waited for: 1 -> 3; matrix products, arithmetic and copies ran while one was open for 0% -> 0% of each run, Pallas kernels for 5% -> 19%
where the time goes in v4:
time: 35.4 us; the launch traced here: 35.1 us
  starting transfers between devices  14 us (40%)
  Pallas kernels  12 us (34%)
  waiting for transfers between devices  8.41 us (24%)
  between operations  0.69 us (2%)
    ppermute x6, waiting for transfers between devices, swap(): return lax.ppermute(piece, 'rows', [(i, i ^ step) for i in range(shards)])  8.41 us
    all_to_all x1, starting transfers between devices, body(): lax.all_to_all(send.reshape(shards, per_peer, 3 * c4), 'rows', split_axis...  7.43 us
    ppermute x6, starting transfers between devices, swap(): return lax.ppermute(piece, 'rows', [(i, i ^ step) for i in range(shards)])  6.56 us
    pallas_call x1, Pallas kernels, body(): pl.pallas_call(join_kernel, out_shape=(shape((out_rows, 4 * GRID_W, feat)...  4.86 us
    pallas_call x1, Pallas kernels, body(): pl.pallas_call(functools.partial(project_kernel, low), out_shape=(pltpu.H...  4.04 us
    pallas_call x1, Pallas kernels, body(): pl.pallas_call(fetch_kernel, out_shape=tuple((pltpu.VMEM(w.shape, w.dtype...  1.62 us
    pallas_call x1, Pallas kernels, body(): pl.pallas_call(rest_kernel, out_shape=(shape((2 * row_count, 2 * GRID_W,...  1.43 us
  transfers between devices with their start and end apart: 7, of which 3 were waited for; matrix products, arithmetic and copies ran while one was open for 0% of the time, Pallas kernels for 19%

profile of v4, /device:TPU:0, one launch (start us, length us, event | category | flops | bytes accessed | tf_op | source)
XLA Modules:
  0.0 35.1 jit_solution(16062862998106397133)
XLA Ops:
  0.6 4.0 %project.1 = (bf16[128,768]{1,0:T(8,128)(2,1)}, bf16[896,128]{1,0:T(8,128)(2,1)S(1)}, bf16[32,1536]{1,0:T(8,128)(2,1)S(1)}, bf16[32,1536]{1,0:T(8,128)(2,1)S(1)}...) custom-call(bf16[3,128,1024]{2,1,0:T(8,128)(2,1)} %hidden.1, s32[16,128]{1,0:T(8,128)} %bitcast.12, ...), custom_call_target="tpu_custom_call" | custom-call | flops 469762048 | bytes 5242880 | tf_op jit(solution)/shard_map/project/pallas_call | solution.py:323
  4.7 7.4 %all-to-all-start = ((bf16[16,8,768]{2,1,0:T(8,128)(2,1)}), bf16[16,8,768]{2,1,0:T(8,128)(2,1)S(1)}, u32[]{:S(2)}, u32[]{:S(2)}) async-start(bf16[16,8,768]{2,1,0:T(8,128)(2,1)} %bitcast.11), calls=%async_computation | async-start | bytes 393216 | tf_op jit(solution)/shard_map/all_to_all | solution.py:351
  12.1 0.4 %collective-permute-start = (bf16[32,1536]{1,0:T(8,128)(2,1)S(1)}, bf16[32,1536]{1,0:T(8,128)(2,1)S(1)}, u32[]{:S(2)}, u32[]{:S(2)}) collective-permute-start(bf16[32,1536]{1,0:T(8,128)(2,1)S(1)} %get-tuple-element.28), channel_id=1, source_target_pairs={{0,1},{1,0},{2,3},{3,2},{4,5},{5,4},{6,7},{7,6},{8,9},{9,8},{10,11... | collective-permute-start | bytes 294920 | tf_op jit(solution)/shard_map/ppermute | solution.py:348
  12.5 1.6 %collective-permute-start.1 = (bf16[32,1536]{1,0:T(8,128)(2,1)S(1)}, bf16[32,1536]{1,0:T(8,128)(2,1)S(1)}, u32[]{:S(2)}, u32[]{:S(2)}) collective-permute-start(bf16[32,1536]{1,0:T(8,128)(2,1)S(1)} %get-tuple-element.29), channel_id=1, source_target_pairs={{0,2},{1,3},{2,0},{3,1},{4,6},{5,7},{6,4},{7,5},{8,10},{9,11},{10,... | collective-permute-start | bytes 294920 | tf_op jit(solution)/shard_map/ppermute | solution.py:348
  14.2 0.0 collective-permute-start.2
  14.2 1.6 %fetch.1 = (bf16[256,4096]{1,0:T(8,128)(2,1)S(1)}, f32[1,256]{1,0:T(1,128)S(1)}, f32[1,512]{1,0:T(1,128)S(1)}) custom-call(bf16[256,4096]{1,0:T(8,128)(2,1)} %w4.3, f32[1,256]{1,0:T(1,128)} %bitcast.18, f32[1,512]{1,0:T(1,128)} %bitcast.17), custom_call_target="tpu_custom_call" | custom-call | flops 1073741824 | bytes 2097152 | tf_op jit(solution)/shard_map/fetch/pallas_call | solution.py:366
  15.8 0.0 collective-permute-done.refs_1_
  15.8 3.7 %collective-permute-done.1.refs_2_ = bf16[32,1536]{1,0:T(8,128)(2,1)S(1)} collective-permute-done((bf16[32,1536]{1,0:T(8,128)(2,1)S(1)}, bf16[32,1536]{1,0:T(8,128)(2,1)S(1)}, u32[]{:S(2)}, u32[]{:S(2)}) %collective-permute-start.1) | collective-permute-done | bytes 98336 | tf_op jit(solution)/shard_map/ppermute | solution.py:348
  19.5 1.4 %collective-permute-done.2.refs_3_ = bf16[32,1536]{1,0:T(8,128)(2,1)S(1)} collective-permute-done((bf16[32,1536]{1,0:T(8,128)(2,1)S(1)}, bf16[32,1536]{1,0:T(8,128)(2,1)S(1)}, u32[]{:S(2)}, u32[]{:S(2)}) %collective-permute-start.2) | collective-permute-done | bytes 98336 | tf_op jit(solution)/shard_map/ppermute | solution.py:348
  20.9 2.1 %collective-permute-start.3 = (bf16[32,1536]{1,0:T(8,128)(2,1)S(1)}, bf16[32,1536]{1,0:T(8,128)(2,1)S(1)}, u32[]{:S(2)}, u32[]{:S(2)}) collective-permute-start(bf16[32,1536]{1,0:T(8,128)(2,1)S(1)} %get-tuple-element.32), channel_id=1, source_target_pairs={{0,4},{1,5},{2,6},{3,7},{4,0},{5,1},{6,2},{7,3},{8,12},{9,13},{10,... | collective-permute-start | bytes 294920 | tf_op jit(solution)/shard_map/ppermute | solution.py:348
  22.9 2.3 %collective-permute-start.4 = (bf16[32,1536]{1,0:T(8,128)(2,1)S(1)}, bf16[32,1536]{1,0:T(8,128)(2,1)S(1)}, u32[]{:S(2)}, u32[]{:S(2)}) collective-permute-start(bf16[32,1536]{1,0:T(8,128)(2,1)S(1)} %get-tuple-element.33), channel_id=1, source_target_pairs={{0,8},{1,9},{2,10},{3,11},{4,12},{5,13},{6,14},{7,15},{8,0},{9,1},... | collective-permute-start | bytes 294920 | tf_op jit(solution)/shard_map/ppermute | solution.py:348
  25.2 0.2 collective-permute-start.5
  25.4 0.0 all-to-all-done
  25.4 4.9 %join.1 = (bf16[8,256,256]{2,1,0:T(8,128)(2,1)}, bf16[512,2048]{1,0:T(8,128)(2,1)S(1)}) custom-call(bf16[128,768]{1,0:T(8,128)(2,1)S(1)} %bitcast.10, bf16[896,128]{1,0:T(8,128)(2,1)S(1)} %get-tuple-element.21.places, bf16[256,4096]{1,0:T(8,128)(2,1)S(1)} %get-tuple-element.22.w4, f32[1,256]{1,0:T(1,128)S(1)} %get-tuple-element.23.b4, ...), custom_call_target="tpu_custom_call" | custom-call | flops 4294967296 | bytes 4194304 | tf_op jit(solution)/shard_map/join/pallas_call | solution.py:378
  30.2 0.0 collective-permute-done.3.refs_1_
  30.3 3.4 %collective-permute-done.4.refs_2_ = bf16[32,1536]{1,0:T(8,128)(2,1)S(1)} collective-permute-done((bf16[32,1536]{1,0:T(8,128)(2,1)S(1)}, bf16[32,1536]{1,0:T(8,128)(2,1)S(1)}, u32[]{:S(2)}, u32[]{:S(2)}) %collective-permute-start.4) | collective-permute-done | bytes 98336 | tf_op jit(solution)/shard_map/ppermute | solution.py:348
  33.6 0.0 collective-permute-done.5.refs_3_
  33.6 1.4 %rest.1 = (bf16[4,128,512]{2,1,0:T(8,128)(2,1)}, bf16[128,1024]{1,0:T(8,128)(2,1)}) custom-call(bf16[896,128]{1,0:T(8,128)(2,1)S(1)} %get-tuple-element.21.places, bf16[512,2048]{1,0:T(8,128)(2,1)S(1)} %get-tuple-element.25.w2, f32[1,512]{1,0:T(1,128)S(1)} %get-tuple-element.26.b2, bf16[32,1536]{1,0:T(8,128)(2,1)S(1)} %get-tuple-element.31.refs_0_, ...), custom_call_target="tpu_custom_call" | custom-call | flops 1073741824 | bytes 4194304 | tf_op jit(solution)/shard_map/rest/pallas_call | solution.py:399
  (1 shorter events, 0.0 us)
Async XLA Ops:
  4.7 20.7 %all-to-all-start = ((bf16[16,8,768]{2,1,0:T(8,128)(2,1)}), bf16[16,8,768]{2,1,0:T(8,128)(2,1)S(1)}, u32[]{:S(2)}, u32[]{:S(2)}) async-start(bf16[16,8,768]{2,1,0:T(8,128)(2,1)} %bitcast.11), calls=%async_computation | async-start | bytes 393216 | tf_op jit(solution)/shard_map/all_to_all | solution.py:351
  12.1 3.7 %collective-permute-start = (bf16[32,1536]{1,0:T(8,128)(2,1)S(1)}, bf16[32,1536]{1,0:T(8,128)(2,1)S(1)}, u32[]{:S(2)}, u32[]{:S(2)}) collective-permute-start(bf16[32,1536]{1,0:T(8,128)(2,1)S(1)} %get-tuple-element.28), channel_id=1, source_target_pairs={{0,1},{1,0},{2,3},{3,2},{4,5},{5,4},{6,7},{7,6},{8,9},{9,8},{10,11... | collective-permute-start | bytes 294920 | tf_op jit(solution)/shard_map/ppermute | solution.py:348
  12.5 6.9 %collective-permute-start.1 = (bf16[32,1536]{1,0:T(8,128)(2,1)S(1)}, bf16[32,1536]{1,0:T(8,128)(2,1)S(1)}, u32[]{:S(2)}, u32[]{:S(2)}) collective-permute-start(bf16[32,1536]{1,0:T(8,128)(2,1)S(1)} %get-tuple-element.29), channel_id=1, source_target_pairs={{0,2},{1,3},{2,0},{3,1},{4,6},{5,7},{6,4},{7,5},{8,10},{9,11},{10,... | collective-permute-start | bytes 294920 | tf_op jit(solution)/shard_map/ppermute | solution.py:348
  14.2 6.7 %collective-permute-start.2 = (bf16[32,1536]{1,0:T(8,128)(2,1)S(1)}, bf16[32,1536]{1,0:T(8,128)(2,1)S(1)}, u32[]{:S(2)}, u32[]{:S(2)}) collective-permute-start(bf16[32,1536]{1,0:T(8,128)(2,1)S(1)} %get-tuple-element.30), channel_id=1, source_target_pairs={{0,3},{1,2},{2,1},{3,0},{4,7},{5,6},{6,5},{7,4},{8,11},{9,10},{10,... | collective-permute-start | bytes 294920 | tf_op jit(solution)/shard_map/ppermute | solution.py:348
  20.9 9.4 %collective-permute-start.3 = (bf16[32,1536]{1,0:T(8,128)(2,1)S(1)}, bf16[32,1536]{1,0:T(8,128)(2,1)S(1)}, u32[]{:S(2)}, u32[]{:S(2)}) collective-permute-start(bf16[32,1536]{1,0:T(8,128)(2,1)S(1)} %get-tuple-element.32), channel_id=1, source_target_pairs={{0,4},{1,5},{2,6},{3,7},{4,0},{5,1},{6,2},{7,3},{8,12},{9,13},{10,... | collective-permute-start | bytes 294920 | tf_op jit(solution)/shard_map/ppermute | solution.py:348
  22.9 10.7 %collective-permute-start.4 = (bf16[32,1536]{1,0:T(8,128)(2,1)S(1)}, bf16[32,1536]{1,0:T(8,128)(2,1)S(1)}, u32[]{:S(2)}, u32[]{:S(2)}) collective-permute-start(bf16[32,1536]{1,0:T(8,128)(2,1)S(1)} %get-tuple-element.33), channel_id=1, source_target_pairs={{0,8},{1,9},{2,10},{3,11},{4,12},{5,13},{6,14},{7,15},{8,0},{9,1},... | collective-permute-start | bytes 294920 | tf_op jit(solution)/shard_map/ppermute | solution.py:348
  25.2 8.4 %collective-permute-start.5 = (bf16[32,1536]{1,0:T(8,128)(2,1)S(1)}, bf16[32,1536]{1,0:T(8,128)(2,1)S(1)}, u32[]{:S(2)}, u32[]{:S(2)}) collective-permute-start(bf16[32,1536]{1,0:T(8,128)(2,1)S(1)} %get-tuple-element.34), channel_id=1, source_target_pairs={{0,12},{1,13},{2,14},{3,15},{4,8},{5,9},{6,10},{7,11},{8,4},{9,5},... | collective-permute-start | bytes 294920 | tf_op jit(solution)/shard_map/ppermute | solution.py:348

commit v5 on v4

--- a/solution.py
+++ b/solution.py
@@ -9,7 +9,7 @@
 
 
 GRID_W = 64
-CHUNK = 256
+CHUNK = 512
 F32 = jnp.float32
 BF16 = jnp.bfloat16
 ANY = pl.BlockSpec(memory_space=pl.ANY)
@@ -97,8 +97,6 @@
     within = jnp.sum(jnp.where(earlier, 1.0, 0.0), axis=0, keepdims=True).astype(jnp.int32)
     slot = block_row * per_peer + within
     order = one_hot(iota(square, 0) == slot)
-    order_above = one_hot(iota(square, 0) == slot + per_peer)
-    order_below = one_hot(iota(square, 0) == slot - per_peer)
 
     apart = jnp.bitwise_xor(block_row, me)
     turn = lax.rem(apart, low) * (shards // low) + lax.div(apart, low)
@@ -126,30 +124,37 @@
 
     places_v[base : base + tok_dev] = one_hot(cell == landing(table, me, tok_dev, per_peer, me))
 
-    for copy in copies[1:4]:
-        copy.wait()
-    c4 = w4_v.shape[1]
-    four = (matmul(hidden_v[0], w4_v[...]) + b4_v[...]).astype(BF16)
-    send_v[:, 0:c4] = matmul(order, four).astype(BF16)
-    send_v[:, c4 : 2 * c4] = matmul(order_above, four).astype(BF16)
-    send_v[:, 2 * c4 : 3 * c4] = matmul(order_below, four).astype(BF16)
+    c4, c2 = w4_v.shape[1], w2_v.shape[1]
+    copies[1].wait()
+    rows_four = matmul(order, hidden_v[0]).astype(BF16)
+    copies[2].wait()
+    copies[3].wait()
+    four = (matmul(rows_four, w4_v[...]) + b4_v[...]).astype(BF16)
+    blank = jnp.zeros((per_peer, c4), BF16)
+    send_v[:, 0:c4] = four
+    send_v[0:per_peer, c4 : 2 * c4] = blank
+    send_v[per_peer:, c4 : 2 * c4] = four[: tok_dev - per_peer]
+    send_v[: tok_dev - per_peer, 2 * c4 :] = four[per_peer:]
+    send_v[tok_dev - per_peer :, 2 * c4 :] = blank
     store = pltpu.make_async_copy(send_v, send, out_sem)
     store.start()
-    c2 = w2_v.shape[1]
-    for copy in copies[4:7]:
-        copy.wait()
-    hand_out(order_turn, matmul(hidden_v[1], w2_v[...]) + b2_v[...], sent, 0)
-    for copy in copies[7:9]:
-        copy.wait()
+    copies[4].wait()
+    rows_two = matmul(order_turn, hidden_v[1]).astype(BF16)
+    copies[5].wait()
+    copies[6].wait()
+    hand_out(matmul(rows_two, w2_v[...]) + b2_v[...], sent, 0)
+    copies[7].wait()
+    rows_same = matmul(order_turn, hidden_v[2]).astype(BF16)
+    copies[8].wait()
     for i in range(chunks):
         copies[9 + i].wait()
-        same = matmul(hidden_v[2], ws_v[i]) + bs_v[:, i * CHUNK : (i + 1) * CHUNK]
-        hand_out(order_turn, same, sent, c2 + i * CHUNK)
+        same = matmul(rows_same, ws_v[i]) + bs_v[:, i * CHUNK : (i + 1) * CHUNK]
+        hand_out(same, sent, c2 + i * CHUNK)
     store.wait()
 
 
-def hand_out(order, projected, sent, at):
-    moved = matmul(order, projected.astype(BF16)).astype(BF16)
+def hand_out(projected, sent, at):
+    moved = projected.astype(BF16)
     rows = sent[0].shape[0]
     for k, out in enumerate(sent):
         out[:, at : at + moved.shape[1]] = moved[k * rows : (k + 1) * rows]
@@ -172,9 +177,11 @@
     arrived, places, w4, b4, wj_hbm, w2_hbm, joined, w2,
     wj, tiles_v, wide_v, acc_v, out_v, weight_sems, sems,
 ):
-    weights = start_all([(wj_hbm, wj), (w2_hbm, w2)], weight_sems)
+    weights = [pltpu.make_async_copy(wj_hbm, wj, weight_sems.at[0]), pltpu.make_async_copy(w2_hbm, w2, weight_sems.at[1])]
+    weights[0].start()
     widen(arrived, places, w4, b4, tiles_v, wide_v)
     weights[0].wait()
+    weights[1].start()
     stores = [
         convolve(chunk, wide_v, wj, joined, acc_v, out_v, sems) for chunk in range(arrived.shape[0] // GRID_W)
     ]

time: 35.4 us -> 34.4 us (0.972)
  Pallas kernels: 12 us -> 11 us
    pallas_call x1, Pallas kernels: 4.04 us -> 3.07 us  [body(): pl.pallas_call(functools.partial(project_kernel, low), out_shape=(pltpu.H...]
where the time goes in v5:
time: 34.4 us; the launch traced here: 34.1 us
  starting transfers between devices  14 us (41%)
  Pallas kernels  11 us (32%)
  waiting for transfers between devices  8.41 us (24%)
  between operations  0.69 us (2%)
    ppermute x6, waiting for transfers between devices, swap(): return lax.ppermute(piece, 'rows', [(i, i ^ step) for i in range(shards)])  8.41 us
    all_to_all x1, starting transfers between devices, body(): lax.all_to_all(send.reshape(shards, per_peer, 3 * c4), 'rows', split_axis...  7.43 us
    ppermute x6, starting transfers between devices, swap(): return lax.ppermute(piece, 'rows', [(i, i ^ step) for i in range(shards)])  6.56 us
    pallas_call x1, Pallas kernels, body(): pl.pallas_call(join_kernel, out_shape=(shape((out_rows, 4 * GRID_W, feat)...  4.86 us
    pallas_call x1, Pallas kernels, body(): pl.pallas_call(functools.partial(project_kernel, low), out_shape=(pltpu.H...  3.07 us
    pallas_call x1, Pallas kernels, body(): pl.pallas_call(fetch_kernel, out_shape=tuple((pltpu.VMEM(w.shape, w.dtype...  1.62 us
    pallas_call x1, Pallas kernels, body(): pl.pallas_call(rest_kernel, out_shape=(shape((2 * row_count, 2 * GRID_W,...  1.43 us
  transfers between devices with their start and end apart: 7, of which 3 were waited for; matrix products, arithmetic and copies ran while one was open for 0% of the time, Pallas kernels for 19%

profile of v5, /device:TPU:0, one launch (start us, length us, event | category | flops | bytes accessed | tf_op | source)
XLA Modules:
  0.0 34.1 jit_solution(8752704719835964883)
XLA Ops:
  0.6 3.1 %project.1 = (bf16[128,768]{1,0:T(8,128)(2,1)}, bf16[896,128]{1,0:T(8,128)(2,1)S(1)}, bf16[32,1536]{1,0:T(8,128)(2,1)S(1)}, bf16[32,1536]{1,0:T(8,128)(2,1)S(1)}...) custom-call(bf16[3,128,1024]{2,1,0:T(8,128)(2,1)} %hidden.1, s32[16,128]{1,0:T(8,128)} %bitcast.12, ...), custom_call_target="tpu_custom_call" | custom-call | flops 469762048 | bytes 5242880 | tf_op jit(solution)/shard_map/project/pallas_call | solution.py:330
  3.7 7.4 %all-to-all-start = ((bf16[16,8,768]{2,1,0:T(8,128)(2,1)}), bf16[16,8,768]{2,1,0:T(8,128)(2,1)S(1)}, u32[]{:S(2)}, u32[]{:S(2)}) async-start(bf16[16,8,768]{2,1,0:T(8,128)(2,1)} %bitcast.11), calls=%async_computation | async-start | bytes 393216 | tf_op jit(solution)/shard_map/all_to_all | solution.py:358
  11.1 0.4 %collective-permute-start = (bf16[32,1536]{1,0:T(8,128)(2,1)S(1)}, bf16[32,1536]{1,0:T(8,128)(2,1)S(1)}, u32[]{:S(2)}, u32[]{:S(2)}) collective-permute-start(bf16[32,1536]{1,0:T(8,128)(2,1)S(1)} %get-tuple-element.28), channel_id=1, source_target_pairs={{0,1},{1,0},{2,3},{3,2},{4,5},{5,4},{6,7},{7,6},{8,9},{9,8},{10,11... | collective-permute-start | bytes 294920 | tf_op jit(solution)/shard_map/ppermute | solution.py:355
  11.6 1.6 %collective-permute-start.1 = (bf16[32,1536]{1,0:T(8,128)(2,1)S(1)}, bf16[32,1536]{1,0:T(8,128)(2,1)S(1)}, u32[]{:S(2)}, u32[]{:S(2)}) collective-permute-start(bf16[32,1536]{1,0:T(8,128)(2,1)S(1)} %get-tuple-element.29), channel_id=1, source_target_pairs={{0,2},{1,3},{2,0},{3,1},{4,6},{5,7},{6,4},{7,5},{8,10},{9,11},{10,... | collective-permute-start | bytes 294920 | tf_op jit(solution)/shard_map/ppermute | solution.py:355
  13.2 0.0 collective-permute-start.2
  13.2 1.6 %fetch.1 = (bf16[256,4096]{1,0:T(8,128)(2,1)S(1)}, f32[1,256]{1,0:T(1,128)S(1)}, f32[1,512]{1,0:T(1,128)S(1)}) custom-call(bf16[256,4096]{1,0:T(8,128)(2,1)} %w4.3, f32[1,256]{1,0:T(1,128)} %bitcast.18, f32[1,512]{1,0:T(1,128)} %bitcast.17), custom_call_target="tpu_custom_call" | custom-call | flops 1073741824 | bytes 2097152 | tf_op jit(solution)/shard_map/fetch/pallas_call | solution.py:373
  14.8 0.0 collective-permute-done.refs_1_
  14.8 3.7 %collective-permute-done.1.refs_2_ = bf16[32,1536]{1,0:T(8,128)(2,1)S(1)} collective-permute-done((bf16[32,1536]{1,0:T(8,128)(2,1)S(1)}, bf16[32,1536]{1,0:T(8,128)(2,1)S(1)}, u32[]{:S(2)}, u32[]{:S(2)}) %collective-permute-start.1) | collective-permute-done | bytes 98336 | tf_op jit(solution)/shard_map/ppermute | solution.py:355
  18.5 1.4 %collective-permute-done.2.refs_3_ = bf16[32,1536]{1,0:T(8,128)(2,1)S(1)} collective-permute-done((bf16[32,1536]{1,0:T(8,128)(2,1)S(1)}, bf16[32,1536]{1,0:T(8,128)(2,1)S(1)}, u32[]{:S(2)}, u32[]{:S(2)}) %collective-permute-start.2) | collective-permute-done | bytes 98336 | tf_op jit(solution)/shard_map/ppermute | solution.py:355
  19.9 2.1 %collective-permute-start.3 = (bf16[32,1536]{1,0:T(8,128)(2,1)S(1)}, bf16[32,1536]{1,0:T(8,128)(2,1)S(1)}, u32[]{:S(2)}, u32[]{:S(2)}) collective-permute-start(bf16[32,1536]{1,0:T(8,128)(2,1)S(1)} %get-tuple-element.32), channel_id=1, source_target_pairs={{0,4},{1,5},{2,6},{3,7},{4,0},{5,1},{6,2},{7,3},{8,12},{9,13},{10,... | collective-permute-start | bytes 294920 | tf_op jit(solution)/shard_map/ppermute | solution.py:355
  22.0 2.3 %collective-permute-start.4 = (bf16[32,1536]{1,0:T(8,128)(2,1)S(1)}, bf16[32,1536]{1,0:T(8,128)(2,1)S(1)}, u32[]{:S(2)}, u32[]{:S(2)}) collective-permute-start(bf16[32,1536]{1,0:T(8,128)(2,1)S(1)} %get-tuple-element.33), channel_id=1, source_target_pairs={{0,8},{1,9},{2,10},{3,11},{4,12},{5,13},{6,14},{7,15},{8,0},{9,1},... | collective-permute-start | bytes 294920 | tf_op jit(solution)/shard_map/ppermute | solution.py:355
  24.2 0.2 collective-permute-start.5
  24.4 0.0 all-to-all-done
  24.4 4.9 %join.1 = (bf16[8,256,256]{2,1,0:T(8,128)(2,1)}, bf16[512,2048]{1,0:T(8,128)(2,1)S(1)}) custom-call(bf16[128,768]{1,0:T(8,128)(2,1)S(1)} %bitcast.10, bf16[896,128]{1,0:T(8,128)(2,1)S(1)} %get-tuple-element.21.places, bf16[256,4096]{1,0:T(8,128)(2,1)S(1)} %get-tuple-element.22.w4, f32[1,256]{1,0:T(1,128)S(1)} %get-tuple-element.23.b4, ...), custom_call_target="tpu_custom_call" | custom-call | flops 4294967296 | bytes 4194304 | tf_op jit(solution)/shard_map/join/pallas_call | solution.py:385
  29.3 0.0 collective-permute-done.3.refs_1_
  29.3 3.4 %collective-permute-done.4.refs_2_ = bf16[32,1536]{1,0:T(8,128)(2,1)S(1)} collective-permute-done((bf16[32,1536]{1,0:T(8,128)(2,1)S(1)}, bf16[32,1536]{1,0:T(8,128)(2,1)S(1)}, u32[]{:S(2)}, u32[]{:S(2)}) %collective-permute-start.4) | collective-permute-done | bytes 98336 | tf_op jit(solution)/shard_map/ppermute | solution.py:355
  32.7 0.0 collective-permute-done.5.refs_3_
  32.7 1.4 %rest.1 = (bf16[4,128,512]{2,1,0:T(8,128)(2,1)}, bf16[128,1024]{1,0:T(8,128)(2,1)}) custom-call(bf16[896,128]{1,0:T(8,128)(2,1)S(1)} %get-tuple-element.21.places, bf16[512,2048]{1,0:T(8,128)(2,1)S(1)} %get-tuple-element.25.w2, f32[1,512]{1,0:T(1,128)S(1)} %get-tuple-element.26.b2, bf16[32,1536]{1,0:T(8,128)(2,1)S(1)} %get-tuple-element.31.refs_0_, ...), custom_call_target="tpu_custom_call" | custom-call | flops 1073741824 | bytes 4194304 | tf_op jit(solution)/shard_map/rest/pallas_call | solution.py:406
  (1 shorter events, 0.0 us)
Async XLA Ops:
  3.7 20.7 %all-to-all-start = ((bf16[16,8,768]{2,1,0:T(8,128)(2,1)}), bf16[16,8,768]{2,1,0:T(8,128)(2,1)S(1)}, u32[]{:S(2)}, u32[]{:S(2)}) async-start(bf16[16,8,768]{2,1,0:T(8,128)(2,1)} %bitcast.11), calls=%async_computation | async-start | bytes 393216 | tf_op jit(solution)/shard_map/all_to_all | solution.py:358
  11.1 3.7 %collective-permute-start = (bf16[32,1536]{1,0:T(8,128)(2,1)S(1)}, bf16[32,1536]{1,0:T(8,128)(2,1)S(1)}, u32[]{:S(2)}, u32[]{:S(2)}) collective-permute-start(bf16[32,1536]{1,0:T(8,128)(2,1)S(1)} %get-tuple-element.28), channel_id=1, source_target_pairs={{0,1},{1,0},{2,3},{3,2},{4,5},{5,4},{6,7},{7,6},{8,9},{9,8},{10,11... | collective-permute-start | bytes 294920 | tf_op jit(solution)/shard_map/ppermute | solution.py:355
  11.6 6.9 %collective-permute-start.1 = (bf16[32,1536]{1,0:T(8,128)(2,1)S(1)}, bf16[32,1536]{1,0:T(8,128)(2,1)S(1)}, u32[]{:S(2)}, u32[]{:S(2)}) collective-permute-start(bf16[32,1536]{1,0:T(8,128)(2,1)S(1)} %get-tuple-element.29), channel_id=1, source_target_pairs={{0,2},{1,3},{2,0},{3,1},{4,6},{5,7},{6,4},{7,5},{8,10},{9,11},{10,... | collective-permute-start | bytes 294920 | tf_op jit(solution)/shard_map/ppermute | solution.py:355
  13.2 6.7 %collective-permute-start.2 = (bf16[32,1536]{1,0:T(8,128)(2,1)S(1)}, bf16[32,1536]{1,0:T(8,128)(2,1)S(1)}, u32[]{:S(2)}, u32[]{:S(2)}) collective-permute-start(bf16[32,1536]{1,0:T(8,128)(2,1)S(1)} %get-tuple-element.30), channel_id=1, source_target_pairs={{0,3},{1,2},{2,1},{3,0},{4,7},{5,6},{6,5},{7,4},{8,11},{9,10},{10,... | collective-permute-start | bytes 294920 | tf_op jit(solution)/shard_map/ppermute | solution.py:355
  19.9 9.4 %collective-permute-start.3 = (bf16[32,1536]{1,0:T(8,128)(2,1)S(1)}, bf16[32,1536]{1,0:T(8,128)(2,1)S(1)}, u32[]{:S(2)}, u32[]{:S(2)}) collective-permute-start(bf16[32,1536]{1,0:T(8,128)(2,1)S(1)} %get-tuple-element.32), channel_id=1, source_target_pairs={{0,4},{1,5},{2,6},{3,7},{4,0},{5,1},{6,2},{7,3},{8,12},{9,13},{10,... | collective-permute-start | bytes 294920 | tf_op jit(solution)/shard_map/ppermute | solution.py:355
  22.0 10.7 %collective-permute-start.4 = (bf16[32,1536]{1,0:T(8,128)(2,1)S(1)}, bf16[32,1536]{1,0:T(8,128)(2,1)S(1)}, u32[]{:S(2)}, u32[]{:S(2)}) collective-permute-start(bf16[32,1536]{1,0:T(8,128)(2,1)S(1)} %get-tuple-element.33), channel_id=1, source_target_pairs={{0,8},{1,9},{2,10},{3,11},{4,12},{5,13},{6,14},{7,15},{8,0},{9,1},... | collective-permute-start | bytes 294920 | tf_op jit(solution)/shard_map/ppermute | solution.py:355
  24.2 8.4 %collective-permute-start.5 = (bf16[32,1536]{1,0:T(8,128)(2,1)S(1)}, bf16[32,1536]{1,0:T(8,128)(2,1)S(1)}, u32[]{:S(2)}, u32[]{:S(2)}) collective-permute-start(bf16[32,1536]{1,0:T(8,128)(2,1)S(1)} %get-tuple-element.34), channel_id=1, source_target_pairs={{0,12},{1,13},{2,14},{3,15},{4,8},{5,9},{6,10},{7,11},{8,4},{9,5},... | collective-permute-start | bytes 294920 | tf_op jit(solution)/shard_map/ppermute | solution.py:355

commit v6 on v5

--- a/solution.py
+++ b/solution.py
@@ -41,7 +41,7 @@
     return 1 << ((shards.bit_length()) // 2)
 
 
-def landing(table, block, tok_dev, per_peer, flip=0):
+def landing(table, block, tok_dev, per_peer, seat):
     shards = table.shape[0]
     start = block * tok_dev
     inside = jnp.logical_and(table >= start, table < start + tok_dev)
@@ -54,7 +54,7 @@
         hit = jnp.logical_and(inside, rank == float(k))
         found = jnp.sum(jnp.where(hit, place, 0.0), axis=1, keepdims=True)
         spread = spread + jnp.where(lax.rem(lane, per_peer) == k, found, 0.0)
-    own = lax.div(lane, per_peer) == jnp.bitwise_xor(iota((shards, tok_dev), 0), flip)
+    own = lax.div(lane, per_peer) == seat
     return jnp.sum(jnp.where(own, spread, 0.0), axis=0, keepdims=True).astype(jnp.int32)
 
 
@@ -65,9 +65,10 @@
     return copies
 
 
-def project_kernel(low, hidden, table_hbm, w4, b4, w2, b2, ws, bs, send, places_v, *refs):
-    sent = refs[:low]
-    hidden_v, table_v, w4_v, w2_v, ws_v, b4_v, b2_v, bs_v, send_v, sems, out_sem = refs[low:]
+def project_kernel(low, hidden, table_hbm, w4, b4, w2, b2, ws, bs, places_v, *refs):
+    high = (len(refs) - 9) - low
+    sent_four, sent = refs[:high], refs[high : high + low]
+    hidden_v, table_v, w4_v, w2_v, ws_v, b4_v, b2_v, bs_v, sems = refs[high + low :]
     chunks = ws.shape[1] // CHUNK
     copies = start_all(
         [
@@ -95,16 +96,17 @@
     square = (tok_dev, tok_dev)
     earlier = jnp.logical_and(block_col == jnp.broadcast_to(block_row, square), iota(square, 0) < iota(square, 1))
     within = jnp.sum(jnp.where(earlier, 1.0, 0.0), axis=0, keepdims=True).astype(jnp.int32)
-    slot = block_row * per_peer + within
-    order = one_hot(iota(square, 0) == slot)
-
+    row = iota(square, 0)
     apart = jnp.bitwise_xor(block_row, me)
-    turn = lax.rem(apart, low) * (shards // low) + lax.div(apart, low)
-    order_turn = one_hot(iota(square, 0) == turn * per_peer + within)
-
-    own = landing(table, me, tok_dev, per_peer)
-    above = landing(table, me - 1, tok_dev, per_peer)
-    below = landing(table, me + 1, tok_dev, per_peer)
+    order_low = one_hot(row == (lax.rem(apart, low) * high + lax.div(apart, low)) * per_peer + within)
+    orders = [one_hot(row == jnp.bitwise_xor(block_row + step, me) * per_peer + within) for step in (0, 1, -1)]
+    order_high = jnp.concatenate(orders, axis=0)
+
+    seat_low = jnp.bitwise_xor(iota((shards, tok_dev), 0), me)
+    seat_high = lax.rem(seat_low, low) * high + lax.div(seat_low, low)
+    own = landing(table, me, tok_dev, per_peer, seat_high)
+    above = landing(table, me - 1, tok_dev, per_peer, seat_high)
+    below = landing(table, me + 1, tok_dev, per_peer, seat_high)
     cell = iota(square, 0)
     col = lax.rem(cell, GRID_W)
     edge = (GRID_W, tok_dev)
@@ -122,35 +124,27 @@
         )
         base += 3 * GRID_W
 
-    places_v[base : base + tok_dev] = one_hot(cell == landing(table, me, tok_dev, per_peer, me))
+    places_v[base : base + tok_dev] = one_hot(cell == landing(table, me, tok_dev, per_peer, seat_low))
 
     c4, c2 = w4_v.shape[1], w2_v.shape[1]
-    copies[1].wait()
-    rows_four = matmul(order, hidden_v[0]).astype(BF16)
-    copies[2].wait()
-    copies[3].wait()
-    four = (matmul(rows_four, w4_v[...]) + b4_v[...]).astype(BF16)
-    blank = jnp.zeros((per_peer, c4), BF16)
-    send_v[:, 0:c4] = four
-    send_v[0:per_peer, c4 : 2 * c4] = blank
-    send_v[per_peer:, c4 : 2 * c4] = four[: tok_dev - per_peer]
-    send_v[: tok_dev - per_peer, 2 * c4 :] = four[per_peer:]
-    send_v[tok_dev - per_peer :, 2 * c4 :] = blank
-    store = pltpu.make_async_copy(send_v, send, out_sem)
-    store.start()
+    for copy in copies[1:4]:
+        copy.wait()
+    four = (matmul(hidden_v[0], w4_v[...]) + b4_v[...]).astype(BF16)
+    moved = matmul(order_high, four)
+    for i in range(3):
+        hand_out(moved[i * tok_dev : (i + 1) * tok_dev], sent_four, i * c4)
     copies[4].wait()
-    rows_two = matmul(order_turn, hidden_v[1]).astype(BF16)
+    rows_two = matmul(order_low, hidden_v[1]).astype(BF16)
     copies[5].wait()
     copies[6].wait()
     hand_out(matmul(rows_two, w2_v[...]) + b2_v[...], sent, 0)
     copies[7].wait()
-    rows_same = matmul(order_turn, hidden_v[2]).astype(BF16)
+    rows_same = matmul(order_low, hidden_v[2]).astype(BF16)
     copies[8].wait()
     for i in range(chunks):
         copies[9 + i].wait()
         same = matmul(rows_same, ws_v[i]) + bs_v[:, i * CHUNK : (i + 1) * CHUNK]
         hand_out(same, sent, c2 + i * CHUNK)
-    store.wait()
 
 
 def hand_out(projected, sent, at):
@@ -160,34 +154,33 @@
         out[:, at : at + moved.shape[1]] = moved[k * rows : (k + 1) * rows]
 
 
-def turn_kernel(low_count, *refs):
-    lows, highs = refs[:low_count], refs[low_count:]
-    rows = lows[0].shape[0] // len(highs)
-    for h, high in enumerate(highs):
-        for k, low in enumerate(lows):
-            high[k * rows : (k + 1) * rows] = low[h * rows : (h + 1) * rows]
-
-
-def fetch_kernel(w4, b4, b2, w4_v, b4_v, b2_v, sems):
-    for copy in start_all([(w4, w4_v), (b4, b4_v), (b2, b2_v)], sems):
+def turn_kernel(count, *refs):
+    arrived, leaving = refs[:count], refs[count:]
+    rows = arrived[0].shape[0] // len(leaving)
+    for to, message in enumerate(leaving):
+        for come, piece in enumerate(arrived):
+            message[come * rows : (come + 1) * rows] = piece[to * rows : (to + 1) * rows]
+
+
+def fetch_kernel(*refs):
+    count = len(refs) // 2
+    for copy in start_all(list(zip(refs[:count], refs[count:-1])), refs[-1]):
         copy.wait()
 
 
-def join_kernel(
-    arrived, places, w4, b4, wj_hbm, w2_hbm, joined, w2,
-    wj, tiles_v, wide_v, acc_v, out_v, weight_sems, sems,
-):
-    weights = [pltpu.make_async_copy(wj_hbm, wj, weight_sems.at[0]), pltpu.make_async_copy(w2_hbm, w2, weight_sems.at[1])]
-    weights[0].start()
-    widen(arrived, places, w4, b4, tiles_v, wide_v)
-    weights[0].wait()
-    weights[1].start()
-    stores = [
-        convolve(chunk, wide_v, wj, joined, acc_v, out_v, sems) for chunk in range(arrived.shape[0] // GRID_W)
-    ]
-    weights[1].wait()
+def join_kernel(places, w4, b4, wj, *refs):
+    pieces, (joined, rows_v, tiles_v, wide_v, acc_v, out_v, sems) = refs[:-7], refs[-7:]
+    gather_rows(pieces, rows_v)
+    widen(rows_v, places, w4, b4, tiles_v, wide_v)
+    stores = [convolve(chunk, wide_v, wj, joined, acc_v, out_v, sems) for chunk in range(rows_v.shape[0] // GRID_W)]
     for store in stores:
         store.wait()
+
+
+def gather_rows(pieces, rows_v):
+    rows = pieces[0].shape[0]
+    for i, piece in enumerate(pieces):
+        rows_v[i * rows : (i + 1) * rows] = piece[...]
 
 
 def widen(arrived, places, w4, b4, tiles_v, wide_v):
@@ -258,9 +251,7 @@
 
 def rest_kernel(places, w2, b2, *refs):
     arrived, (up_two, same, rows_v, acc_v, out_v, same_v, sems, same_sem) = refs[:-8], refs[-8:]
-    rows = arrived[0].shape[0]
-    for h, piece in enumerate(arrived):
-        rows_v[h * rows : (h + 1) * rows] = piece[...]
+    gather_rows(arrived, rows_v)
     tok_dev = rows_v.shape[0]
     c2 = w2.shape[0]
     row_count = tok_dev // GRID_W
@@ -327,12 +318,15 @@
         proj_same_weight,
         biases[2],
     )
-    send, places, *sent = pl.pallas_call(
+    four_shape = (low * per_peer, 3 * c4)
+    rest_shape = (high * per_peer, c2 + cs)
+    places, *sent = pl.pallas_call(
         functools.partial(project_kernel, low),
-        out_shape=(pltpu.HBM((tok_dev, 3 * c4), BF16), pltpu.VMEM((place_rows, tok_dev), BF16))
-        + (pltpu.VMEM((high * per_peer, c2 + cs), BF16),) * low,
+        out_shape=(pltpu.VMEM((place_rows, tok_dev), BF16),)
+        + (pltpu.VMEM(four_shape, BF16),) * high
+        + (pltpu.VMEM(rest_shape, BF16),) * low,
         in_specs=[ANY] * 8,
-        out_specs=(ANY,) + (VMEM,) * (1 + low),
+        out_specs=(VMEM,) * (1 + high + low),
         scratch_shapes=[
             pltpu.VMEM(hidden_states.shape, BF16),
             pltpu.VMEM(table.shape, jnp.int32),
@@ -342,71 +336,77 @@
             pltpu.VMEM((1, c4), F32),
             pltpu.VMEM((1, c2), F32),
             pltpu.VMEM((1, cs), F32),
-            pltpu.VMEM((tok_dev, 3 * c4), BF16),
             pltpu.SemaphoreType.DMA((9 + cs // CHUNK,)),
-            pltpu.SemaphoreType.DMA,
         ],
         compiler_params=pltpu.CompilerParams(vmem_limit_bytes=10 << 20),
         cost_estimate=pl.CostEstimate(flops=2 * tok_dev * hid * (c4 + c2 + cs), bytes_accessed=5 << 20, transcendentals=0),
         name="project",
     )(*(in_hbm(x) for x in inputs))
 
-    def swap(piece, step):
-        return lax.ppermute(piece, "rows", [(i, i ^ step) for i in range(shards)])
-
-    crossed = [sent[0]] + [swap(sent[k], k) for k in range(1, low)]
-    arrived = lax.all_to_all(
-        send.reshape(shards, per_peer, 3 * c4), "rows", split_axis=0, concat_axis=0, tiled=True
-    ).reshape(tok_dev, 3 * c4)
-    turned = pl.pallas_call(
-        functools.partial(turn_kernel, low),
-        out_shape=(shape((low * per_peer, c2 + cs), BF16),) * high,
-        in_specs=[VMEM] * low,
-        out_specs=(VMEM,) * high,
-        compiler_params=pltpu.CompilerParams(vmem_limit_bytes=4 << 20),
-        cost_estimate=pl.CostEstimate(flops=1 << 26, bytes_accessed=1 << 20, transcendentals=0),
-        name="turn",
-    )(*crossed)
-    landed = [turned[0]] + [swap(turned[h], h * low) for h in range(1, high)]
-
-    weights = (up4_weight, up4_bias.reshape(1, -1), up2_bias.reshape(1, -1))
-    w4, b4, b2 = pl.pallas_call(
+    def swap(pieces, unit):
+        return [pieces[0]] + [
+            lax.ppermute(piece, "rows", [(i, i ^ (step * unit)) for i in range(shards)])
+            for step, piece in enumerate(pieces[1:], 1)
+        ]
+
+    def turn(pieces, out_shape, count):
+        return pl.pallas_call(
+            functools.partial(turn_kernel, len(pieces)),
+            out_shape=(pltpu.VMEM(out_shape, BF16),) * count,
+            in_specs=[VMEM] * len(pieces),
+            out_specs=(VMEM,) * count,
+            compiler_params=pltpu.CompilerParams(vmem_limit_bytes=4 << 20),
+            cost_estimate=pl.CostEstimate(flops=1 << 26, bytes_accessed=1 << 20, transcendentals=0),
+            name="turn",
+        )(*pieces)
+
+    rest = swap(sent[high:], 1)
+    four = swap(sent[:high], low)
+    rest = turn(rest, (low * per_peer, c2 + cs), high)
+    rest = swap(rest, low)
+    four = turn(four, (high * per_peer, 3 * c4), low)
+    four = swap(four, 1)
+
+    weights = (
+        up4_weight,
+        up4_bias.reshape(1, -1),
+        join_weight.reshape(3, 3 * c4, feat),
+        up2_weight,
+        up2_bias.reshape(1, -1),
+    )
+    w4, b4, wj, w2, b2 = pl.pallas_call(
         fetch_kernel,
         out_shape=tuple(pltpu.VMEM(w.shape, w.dtype) for w in weights),
-        in_specs=[ANY] * 3,
-        out_specs=(VMEM,) * 3,
-        scratch_shapes=[pltpu.SemaphoreType.DMA((3,))],
-        cost_estimate=pl.CostEstimate(flops=1 << 30, bytes_accessed=2 << 20, transcendentals=0),
-        compiler_params=pltpu.CompilerParams(vmem_limit_bytes=4 << 20),
+        in_specs=[ANY] * 5,
+        out_specs=(VMEM,) * 5,
+        scratch_shapes=[pltpu.SemaphoreType.DMA((5,))],
+        cost_estimate=pl.CostEstimate(flops=1 << 30, bytes_accessed=5 << 20, transcendentals=0),
+        compiler_params=pltpu.CompilerParams(vmem_limit_bytes=8 << 20),
         name="fetch",
     )(*(in_hbm(w) for w in weights))
 
     out_rows = 4 * row_count
-    joined, w2 = pl.pallas_call(
+    joined = pl.pallas_call(
         join_kernel,
-        out_shape=(
-            shape((out_rows, 4 * GRID_W, feat), BF16),
-            pltpu.VMEM(up2_weight.shape, BF16),
-        ),
-        in_specs=[VMEM] * 4 + [ANY] * 2,
-        out_specs=(ANY, VMEM),
+        out_shape=shape((out_rows, 4 * GRID_W, feat), BF16),
+        in_specs=[VMEM] * (4 + low),
+        out_specs=ANY,
         scratch_shapes=[
-            pltpu.VMEM((3, 3 * c4, feat), BF16),
+            pltpu.VMEM((tok_dev, 3 * c4), BF16),
             pltpu.VMEM((place_rows, c4), BF16),
             pltpu.VMEM(((out_rows + 2) * GRID_W, 6 * c4), BF16),
             pltpu.VMEM((out_rows, feat // 128, 4 * GRID_W, 128), F32),
             pltpu.VMEM((out_rows, 4 * GRID_W, feat), BF16),
-            pltpu.SemaphoreType.DMA((2,)),
             pltpu.SemaphoreType.DMA((row_count,)),
         ],
         compiler_params=pltpu.CompilerParams(vmem_limit_bytes=20 << 20),
         cost_estimate=pl.CostEstimate(flops=4 << 30, bytes_accessed=4 << 20, transcendentals=0),
         name="join",
-    )(arrived, places, w4, b4, in_hbm(join_weight.reshape(3, 3 * c4, feat)), in_hbm(up2_weight))
+    )(places, w4, b4, wj, *four)
     upsampled_two, same_scale = pl.pallas_call(
         rest_kernel,
         out_shape=(shape((2 * row_count, 2 * GRID_W, c2), BF16), shape((tok_dev, cs), BF16)),
-        in_specs=[VMEM] * (3 + high),
+        in_specs=[VMEM] * (3 + len(rest)),
         out_specs=(ANY, ANY),
         scratch_shapes=[
             pltpu.VMEM((tok_dev, c2 + cs), BF16),
@@ -419,7 +419,7 @@
         compiler_params=pltpu.CompilerParams(vmem_limit_bytes=8 << 20),
         cost_estimate=pl.CostEstimate(flops=1 << 30, bytes_accessed=4 << 20, transcendentals=0),
         name="rest",
-    )(places, w2, b2, *landed)
+    )(places, w2, b2, *rest)
     return (joined, upsampled_two, same_scale.reshape(row_count, GRID_W, cs))
 
 

time: 34.4 us -> 32.3 us (0.939)
  waiting for transfers between devices: 8.41 us -> 6.71 us
  starting transfers between devices: 14 us -> 13 us
  Pallas kernels: 11 us -> 11.6 us
    all_to_all x1 -> x0, starting transfers between devices: 7.43 us -> none  [body(): lax.all_to_all(send.reshape(shards, per_peer, 3 * c4), 'rows', split_axis...]
    ppermute x6 -> x12, starting transfers between devices: 6.56 us -> 13 us  [swap(): lax.ppermute(piece, 'rows', [(i, i ^ step * unit) for i in range(shards)])]
    ppermute x6 -> x12, waiting for transfers between devices: 8.41 us -> 6.71 us  [swap(): lax.ppermute(piece, 'rows', [(i, i ^ step * unit) for i in range(shards)])]
    pallas_call x1, Pallas kernels: 1.62 us -> 2.64 us  [body(): pl.pallas_call(fetch_kernel, out_shape=tuple((pltpu.VMEM(w.shape, w.dtype...]
    pallas_call x3 -> x4, Pallas kernels: 7.96 us -> 7.58 us  [the longest x1 4.38 us: body(): pl.pallas_call(join_kernel, out_shape=shape((out_rows, 4 * GRID_W, feat),...]
  transfers between devices with their start and end apart: 7 -> 12, of which waited for: 3 -> 4; matrix products, arithmetic and copies ran while one was open for 0% -> 0% of each run, Pallas kernels for 19% -> 22%
where the time goes in v6:
time: 32.3 us; the launch traced here: 32.1 us
  starting transfers between devices  13 us (40%)
  Pallas kernels  11.6 us (36%)
  waiting for transfers between devices  6.71 us (21%)
  between operations  0.7 us (2%)
    ppermute x12, starting transfers between devices, swap(): lax.ppermute(piece, 'rows', [(i, i ^ step * unit) for i in range(shards)])  13 us
    ppermute x12, waiting for transfers between devices, swap(): lax.ppermute(piece, 'rows', [(i, i ^ step * unit) for i in range(shards)])  6.71 us
    pallas_call x1, Pallas kernels, body(): pl.pallas_call(join_kernel, out_shape=shape((out_rows, 4 * GRID_W, feat),...  4.38 us
    pallas_call x1, Pallas kernels, body(): pl.pallas_call(functools.partial(project_kernel, low), out_shape=(pltpu.V...  3.16 us
    pallas_call x1, Pallas kernels, body(): pl.pallas_call(fetch_kernel, out_shape=tuple((pltpu.VMEM(w.shape, w.dtype...  2.64 us
    pallas_call x1, Pallas kernels, body(): pl.pallas_call(rest_kernel, out_shape=(shape((2 * row_count, 2 * GRID_W,...  1.43 us
  transfers between devices with their start and end apart: 12, of which 4 were waited for; matrix products, arithmetic and copies ran while one was open for 0% of the time, Pallas kernels for 22%

profile of v6, /device:TPU:0, one launch (start us, length us, event | category | flops | bytes accessed | tf_op | source)
XLA Modules:
  0.0 32.1 jit_solution(797369059611708735)
XLA Ops:
  0.6 3.2 %project.1 = (bf16[896,128]{1,0:T(8,128)(2,1)S(1)}, bf16[32,768]{1,0:T(8,128)(2,1)S(1)}, bf16[32,768]{1,0:T(8,128)(2,1)S(1)}, bf16[32,768]{1,0:T(8,128)(2,1)S(1)...) custom-call(bf16[3,128,1024]{2,1,0:T(8,128)(2,1)} %hidden.1, ...), custom_call_target="tpu_custom_call" | custom-call | flops 469762048 | bytes 5242880 | tf_op jit(solution)/shard_map/project/pallas_call | solution.py:323
  3.8 0.6 %collective-permute-start.6 = (bf16[32,1536]{1,0:T(8,128)(2,1)S(1)}, bf16[32,1536]{1,0:T(8,128)(2,1)S(1)}, u32[]{:S(2)}, u32[]{:S(2)}) collective-permute-start(bf16[32,1536]{1,0:T(8,128)(2,1)S(1)} %get-tuple-element.42), channel_id=1, source_target_pairs={{0,1},{1,0},{2,3},{3,2},{4,5},{5,4},{6,7},{7,6},{8,9},{9,8},{10,11... | collective-permute-start | bytes 294920 | tf_op jit(solution)/shard_map/ppermute | solution.py:348
  4.4 2.6 %collective-permute-start = (bf16[32,768]{1,0:T(8,128)(2,1)S(1)}, bf16[32,768]{1,0:T(8,128)(2,1)S(1)}, u32[]{:S(2)}, u32[]{:S(2)}) collective-permute-start(bf16[32,768]{1,0:T(8,128)(2,1)S(1)} %get-tuple-element.32), channel_id=1, source_target_pairs={{0,4},{1,5},{2,6},{3,7},{4,0},{5,1},{6,2},{7,3},{8,12},{9,13},{10,... | collective-permute-start | bytes 147464 | tf_op jit(solution)/shard_map/ppermute | solution.py:348
  7.0 2.6 %collective-permute-start.1 = (bf16[32,768]{1,0:T(8,128)(2,1)S(1)}, bf16[32,768]{1,0:T(8,128)(2,1)S(1)}, u32[]{:S(2)}, u32[]{:S(2)}) collective-permute-start(bf16[32,768]{1,0:T(8,128)(2,1)S(1)} %get-tuple-element.33), channel_id=1, source_target_pairs={{0,8},{1,9},{2,10},{3,11},{4,12},{5,13},{6,14},{7,15},{8,0},{9,1},... | collective-permute-start | bytes 147464 | tf_op jit(solution)/shard_map/ppermute | solution.py:348
  9.6 0.0 collective-permute-start.2
  9.6 1.7 %collective-permute-start.7 = (bf16[32,1536]{1,0:T(8,128)(2,1)S(1)}, bf16[32,1536]{1,0:T(8,128)(2,1)S(1)}, u32[]{:S(2)}, u32[]{:S(2)}) collective-permute-start(bf16[32,1536]{1,0:T(8,128)(2,1)S(1)} %get-tuple-element.43), channel_id=1, source_target_pairs={{0,2},{1,3},{2,0},{3,1},{4,6},{5,7},{6,4},{7,5},{8,10},{9,11},{10,... | collective-permute-start | bytes 294920 | tf_op jit(solution)/shard_map/ppermute | solution.py:348
  11.3 0.0 collective-permute-done.refs_1_
  11.3 0.0 collective-permute-start.8
  11.3 1.8 %collective-permute-done.1.refs_2_ = bf16[32,768]{1,0:T(8,128)(2,1)S(1)} collective-permute-done((bf16[32,768]{1,0:T(8,128)(2,1)S(1)}, bf16[32,768]{1,0:T(8,128)(2,1)S(1)}, u32[]{:S(2)}, u32[]{:S(2)}) %collective-permute-start.1) | collective-permute-done | bytes 49184 | tf_op jit(solution)/shard_map/ppermute | solution.py:348
  13.1 2.4 %collective-permute-done.2.refs_3_ = bf16[32,768]{1,0:T(8,128)(2,1)S(1)} collective-permute-done((bf16[32,768]{1,0:T(8,128)(2,1)S(1)}, bf16[32,768]{1,0:T(8,128)(2,1)S(1)}, u32[]{:S(2)}, u32[]{:S(2)}) %collective-permute-start.2) | collective-permute-done | bytes 49184 | tf_op jit(solution)/shard_map/ppermute | solution.py:348
  15.5 0.1 collective-permute-start.3
  15.6 1.6 %collective-permute-start.4 = (bf16[32,768]{1,0:T(8,128)(2,1)S(1)}, bf16[32,768]{1,0:T(8,128)(2,1)S(1)}, u32[]{:S(2)}, u32[]{:S(2)}) collective-permute-start(bf16[32,768]{1,0:T(8,128)(2,1)S(1)} %get-tuple-element.37), channel_id=1, source_target_pairs={{0,2},{1,3},{2,0},{3,1},{4,6},{5,7},{6,4},{7,5},{8,10},{9,11},{10,... | collective-permute-start | bytes 147464 | tf_op jit(solution)/shard_map/ppermute | solution.py:348
  17.2 0.0 collective-permute-done.6.refs_1_
  17.2 0.3 collective-permute-start.5
  17.4 2.6 %fetch.1 = (bf16[256,4096]{1,0:T(8,128)(2,1)S(1)}, f32[1,256]{1,0:T(1,128)S(1)}, bf16[3,768,256]{2,1,0:T(8,128)(2,1)S(1)}, bf16[512,2048]{1,0:T(8,128)(2,1)S(1)}, f32[1,512]{1,0:T(1,128)S(1)}) custom-call(bf16[256,4096]{1,0:T(8,128)(2,1)} %refs_0_.1, f32[1,256]{1,0:T(1,128)} %bitcast.14, bf16[3,768,256]{2,1,0:T(8,128)(2,1)} %bitcast.8, ...), custom_call_target="tpu_custom_call" | custom-call | flops 1073741824 | bytes 5242880 | tf_op jit(solution)/shard_map/fetch/pallas_call | solution.py:377
  20.1 0.0 collective-permute-done.7.refs_2_
  20.1 1.0 %collective-permute-start.10 = (bf16[32,1536]{1,0:T(8,128)(2,1)S(1)}, bf16[32,1536]{1,0:T(8,128)(2,1)S(1)}, u32[]{:S(2)}, u32[]{:S(2)}) collective-permute-start(bf16[32,1536]{1,0:T(8,128)(2,1)S(1)} %get-tuple-element.47), channel_id=1, source_target_pairs={{0,8},{1,9},{2,10},{3,11},{4,12},{5,13},{6,14},{7,15},{8,0},{9,1},... | collective-permute-start | bytes 294920 | tf_op jit(solution)/shard_map/ppermute | solution.py:348
  21.1 0.5 %collective-permute-start.11 = (bf16[32,1536]{1,0:T(8,128)(2,1)S(1)}, bf16[32,1536]{1,0:T(8,128)(2,1)S(1)}, u32[]{:S(2)}, u32[]{:S(2)}) collective-permute-start(bf16[32,1536]{1,0:T(8,128)(2,1)S(1)} %get-tuple-element.48), channel_id=1, source_target_pairs={{0,12},{1,13},{2,14},{3,15},{4,8},{5,9},{6,10},{7,11},{8,4},{9,5},... | collective-permute-start | bytes 294920 | tf_op jit(solution)/shard_map/ppermute | solution.py:348
  21.6 2.1 %collective-permute-start.9 = (bf16[32,1536]{1,0:T(8,128)(2,1)S(1)}, bf16[32,1536]{1,0:T(8,128)(2,1)S(1)}, u32[]{:S(2)}, u32[]{:S(2)}) collective-permute-start(bf16[32,1536]{1,0:T(8,128)(2,1)S(1)} %get-tuple-element.46), channel_id=1, source_target_pairs={{0,4},{1,5},{2,6},{3,7},{4,0},{5,1},{6,2},{7,3},{8,12},{9,13},{10,... | collective-permute-start | bytes 294920 | tf_op jit(solution)/shard_map/ppermute | solution.py:348
  23.7 4.4 %join.1 = bf16[8,256,256]{2,1,0:T(8,128)(2,1)} custom-call(bf16[896,128]{1,0:T(8,128)(2,1)S(1)} %get-tuple-element.27.places, bf16[256,4096]{1,0:T(8,128)(2,1)S(1)} %get-tuple-element.28.w4, f32[1,256]{1,0:T(1,128)S(1)} %get-tuple-element.29.b4, bf16[3,768,256]{2,1,0:T(8,128)(2,1)S(1)} %get-tuple-element.30.wj, ...), custom_call_target="tpu_custom_call" | custom-call | flops 4294967296 | bytes 4194304 | tf_op jit(solution)/shard_map/join/pallas_call | solution.py:389
  28.1 1.1 %collective-permute-done.10.refs_2_ = bf16[32,1536]{1,0:T(8,128)(2,1)S(1)} collective-permute-done((bf16[32,1536]{1,0:T(8,128)(2,1)S(1)}, bf16[32,1536]{1,0:T(8,128)(2,1)S(1)}, u32[]{:S(2)}, u32[]{:S(2)}) %collective-permute-start.10) | collective-permute-done | bytes 98336 | tf_op jit(solution)/shard_map/ppermute | solution.py:348
  29.2 0.0 collective-permute-done.11.refs_3_
  29.2 1.5 %collective-permute-done.9.refs_1_ = bf16[32,1536]{1,0:T(8,128)(2,1)S(1)} collective-permute-done((bf16[32,1536]{1,0:T(8,128)(2,1)S(1)}, bf16[32,1536]{1,0:T(8,128)(2,1)S(1)}, u32[]{:S(2)}, u32[]{:S(2)}) %collective-permute-start.9) | collective-permute-done | bytes 98336 | tf_op jit(solution)/shard_map/ppermute | solution.py:348
  30.6 1.4 %rest.1 = (bf16[4,128,512]{2,1,0:T(8,128)(2,1)}, bf16[128,1024]{1,0:T(8,128)(2,1)}) custom-call(bf16[896,128]{1,0:T(8,128)(2,1)S(1)} %get-tuple-element.27.places, bf16[512,2048]{1,0:T(8,128)(2,1)S(1)} %get-tuple-element.39.w2, f32[1,512]{1,0:T(1,128)S(1)} %get-tuple-element.40.b2, bf16[32,1536]{1,0:T(8,128)(2,1)S(1)} %get-tuple-element.45.refs_0_, ...), custom_call_target="tpu_custom_call" | custom-call | flops 1073741824 | bytes 4194304 | tf_op jit(solution)/shard_map/rest/pallas_call | solution.py:406
  (6 shorter events, 0.1 us)
Async XLA Ops:
  3.8 13.4 %collective-permute-start.6 = (bf16[32,1536]{1,0:T(8,128)(2,1)S(1)}, bf16[32,1536]{1,0:T(8,128)(2,1)S(1)}, u32[]{:S(2)}, u32[]{:S(2)}) collective-permute-start(bf16[32,1536]{1,0:T(8,128)(2,1)S(1)} %get-tuple-element.42), channel_id=1, source_target_pairs={{0,1},{1,0},{2,3},{3,2},{4,5},{5,4},{6,7},{7,6},{8,9},{9,8},{10,11... | collective-permute-start | bytes 294920 | tf_op jit(solution)/shard_map/ppermute | solution.py:348
  4.4 7.0 %collective-permute-start = (bf16[32,768]{1,0:T(8,128)(2,1)S(1)}, bf16[32,768]{1,0:T(8,128)(2,1)S(1)}, u32[]{:S(2)}, u32[]{:S(2)}) collective-permute-start(bf16[32,768]{1,0:T(8,128)(2,1)S(1)} %get-tuple-element.32), channel_id=1, source_target_pairs={{0,4},{1,5},{2,6},{3,7},{4,0},{5,1},{6,2},{7,3},{8,12},{9,13},{10,... | collective-permute-start | bytes 147464 | tf_op jit(solution)/shard_map/ppermute | solution.py:348
  7.0 6.1 %collective-permute-start.1 = (bf16[32,768]{1,0:T(8,128)(2,1)S(1)}, bf16[32,768]{1,0:T(8,128)(2,1)S(1)}, u32[]{:S(2)}, u32[]{:S(2)}) collective-permute-start(bf16[32,768]{1,0:T(8,128)(2,1)S(1)} %get-tuple-element.33), channel_id=1, source_target_pairs={{0,8},{1,9},{2,10},{3,11},{4,12},{5,13},{6,14},{7,15},{8,0},{9,1},... | collective-permute-start | bytes 147464 | tf_op jit(solution)/shard_map/ppermute | solution.py:348
  9.6 5.9 %collective-permute-start.2 = (bf16[32,768]{1,0:T(8,128)(2,1)S(1)}, bf16[32,768]{1,0:T(8,128)(2,1)S(1)}, u32[]{:S(2)}, u32[]{:S(2)}) collective-permute-start(bf16[32,768]{1,0:T(8,128)(2,1)S(1)} %get-tuple-element.34), channel_id=1, source_target_pairs={{0,12},{1,13},{2,14},{3,15},{4,8},{5,9},{6,10},{7,11},{8,4},{9,5},... | collective-permute-start | bytes 147464 | tf_op jit(solution)/shard_map/ppermute | solution.py:348
  9.6 10.5 %collective-permute-start.7 = (bf16[32,1536]{1,0:T(8,128)(2,1)S(1)}, bf16[32,1536]{1,0:T(8,128)(2,1)S(1)}, u32[]{:S(2)}, u32[]{:S(2)}) collective-permute-start(bf16[32,1536]{1,0:T(8,128)(2,1)S(1)} %get-tuple-element.43), channel_id=1, source_target_pairs={{0,2},{1,3},{2,0},{3,1},{4,6},{5,7},{6,4},{7,5},{8,10},{9,11},{10,... | collective-permute-start | bytes 294920 | tf_op jit(solution)/shard_map/ppermute | solution.py:348
  11.3 8.8 %collective-permute-start.8 = (bf16[32,1536]{1,0:T(8,128)(2,1)S(1)}, bf16[32,1536]{1,0:T(8,128)(2,1)S(1)}, u32[]{:S(2)}, u32[]{:S(2)}) collective-permute-start(bf16[32,1536]{1,0:T(8,128)(2,1)S(1)} %get-tuple-element.44), channel_id=1, source_target_pairs={{0,3},{1,2},{2,1},{3,0},{4,7},{5,6},{6,5},{7,4},{8,11},{9,10},{10,... | collective-permute-start | bytes 294920 | tf_op jit(solution)/shard_map/ppermute | solution.py:348
  15.5 6.1 %collective-permute-start.3 = (bf16[32,768]{1,0:T(8,128)(2,1)S(1)}, bf16[32,768]{1,0:T(8,128)(2,1)S(1)}, u32[]{:S(2)}, u32[]{:S(2)}) collective-permute-start(bf16[32,768]{1,0:T(8,128)(2,1)S(1)} %get-tuple-element.36), channel_id=1, source_target_pairs={{0,1},{1,0},{2,3},{3,2},{4,5},{5,4},{6,7},{7,6},{8,9},{9,8},{10,11... | collective-permute-start | bytes 147464 | tf_op jit(solution)/shard_map/ppermute | solution.py:348
  15.6 8.1 %collective-permute-start.4 = (bf16[32,768]{1,0:T(8,128)(2,1)S(1)}, bf16[32,768]{1,0:T(8,128)(2,1)S(1)}, u32[]{:S(2)}, u32[]{:S(2)}) collective-permute-start(bf16[32,768]{1,0:T(8,128)(2,1)S(1)} %get-tuple-element.37), channel_id=1, source_target_pairs={{0,2},{1,3},{2,0},{3,1},{4,6},{5,7},{6,4},{7,5},{8,10},{9,11},{10,... | collective-permute-start | bytes 147464 | tf_op jit(solution)/shard_map/ppermute | solution.py:348
  17.2 6.5 %collective-permute-start.5 = (bf16[32,768]{1,0:T(8,128)(2,1)S(1)}, bf16[32,768]{1,0:T(8,128)(2,1)S(1)}, u32[]{:S(2)}, u32[]{:S(2)}) collective-permute-start(bf16[32,768]{1,0:T(8,128)(2,1)S(1)} %get-tuple-element.38), channel_id=1, source_target_pairs={{0,3},{1,2},{2,1},{3,0},{4,7},{5,6},{6,5},{7,4},{8,11},{9,10},{10,... | collective-permute-start | bytes 147464 | tf_op jit(solution)/shard_map/ppermute | solution.py:348
  20.1 9.0 %collective-permute-start.10 = (bf16[32,1536]{1,0:T(8,128)(2,1)S(1)}, bf16[32,1536]{1,0:T(8,128)(2,1)S(1)}, u32[]{:S(2)}, u32[]{:S(2)}) collective-permute-start(bf16[32,1536]{1,0:T(8,128)(2,1)S(1)} %get-tuple-element.47), channel_id=1, source_target_pairs={{0,8},{1,9},{2,10},{3,11},{4,12},{5,13},{6,14},{7,15},{8,0},{9,1},... | collective-permute-start | bytes 294920 | tf_op jit(solution)/shard_map/ppermute | solution.py:348
  21.1 8.0 %collective-permute-start.11 = (bf16[32,1536]{1,0:T(8,128)(2,1)S(1)}, bf16[32,1536]{1,0:T(8,128)(2,1)S(1)}, u32[]{:S(2)}, u32[]{:S(2)}) collective-permute-start(bf16[32,1536]{1,0:T(8,128)(2,1)S(1)} %get-tuple-element.48), channel_id=1, source_target_pairs={{0,12},{1,13},{2,14},{3,15},{4,8},{5,9},{6,10},{7,11},{8,4},{9,5},... | collective-permute-start | bytes 294920 | tf_op jit(solution)/shard_map/ppermute | solution.py:348
  21.6 9.0 %collective-permute-start.9 = (bf16[32,1536]{1,0:T(8,128)(2,1)S(1)}, bf16[32,1536]{1,0:T(8,128)(2,1)S(1)}, u32[]{:S(2)}, u32[]{:S(2)}) collective-permute-start(bf16[32,1536]{1,0:T(8,128)(2,1)S(1)} %get-tuple-element.46), channel_id=1, source_target_pairs={{0,4},{1,5},{2,6},{3,7},{4,0},{5,1},{6,2},{7,3},{8,12},{9,13},{10,... | collective-permute-start | bytes 294920 | tf_op jit(solution)/shard_map/ppermute | solution.py:348

commit v7 on v6

--- a/solution.py
+++ b/solution.py
@@ -109,21 +109,14 @@
     below = landing(table, me + 1, tok_dev, per_peer, seat_high)
     cell = iota(square, 0)
     col = lax.rem(cell, GRID_W)
-    edge = (GRID_W, tok_dev)
-    edge_col = iota(edge, 0)
-    last = edge_col + (tok_dev - GRID_W)
-    places_v[0:tok_dev] = one_hot(cell == own)
-    places_v[tok_dev : 2 * tok_dev] = one_hot(jnp.logical_and(cell == own + 1, col != 0))
-    places_v[2 * tok_dev : 3 * tok_dev] = one_hot(jnp.logical_and(cell == own - 1, col != GRID_W - 1))
-    base = 3 * tok_dev
-    for source, target in ((above, last), (below, edge_col)):
-        places_v[base : base + GRID_W] = one_hot(target == source)
-        places_v[base + GRID_W : base + 2 * GRID_W] = one_hot(jnp.logical_and(target == source + 1, edge_col != 0))
-        places_v[base + 2 * GRID_W : base + 3 * GRID_W] = one_hot(
-            jnp.logical_and(target == source - 1, edge_col != GRID_W - 1)
-        )
-        base += 3 * GRID_W
-
+    edge_col = iota((GRID_W, tok_dev), 0)
+    base = 0
+    for source, target, at in ((own, cell, col), (above, edge_col + (tok_dev - GRID_W), edge_col), (below, edge_col, edge_col)):
+        size = target.shape[0]
+        places_v[base : base + size] = one_hot(jnp.logical_and(target == source + 1, at != 0))
+        places_v[base + size : base + 2 * size] = one_hot(target == source)
+        places_v[base + 2 * size : base + 3 * size] = one_hot(jnp.logical_and(target == source - 1, at != GRID_W - 1))
+        base += 3 * size
     places_v[base : base + tok_dev] = one_hot(cell == landing(table, me, tok_dev, per_peer, seat_low))
 
     c4, c2 = w4_v.shape[1], w2_v.shape[1]
@@ -169,12 +162,11 @@
 
 
 def join_kernel(places, w4, b4, wj, *refs):
-    pieces, (joined, rows_v, tiles_v, wide_v, acc_v, out_v, sems) = refs[:-7], refs[-7:]
+    pieces, (begun, wide_v, rows_v, tiles_v, acc_v) = refs[:-5], refs[-5:]
     gather_rows(pieces, rows_v)
     widen(rows_v, places, w4, b4, tiles_v, wide_v)
-    stores = [convolve(chunk, wide_v, wj, joined, acc_v, out_v, sems) for chunk in range(rows_v.shape[0] // GRID_W)]
-    for store in stores:
-        store.wait()
+    for chunk in range(begun.shape[0] // 4):
+        convolve(chunk, wide_v, wj, acc_v, begun, 4 * chunk)
 
 
 def gather_rows(pieces, rows_v):
@@ -201,33 +193,29 @@
     left = jnp.where(iota((GRID_W, 1), 0) == 0, 0.0, 1.0)
     right = jnp.where(iota((GRID_W, 1), 0) == GRID_W - 1, 0.0, 1.0)
 
-    def fill(first, stride, rows, tap, to, scale):
+    def fill(first, rows, tap, to, scale):
         size = rows * GRID_W
         for b in range(4):
-            part = matmul(tiles_v[first : first + size], w4[:, (tap * 4 + b) * feat : (tap * 4 + b + 1) * feat]) + bias
+            start = first + (0 if b == 3 else size)
+            stop = first + (3 if b == 0 else 2) * size
+            part = matmul(tiles_v[start:stop], w4[:, (tap * 4 + b) * feat : (tap * 4 + b + 1) * feat]) + bias
             if scale is not None:
                 part = part * scale
-            for i in range(rows):
-                wide_v[pl.ds(to(i) * GRID_W, GRID_W), (b + 1) * feat : (b + 2) * feat] = part[
-                    i * GRID_W : (i + 1) * GRID_W
-                ].astype(BF16)
-        for b, shift, edge, block in ((3, 1, left, 0), (0, 2, right, 5)):
-            start = first + shift * stride
-            part = matmul(tiles_v[start : start + size], w4[:, (tap * 4 + b) * feat : (tap * 4 + b + 1) * feat]) + bias
-            if scale is not None:
-                part = part * scale
-            for i in range(rows):
-                wide_v[pl.ds(to(i) * GRID_W, GRID_W), block * feat : (block + 1) * feat] = (
-                    part[i * GRID_W : (i + 1) * GRID_W] * edge
-                ).astype(BF16)
+            blocks = {0: ((1, None), (5, right)), 3: ((0, left), (4, None))}.get(b, ((b + 1, None),))
+            for place, (block, edge) in enumerate(blocks):
+                for i in range(rows):
+                    piece = part[(place * rows + i) * GRID_W : (place * rows + i + 1) * GRID_W]
+                    if edge is not None:
+                        piece = piece * edge
+                    wide_v[pl.ds(to(i) * GRID_W, GRID_W), block * feat : (block + 1) * feat] = piece.astype(BF16)
 
     for tap in range(4):
-        fill(0, tok_dev, row_count, tap, lambda i, tap=tap: 4 * i + tap + 1, None)
-    fill(3 * tok_dev, GRID_W, 1, 3, lambda i: 0, top)
-    fill(3 * tok_dev + 3 * GRID_W, GRID_W, 1, 0, lambda i: 4 * row_count + 1, bottom)
-
-
-def convolve(chunk, wide_v, wj, joined, acc_v, out_v, sems):
+        fill(0, row_count, tap, lambda i, tap=tap: 4 * i + tap + 1, None)
+    fill(3 * tok_dev, 1, 3, lambda i: 0, top)
+    fill(3 * tok_dev + 3 * GRID_W, 1, 0, lambda i: 4 * row_count + 1, bottom)
+
+
+def convolve(chunk, wide_v, wj, acc_v, out_v, at):
     feat = wj.shape[2]
     for b in range(4):
         total = None
@@ -237,28 +225,33 @@
             total = term if total is None else total + term
         for r in range(4):
             for block in range(feat // 128):
-                acc_v[4 * chunk + r, block, pl.ds(b, GRID_W, 4), :] = total[
+                acc_v[r, block, pl.ds(b, GRID_W, 4), :] = total[
                     r * GRID_W : (r + 1) * GRID_W, block * 128 : (block + 1) * 128
                 ]
-    for r in range(4 * chunk, 4 * chunk + 4):
+    for r in range(4):
         for block in range(feat // 128):
-            out_v[r, :, block * 128 : (block + 1) * 128] = acc_v[r, block].astype(BF16)
-    rows = pl.ds(4 * chunk, 4)
-    store = pltpu.make_async_copy(out_v.at[rows], joined.at[rows], sems.at[chunk])
-    store.start()
-    return store
-
-
-def rest_kernel(places, w2, b2, *refs):
-    arrived, (up_two, same, rows_v, acc_v, out_v, same_v, sems, same_sem) = refs[:-8], refs[-8:]
+            out_v[at + r, :, block * 128 : (block + 1) * 128] = acc_v[r, block].astype(BF16)
+
+
+def rest_kernel(begun, wide, wj, places, w2, b2, *refs):
+    arrived, outs = refs[:-12], refs[-12:]
+    joined, up_two, same, rows_v, acc_v, out_v, same_v, acc_join_v, join_v, sems, same_sem, join_sems = outs
+    cut = begun.shape[0]
+    joins = [
+        pltpu.make_async_copy(begun, joined.at[pl.ds(0, cut)], join_sems.at[0]),
+        pltpu.make_async_copy(join_v, joined.at[pl.ds(cut, 4)], join_sems.at[1]),
+    ]
+    joins[0].start()
     gather_rows(arrived, rows_v)
     tok_dev = rows_v.shape[0]
     c2 = w2.shape[0]
     row_count = tok_dev // GRID_W
     place = places[places.shape[0] - tok_dev :]
     same_v[...] = matmul(place, rows_v[:, c2:]).astype(BF16)
-    stores = [pltpu.make_async_copy(same_v, same, same_sem)]
+    stores = [pltpu.make_async_copy(same_v, same, same_sem), *joins]
     stores[0].start()
+    convolve(row_count - 1, wide, wj, acc_join_v, join_v, 0)
+    joins[1].start()
     tile = matmul(place, rows_v[:, 0:c2]).astype(BF16)
     bias = b2[...]
     for a in range(2):
@@ -386,40 +379,45 @@
     )(*(in_hbm(w) for w in weights))
 
     out_rows = 4 * row_count
-    joined = pl.pallas_call(
+    join_shape = (out_rows, 4 * GRID_W, feat)
+    wide_shape = ((out_rows + 2) * GRID_W, 6 * c4)
+
+    acc_shape = (4, feat // 128, 4 * GRID_W, 128)
+
+    begun, wide = pl.pallas_call(
         join_kernel,
-        out_shape=shape((out_rows, 4 * GRID_W, feat), BF16),
+        out_shape=(pltpu.VMEM((out_rows - 4, 4 * GRID_W, feat), BF16), pltpu.VMEM(wide_shape, BF16)),
         in_specs=[VMEM] * (4 + low),
-        out_specs=ANY,
+        out_specs=(VMEM, VMEM),
         scratch_shapes=[
             pltpu.VMEM((tok_dev, 3 * c4), BF16),
             pltpu.VMEM((place_rows, c4), BF16),
-            pltpu.VMEM(((out_rows + 2) * GRID_W, 6 * c4), BF16),
-            pltpu.VMEM((out_rows, feat // 128, 4 * GRID_W, 128), F32),
-            pltpu.VMEM((out_rows, 4 * GRID_W, feat), BF16),
-            pltpu.SemaphoreType.DMA((row_count,)),
+            pltpu.VMEM(acc_shape, F32),
         ],
         compiler_params=pltpu.CompilerParams(vmem_limit_bytes=20 << 20),
         cost_estimate=pl.CostEstimate(flops=4 << 30, bytes_accessed=4 << 20, transcendentals=0),
         name="join",
     )(places, w4, b4, wj, *four)
-    upsampled_two, same_scale = pl.pallas_call(
+    joined, upsampled_two, same_scale = pl.pallas_call(
         rest_kernel,
-        out_shape=(shape((2 * row_count, 2 * GRID_W, c2), BF16), shape((tok_dev, cs), BF16)),
-        in_specs=[VMEM] * (3 + len(rest)),
-        out_specs=(ANY, ANY),
+        out_shape=(shape(join_shape, BF16), shape((2 * row_count, 2 * GRID_W, c2), BF16), shape((tok_dev, cs), BF16)),
+        in_specs=[VMEM] * (6 + len(rest)),
+        out_specs=(ANY, ANY, ANY),
         scratch_shapes=[
             pltpu.VMEM((tok_dev, c2 + cs), BF16),
             pltpu.VMEM((2 * row_count, c2 // 128, 2 * GRID_W, 128), F32),
             pltpu.VMEM((2 * row_count, 2 * GRID_W, c2), BF16),
             pltpu.VMEM((tok_dev, cs), BF16),
+            pltpu.VMEM(acc_shape, F32),
+            pltpu.VMEM((4, 4 * GRID_W, feat), BF16),
             pltpu.SemaphoreType.DMA((2 * row_count,)),
             pltpu.SemaphoreType.DMA,
+            pltpu.SemaphoreType.DMA((2,)),
         ],
-        compiler_params=pltpu.CompilerParams(vmem_limit_bytes=8 << 20),
-        cost_estimate=pl.CostEstimate(flops=1 << 30, bytes_accessed=4 << 20, transcendentals=0),
+        compiler_params=pltpu.CompilerParams(vmem_limit_bytes=12 << 20),
+        cost_estimate=pl.CostEstimate(flops=2 << 30, bytes_accessed=4 << 20, transcendentals=0),
         name="rest",
-    )(places, w2, b2, *rest)
+    )(begun, wide, wj, places, w2, b2, *rest)
     return (joined, upsampled_two, same_scale.reshape(row_count, GRID_W, cs))
 
 

time: 32.3 us -> 34 us (1.053)
  waiting for transfers between devices: 6.71 us -> 8.5 us
  Pallas kernels: 11.6 us -> 10.7 us
  starting transfers between devices: 13 us -> 13.9 us
    ppermute x12, waiting for transfers between devices: 6.71 us -> 8.5 us  [swap(): lax.ppermute(piece, 'rows', [(i, i ^ step * unit) for i in range(shards)])]
    pallas_call x2, Pallas kernels: 5.81 us -> 4.88 us  [the longest x1 2.72 us: body(): pl.pallas_call(rest_kernel, out_shape=(shape(join_shape, BF16), shape((2...]
    ppermute x12, starting transfers between devices: 13 us -> 13.9 us  [swap(): lax.ppermute(piece, 'rows', [(i, i ^ step * unit) for i in range(shards)])]
  transfers between devices with their start and end apart: 12 -> 12, of which waited for: 4 -> 3; matrix products, arithmetic and copies ran while one was open for 0% -> 0% of each run, Pallas kernels for 22% -> 14%
where the time goes in v7:
time: 34 us; the launch traced here: 33.8 us
  starting transfers between devices  13.9 us (41%)
  Pallas kernels  10.7 us (31%)
  waiting for transfers between devices  8.5 us (25%)
  between operations  0.71 us (2%)
    ppermute x12, starting transfers between devices, swap(): lax.ppermute(piece, 'rows', [(i, i ^ step * unit) for i in range(shards)])  13.9 us
    ppermute x12, waiting for transfers between devices, swap(): lax.ppermute(piece, 'rows', [(i, i ^ step * unit) for i in range(shards)])  8.5 us
    pallas_call x1, Pallas kernels, body(): pl.pallas_call(functools.partial(project_kernel, low), out_shape=(pltpu.V...  3.16 us
    pallas_call x1, Pallas kernels, body(): pl.pallas_call(rest_kernel, out_shape=(shape(join_shape, BF16), shape((2...  2.72 us
    pallas_call x1, Pallas kernels, body(): pl.pallas_call(fetch_kernel, out_shape=tuple((pltpu.VMEM(w.shape, w.dtype...  2.64 us
    pallas_call x1, Pallas kernels, body(): pl.pallas_call(join_kernel, out_shape=(pltpu.VMEM((out_rows - 4, 4 * GRID...  2.16 us
  transfers between devices with their start and end apart: 12, of which 3 were waited for; matrix products, arithmetic and copies ran while one was open for 0% of the time, Pallas kernels for 14%

profile of v7, /device:TPU:0, one launch (start us, length us, event | category | flops | bytes accessed | tf_op | source)
XLA Modules:
  0.0 33.8 jit_solution(2452399197771610958)
XLA Ops:
  0.6 3.2 %project.1 = (bf16[896,128]{1,0:T(8,128)(2,1)S(1)}, bf16[32,768]{1,0:T(8,128)(2,1)S(1)}, bf16[32,768]{1,0:T(8,128)(2,1)S(1)}, bf16[32,768]{1,0:T(8,128)(2,1)S(1)...) custom-call(bf16[3,128,1024]{2,1,0:T(8,128)(2,1)} %hidden.1, ...), custom_call_target="tpu_custom_call" | custom-call | flops 469762048 | bytes 5242880 | tf_op jit(solution)/shard_map/project/pallas_call | solution.py:316
  3.8 0.6 %collective-permute-start.6 = (bf16[32,1536]{1,0:T(8,128)(2,1)S(1)}, bf16[32,1536]{1,0:T(8,128)(2,1)S(1)}, u32[]{:S(2)}, u32[]{:S(2)}) collective-permute-start(bf16[32,1536]{1,0:T(8,128)(2,1)S(1)} %get-tuple-element.47), channel_id=1, source_target_pairs={{0,1},{1,0},{2,3},{3,2},{4,5},{5,4},{6,7},{7,6},{8,9},{9,8},{10,11... | collective-permute-start | bytes 294920 | tf_op jit(solution)/shard_map/ppermute | solution.py:341
  4.4 2.6 %collective-permute-start = (bf16[32,768]{1,0:T(8,128)(2,1)S(1)}, bf16[32,768]{1,0:T(8,128)(2,1)S(1)}, u32[]{:S(2)}, u32[]{:S(2)}) collective-permute-start(bf16[32,768]{1,0:T(8,128)(2,1)S(1)} %get-tuple-element.35), channel_id=1, source_target_pairs={{0,4},{1,5},{2,6},{3,7},{4,0},{5,1},{6,2},{7,3},{8,12},{9,13},{10,... | collective-permute-start | bytes 147464 | tf_op jit(solution)/shard_map/ppermute | solution.py:341
  7.0 2.6 %collective-permute-start.1 = (bf16[32,768]{1,0:T(8,128)(2,1)S(1)}, bf16[32,768]{1,0:T(8,128)(2,1)S(1)}, u32[]{:S(2)}, u32[]{:S(2)}) collective-permute-start(bf16[32,768]{1,0:T(8,128)(2,1)S(1)} %get-tuple-element.36), channel_id=1, source_target_pairs={{0,8},{1,9},{2,10},{3,11},{4,12},{5,13},{6,14},{7,15},{8,0},{9,1},... | collective-permute-start | bytes 147464 | tf_op jit(solution)/shard_map/ppermute | solution.py:341
  9.6 0.0 collective-permute-start.2
  9.6 1.7 %collective-permute-start.7 = (bf16[32,1536]{1,0:T(8,128)(2,1)S(1)}, bf16[32,1536]{1,0:T(8,128)(2,1)S(1)}, u32[]{:S(2)}, u32[]{:S(2)}) collective-permute-start(bf16[32,1536]{1,0:T(8,128)(2,1)S(1)} %get-tuple-element.48), channel_id=1, source_target_pairs={{0,2},{1,3},{2,0},{3,1},{4,6},{5,7},{6,4},{7,5},{8,10},{9,11},{10,... | collective-permute-start | bytes 294920 | tf_op jit(solution)/shard_map/ppermute | solution.py:341
  11.3 0.0 collective-permute-done.refs_1_
  11.3 0.0 collective-permute-start.8
  11.3 1.8 %collective-permute-done.1.refs_2_ = bf16[32,768]{1,0:T(8,128)(2,1)S(1)} collective-permute-done((bf16[32,768]{1,0:T(8,128)(2,1)S(1)}, bf16[32,768]{1,0:T(8,128)(2,1)S(1)}, u32[]{:S(2)}, u32[]{:S(2)}) %collective-permute-start.1) | collective-permute-done | bytes 49184 | tf_op jit(solution)/shard_map/ppermute | solution.py:341
  13.1 2.4 %collective-permute-done.2.refs_3_ = bf16[32,768]{1,0:T(8,128)(2,1)S(1)} collective-permute-done((bf16[32,768]{1,0:T(8,128)(2,1)S(1)}, bf16[32,768]{1,0:T(8,128)(2,1)S(1)}, u32[]{:S(2)}, u32[]{:S(2)}) %collective-permute-start.2) | collective-permute-done | bytes 49184 | tf_op jit(solution)/shard_map/ppermute | solution.py:341
  15.5 0.1 collective-permute-start.3
  15.6 1.6 %collective-permute-start.4 = (bf16[32,768]{1,0:T(8,128)(2,1)S(1)}, bf16[32,768]{1,0:T(8,128)(2,1)S(1)}, u32[]{:S(2)}, u32[]{:S(2)}) collective-permute-start(bf16[32,768]{1,0:T(8,128)(2,1)S(1)} %get-tuple-element.40), channel_id=1, source_target_pairs={{0,2},{1,3},{2,0},{3,1},{4,6},{5,7},{6,4},{7,5},{8,10},{9,11},{10,... | collective-permute-start | bytes 147464 | tf_op jit(solution)/shard_map/ppermute | solution.py:341
  17.2 0.0 collective-permute-done.6.refs_1_
  17.2 0.3 collective-permute-start.5
  17.4 2.6 %fetch.1 = (bf16[256,4096]{1,0:T(8,128)(2,1)S(1)}, f32[1,256]{1,0:T(1,128)S(1)}, bf16[3,768,256]{2,1,0:T(8,128)(2,1)S(1)}, bf16[512,2048]{1,0:T(8,128)(2,1)S(1)}, f32[1,512]{1,0:T(1,128)S(1)}) custom-call(bf16[256,4096]{1,0:T(8,128)(2,1)} %refs_0_.1, f32[1,256]{1,0:T(1,128)} %bitcast.14, bf16[3,768,256]{2,1,0:T(8,128)(2,1)} %bitcast.8, ...), custom_call_target="tpu_custom_call" | custom-call | flops 1073741824 | bytes 5242880 | tf_op jit(solution)/shard_map/fetch/pallas_call | solution.py:370
  20.1 0.0 collective-permute-done.7.refs_2_
  20.1 0.0 collective-permute-done.8.refs_3_
  20.1 0.1 collective-permute-start.9
  20.2 1.9 %collective-permute-start.10 = (bf16[32,1536]{1,0:T(8,128)(2,1)S(1)}, bf16[32,1536]{1,0:T(8,128)(2,1)S(1)}, u32[]{:S(2)}, u32[]{:S(2)}) collective-permute-start(bf16[32,1536]{1,0:T(8,128)(2,1)S(1)} %get-tuple-element.52), channel_id=1, source_target_pairs={{0,8},{1,9},{2,10},{3,11},{4,12},{5,13},{6,14},{7,15},{8,0},{9,1},... | collective-permute-start | bytes 294920 | tf_op jit(solution)/shard_map/ppermute | solution.py:341
  22.1 2.5 %collective-permute-start.11 = (bf16[32,1536]{1,0:T(8,128)(2,1)S(1)}, bf16[32,1536]{1,0:T(8,128)(2,1)S(1)}, u32[]{:S(2)}, u32[]{:S(2)}) collective-permute-start(bf16[32,1536]{1,0:T(8,128)(2,1)S(1)} %get-tuple-element.53), channel_id=1, source_target_pairs={{0,12},{1,13},{2,14},{3,15},{4,8},{5,9},{6,10},{7,11},{8,4},{9,5},... | collective-permute-start | bytes 294920 | tf_op jit(solution)/shard_map/ppermute | solution.py:341
  24.6 2.2 %join.1 = (bf16[4,256,256]{2,1,0:T(8,128)(2,1)S(1)}, bf16[640,1536]{1,0:T(8,128)(2,1)S(1)}) custom-call(bf16[896,128]{1,0:T(8,128)(2,1)S(1)} %get-tuple-element.30.places, bf16[256,4096]{1,0:T(8,128)(2,1)S(1)} %get-tuple-element.31.w4, f32[1,256]{1,0:T(1,128)S(1)} %get-tuple-element.32.b4, bf16[3,768,256]{2,1,0:T(8,128)(2,1)S(1)} %get-tuple-element.33.wj, ...), custom_call_target="tpu_custom_call" | custom-call | flops 4294967296 | bytes 4194304 | tf_op jit(solution)/shard_map/join/pallas_call | solution.py:387
  26.8 0.0 collective-permute-done.9.refs_1_
  26.8 4.3 %collective-permute-done.10.refs_2_ = bf16[32,1536]{1,0:T(8,128)(2,1)S(1)} collective-permute-done((bf16[32,1536]{1,0:T(8,128)(2,1)S(1)}, bf16[32,1536]{1,0:T(8,128)(2,1)S(1)}, u32[]{:S(2)}, u32[]{:S(2)}) %collective-permute-start.10) | collective-permute-done | bytes 98336 | tf_op jit(solution)/shard_map/ppermute | solution.py:341
  31.1 2.7 %rest.1 = (bf16[8,256,256]{2,1,0:T(8,128)(2,1)}, bf16[4,128,512]{2,1,0:T(8,128)(2,1)}, bf16[128,1024]{1,0:T(8,128)(2,1)}) custom-call(bf16[4,256,256]{2,1,0:T(8,128)(2,1)S(1)} %get-tuple-element.42.begun, bf16[640,1536]{1,0:T(8,128)(2,1)S(1)} %get-tuple-element.43.wide, bf16[3,768,256]{2,1,0:T(8,128)(2,1)S(1)} %get-tuple-element.33.wj, ...), custom_call_target="tpu_custom_call" | custom-call | flops 2147483648 | bytes 4194304 | tf_op jit(solution)/shard_map/rest/pallas_call | solution.py:401
  (6 shorter events, 0.1 us)
Async XLA Ops:
  3.8 13.4 %collective-permute-start.6 = (bf16[32,1536]{1,0:T(8,128)(2,1)S(1)}, bf16[32,1536]{1,0:T(8,128)(2,1)S(1)}, u32[]{:S(2)}, u32[]{:S(2)}) collective-permute-start(bf16[32,1536]{1,0:T(8,128)(2,1)S(1)} %get-tuple-element.47), channel_id=1, source_target_pairs={{0,1},{1,0},{2,3},{3,2},{4,5},{5,4},{6,7},{7,6},{8,9},{9,8},{10,11... | collective-permute-start | bytes 294920 | tf_op jit(solution)/shard_map/ppermute | solution.py:341
  4.4 7.0 %collective-permute-start = (bf16[32,768]{1,0:T(8,128)(2,1)S(1)}, bf16[32,768]{1,0:T(8,128)(2,1)S(1)}, u32[]{:S(2)}, u32[]{:S(2)}) collective-permute-start(bf16[32,768]{1,0:T(8,128)(2,1)S(1)} %get-tuple-element.35), channel_id=1, source_target_pairs={{0,4},{1,5},{2,6},{3,7},{4,0},{5,1},{6,2},{7,3},{8,12},{9,13},{10,... | collective-permute-start | bytes 147464 | tf_op jit(solution)/shard_map/ppermute | solution.py:341
  7.0 6.1 %collective-permute-start.1 = (bf16[32,768]{1,0:T(8,128)(2,1)S(1)}, bf16[32,768]{1,0:T(8,128)(2,1)S(1)}, u32[]{:S(2)}, u32[]{:S(2)}) collective-permute-start(bf16[32,768]{1,0:T(8,128)(2,1)S(1)} %get-tuple-element.36), channel_id=1, source_target_pairs={{0,8},{1,9},{2,10},{3,11},{4,12},{5,13},{6,14},{7,15},{8,0},{9,1},... | collective-permute-start | bytes 147464 | tf_op jit(solution)/shard_map/ppermute | solution.py:341
  9.6 5.9 %collective-permute-start.2 = (bf16[32,768]{1,0:T(8,128)(2,1)S(1)}, bf16[32,768]{1,0:T(8,128)(2,1)S(1)}, u32[]{:S(2)}, u32[]{:S(2)}) collective-permute-start(bf16[32,768]{1,0:T(8,128)(2,1)S(1)} %get-tuple-element.37), channel_id=1, source_target_pairs={{0,12},{1,13},{2,14},{3,15},{4,8},{5,9},{6,10},{7,11},{8,4},{9,5},... | collective-permute-start | bytes 147464 | tf_op jit(solution)/shard_map/ppermute | solution.py:341
  9.6 10.5 %collective-permute-start.7 = (bf16[32,1536]{1,0:T(8,128)(2,1)S(1)}, bf16[32,1536]{1,0:T(8,128)(2,1)S(1)}, u32[]{:S(2)}, u32[]{:S(2)}) collective-permute-start(bf16[32,1536]{1,0:T(8,128)(2,1)S(1)} %get-tuple-element.48), channel_id=1, source_target_pairs={{0,2},{1,3},{2,0},{3,1},{4,6},{5,7},{6,4},{7,5},{8,10},{9,11},{10,... | collective-permute-start | bytes 294920 | tf_op jit(solution)/shard_map/ppermute | solution.py:341
  11.3 8.8 %collective-permute-start.8 = (bf16[32,1536]{1,0:T(8,128)(2,1)S(1)}, bf16[32,1536]{1,0:T(8,128)(2,1)S(1)}, u32[]{:S(2)}, u32[]{:S(2)}) collective-permute-start(bf16[32,1536]{1,0:T(8,128)(2,1)S(1)} %get-tuple-element.49), channel_id=1, source_target_pairs={{0,3},{1,2},{2,1},{3,0},{4,7},{5,6},{6,5},{7,4},{8,11},{9,10},{10,... | collective-permute-start | bytes 294920 | tf_op jit(solution)/shard_map/ppermute | solution.py:341
  15.5 6.6 %collective-permute-start.3 = (bf16[32,768]{1,0:T(8,128)(2,1)S(1)}, bf16[32,768]{1,0:T(8,128)(2,1)S(1)}, u32[]{:S(2)}, u32[]{:S(2)}) collective-permute-start(bf16[32,768]{1,0:T(8,128)(2,1)S(1)} %get-tuple-element.39), channel_id=1, source_target_pairs={{0,1},{1,0},{2,3},{3,2},{4,5},{5,4},{6,7},{7,6},{8,9},{9,8},{10,11... | collective-permute-start | bytes 147464 | tf_op jit(solution)/shard_map/ppermute | solution.py:341
  15.6 9.0 %collective-permute-start.4 = (bf16[32,768]{1,0:T(8,128)(2,1)S(1)}, bf16[32,768]{1,0:T(8,128)(2,1)S(1)}, u32[]{:S(2)}, u32[]{:S(2)}) collective-permute-start(bf16[32,768]{1,0:T(8,128)(2,1)S(1)} %get-tuple-element.40), channel_id=1, source_target_pairs={{0,2},{1,3},{2,0},{3,1},{4,6},{5,7},{6,4},{7,5},{8,10},{9,11},{10,... | collective-permute-start | bytes 147464 | tf_op jit(solution)/shard_map/ppermute | solution.py:341
  17.2 7.4 %collective-permute-start.5 = (bf16[32,768]{1,0:T(8,128)(2,1)S(1)}, bf16[32,768]{1,0:T(8,128)(2,1)S(1)}, u32[]{:S(2)}, u32[]{:S(2)}) collective-permute-start(bf16[32,768]{1,0:T(8,128)(2,1)S(1)} %get-tuple-element.41), channel_id=1, source_target_pairs={{0,3},{1,2},{2,1},{3,0},{4,7},{5,6},{6,5},{7,4},{8,11},{9,10},{10,... | collective-permute-start | bytes 147464 | tf_op jit(solution)/shard_map/ppermute | solution.py:341
  20.1 6.7 %collective-permute-start.9 = (bf16[32,1536]{1,0:T(8,128)(2,1)S(1)}, bf16[32,1536]{1,0:T(8,128)(2,1)S(1)}, u32[]{:S(2)}, u32[]{:S(2)}) collective-permute-start(bf16[32,1536]{1,0:T(8,128)(2,1)S(1)} %get-tuple-element.51), channel_id=1, source_target_pairs={{0,4},{1,5},{2,6},{3,7},{4,0},{5,1},{6,2},{7,3},{8,12},{9,13},{10,... | collective-permute-start | bytes 294920 | tf_op jit(solution)/shard_map/ppermute | solution.py:341
  20.2 10.9 %collective-permute-start.10 = (bf16[32,1536]{1,0:T(8,128)(2,1)S(1)}, bf16[32,1536]{1,0:T(8,128)(2,1)S(1)}, u32[]{:S(2)}, u32[]{:S(2)}) collective-permute-start(bf16[32,1536]{1,0:T(8,128)(2,1)S(1)} %get-tuple-element.52), channel_id=1, source_target_pairs={{0,8},{1,9},{2,10},{3,11},{4,12},{5,13},{6,14},{7,15},{8,0},{9,1},... | collective-permute-start | bytes 294920 | tf_op jit(solution)/shard_map/ppermute | solution.py:341
  22.1 9.0 %collective-permute-start.11 = (bf16[32,1536]{1,0:T(8,128)(2,1)S(1)}, bf16[32,1536]{1,0:T(8,128)(2,1)S(1)}, u32[]{:S(2)}, u32[]{:S(2)}) collective-permute-start(bf16[32,1536]{1,0:T(8,128)(2,1)S(1)} %get-tuple-element.53), channel_id=1, source_target_pairs={{0,12},{1,13},{2,14},{3,15},{4,8},{5,9},{6,10},{7,11},{8,4},{9,5},... | collective-permute-start | bytes 294920 | tf_op jit(solution)/shard_map/ppermute | solution.py:341

commit v8 on v7

--- a/solution.py
+++ b/solution.py
@@ -9,7 +9,7 @@
 
 
 GRID_W = 64
-CHUNK = 512
+CHUNK = 1024
 F32 = jnp.float32
 BF16 = jnp.bfloat16
 ANY = pl.BlockSpec(memory_space=pl.ANY)
@@ -99,8 +99,18 @@
     row = iota(square, 0)
     apart = jnp.bitwise_xor(block_row, me)
     order_low = one_hot(row == (lax.rem(apart, low) * high + lax.div(apart, low)) * per_peer + within)
-    orders = [one_hot(row == jnp.bitwise_xor(block_row + step, me) * per_peer + within) for step in (0, 1, -1)]
-    order_high = jnp.concatenate(orders, axis=0)
+    plane, unit = lax.div(block_row, low), lax.rem(block_row, low)
+    my_plane = lax.div(me, low)
+
+    def row_of(to_plane, to_unit):
+        return (jnp.bitwise_xor(to_plane, my_plane) * (low + 2) + to_unit) * per_peer + within
+
+    row = iota((high * (low + 2) * per_peer, tok_dev), 0)
+    nowhere = jnp.full_like(unit, -1)
+    here = row == row_of(plane, unit + 1)
+    next_plane = row == jnp.where(unit == low - 1, row_of(plane + 1, 0), nowhere)
+    last_plane = row == jnp.where(unit == 0, row_of(plane - 1, low + 1), nowhere)
+    order_high = one_hot(jnp.logical_or(here, jnp.logical_or(next_plane, last_plane)))
 
     seat_low = jnp.bitwise_xor(iota((shards, tok_dev), 0), me)
     seat_high = lax.rem(seat_low, low) * high + lax.div(seat_low, low)
@@ -119,13 +129,11 @@
         base += 3 * size
     places_v[base : base + tok_dev] = one_hot(cell == landing(table, me, tok_dev, per_peer, seat_low))
 
-    c4, c2 = w4_v.shape[1], w2_v.shape[1]
+    c2 = w2_v.shape[1]
     for copy in copies[1:4]:
         copy.wait()
     four = (matmul(hidden_v[0], w4_v[...]) + b4_v[...]).astype(BF16)
-    moved = matmul(order_high, four)
-    for i in range(3):
-        hand_out(moved[i * tok_dev : (i + 1) * tok_dev], sent_four, i * c4)
+    hand_out(matmul(order_high, four), sent_four, 0)
     copies[4].wait()
     rows_two = matmul(order_low, hidden_v[1]).astype(BF16)
     copies[5].wait()
@@ -155,6 +163,34 @@
             message[come * rows : (come + 1) * rows] = piece[to * rows : (to + 1) * rows]
 
 
+def turn_four_kernel(low, per_peer, *refs):
+    high = len(refs) - low - 1
+    arrived, leaving, rows_v = refs[:high], refs[high:-1], refs[-1]
+    mine = lax.rem(lax.axis_index("rows"), low)
+    c4 = rows_v.shape[1]
+    count = high * per_peer
+    if per_peer % 8 == 0:
+        for k, message in enumerate(leaving):
+            unit = jnp.bitwise_xor(mine, k)
+            for h, piece in enumerate(arrived):
+                for place, step in enumerate((1, 0, 2)):
+                    first = pl.multiple_of((unit + step) * per_peer, per_peer)
+                    message[h * per_peer : (h + 1) * per_peer, place * c4 : (place + 1) * c4] = piece[
+                        pl.ds(first, per_peer), :
+                    ]
+        return
+    gather_rows(arrived, rows_v)
+    total = rows_v.shape[0]
+    to = iota((low * count, total), 0)
+    h = lax.rem(lax.div(to, per_peer), high)
+    unit = jnp.bitwise_xor(lax.div(to, count), mine)
+    for place, step in enumerate((1, 0, 2)):
+        source = (h * (low + 2) + unit + step) * per_peer + lax.rem(to, per_peer)
+        moved = matmul(one_hot(iota(to.shape, 1) == source), rows_v[...]).astype(BF16)
+        for k, message in enumerate(leaving):
+            message[:, place * c4 : (place + 1) * c4] = moved[k * count : (k + 1) * count]
+
+
 def fetch_kernel(*refs):
     count = len(refs) // 2
     for copy in start_all(list(zip(refs[:count], refs[count:-1])), refs[-1]):
@@ -162,11 +198,18 @@
 
 
 def join_kernel(places, w4, b4, wj, *refs):
-    pieces, (begun, wide_v, rows_v, tiles_v, acc_v) = refs[:-5], refs[-5:]
+    pieces, (begun, last, rows_v, tiles_v, wide_v, acc_v, out_v, sems) = refs[:-8], refs[-8:]
     gather_rows(pieces, rows_v)
     widen(rows_v, places, w4, b4, tiles_v, wide_v)
-    for chunk in range(begun.shape[0] // 4):
-        convolve(chunk, wide_v, wj, acc_v, begun, 4 * chunk)
+    stores = []
+    for chunk in range(out_v.shape[0] // 4):
+        rows = pl.ds(4 * chunk, 4)
+        convolve(chunk, wide_v, wj, acc_v, out_v, 4 * chunk)
+        stores.append(pltpu.make_async_copy(out_v.at[rows], begun.at[rows], sems.at[chunk]))
+        stores[-1].start()
+    convolve(out_v.shape[0] // 4, wide_v, wj, acc_v, last, 0)
+    for store in stores:
+        store.wait()
 
 
 def gather_rows(pieces, rows_v):
@@ -217,6 +260,7 @@
 
 def convolve(chunk, wide_v, wj, acc_v, out_v, at):
     feat = wj.shape[2]
+    slot = chunk % 2
     for b in range(4):
         total = None
         for row_tap in range(3):
@@ -225,33 +269,32 @@
             total = term if total is None else total + term
         for r in range(4):
             for block in range(feat // 128):
-                acc_v[r, block, pl.ds(b, GRID_W, 4), :] = total[
+                acc_v[4 * slot + r, block, pl.ds(b, GRID_W, 4), :] = total[
                     r * GRID_W : (r + 1) * GRID_W, block * 128 : (block + 1) * 128
                 ]
     for r in range(4):
         for block in range(feat // 128):
-            out_v[at + r, :, block * 128 : (block + 1) * 128] = acc_v[r, block].astype(BF16)
-
-
-def rest_kernel(begun, wide, wj, places, w2, b2, *refs):
-    arrived, outs = refs[:-12], refs[-12:]
-    joined, up_two, same, rows_v, acc_v, out_v, same_v, acc_join_v, join_v, sems, same_sem, join_sems = outs
-    cut = begun.shape[0]
-    joins = [
-        pltpu.make_async_copy(begun, joined.at[pl.ds(0, cut)], join_sems.at[0]),
-        pltpu.make_async_copy(join_v, joined.at[pl.ds(cut, 4)], join_sems.at[1]),
+            out_v[at + r, :, block * 128 : (block + 1) * 128] = acc_v[4 * slot + r, block].astype(BF16)
+
+
+def rest_kernel(begun, last, places, w2, b2, *refs):
+    del begun
+    arrived, outs = refs[:-9], refs[-9:]
+    joined, up_two, same, rows_v, acc_v, out_v, same_v, sems, end_sems = outs
+    tail = joined.shape[0] - last.shape[0]
+    ends = [
+        pltpu.make_async_copy(last, joined.at[pl.ds(tail, last.shape[0])], end_sems.at[0]),
+        pltpu.make_async_copy(same_v, same, end_sems.at[1]),
     ]
-    joins[0].start()
+    ends[0].start()
     gather_rows(arrived, rows_v)
     tok_dev = rows_v.shape[0]
     c2 = w2.shape[0]
     row_count = tok_dev // GRID_W
     place = places[places.shape[0] - tok_dev :]
     same_v[...] = matmul(place, rows_v[:, c2:]).astype(BF16)
-    stores = [pltpu.make_async_copy(same_v, same, same_sem), *joins]
-    stores[0].start()
-    convolve(row_count - 1, wide, wj, acc_join_v, join_v, 0)
-    joins[1].start()
+    ends[1].start()
+    stores = [*ends]
     tile = matmul(place, rows_v[:, 0:c2]).astype(BF16)
     bias = b2[...]
     for a in range(2):
@@ -311,7 +354,7 @@
         proj_same_weight,
         biases[2],
     )
-    four_shape = (low * per_peer, 3 * c4)
+    four_shape = ((low + 2) * per_peer, c4)
     rest_shape = (high * per_peer, c2 + cs)
     places, *sent = pl.pallas_call(
         functools.partial(project_kernel, low),
@@ -337,17 +380,18 @@
     )(*(in_hbm(x) for x in inputs))
 
     def swap(pieces, unit):
-        return [pieces[0]] + [
-            lax.ppermute(piece, "rows", [(i, i ^ (step * unit)) for i in range(shards)])
-            for step, piece in enumerate(pieces[1:], 1)
-        ]
-
-    def turn(pieces, out_shape, count):
+        moved = [pieces[0]]
+        for step, piece in enumerate(pieces[1:], 1):
+            moved.append(lax.ppermute(piece, "rows", [(i, i ^ (step * unit)) for i in range(shards)]))
+        return moved
+
+    def turn(kernel, pieces, out_shape, count, scratch=()):
         return pl.pallas_call(
-            functools.partial(turn_kernel, len(pieces)),
+            kernel,
             out_shape=(pltpu.VMEM(out_shape, BF16),) * count,
             in_specs=[VMEM] * len(pieces),
             out_specs=(VMEM,) * count,
+            scratch_shapes=scratch,
             compiler_params=pltpu.CompilerParams(vmem_limit_bytes=4 << 20),
             cost_estimate=pl.CostEstimate(flops=1 << 26, bytes_accessed=1 << 20, transcendentals=0),
             name="turn",
@@ -355,9 +399,15 @@
 
     rest = swap(sent[high:], 1)
     four = swap(sent[:high], low)
-    rest = turn(rest, (low * per_peer, c2 + cs), high)
+    rest = turn(functools.partial(turn_kernel, low), rest, (low * per_peer, c2 + cs), high)
     rest = swap(rest, low)
-    four = turn(four, (high * per_peer, 3 * c4), low)
+    four = turn(
+        functools.partial(turn_four_kernel, low, per_peer),
+        four,
+        (high * per_peer, 3 * c4),
+        low,
+        [pltpu.VMEM((high * (low + 2) * per_peer, c4), BF16)],
+    )
     four = swap(four, 1)
 
     weights = (
@@ -380,19 +430,18 @@
 
     out_rows = 4 * row_count
     join_shape = (out_rows, 4 * GRID_W, feat)
-    wide_shape = ((out_rows + 2) * GRID_W, 6 * c4)
-
-    acc_shape = (4, feat // 128, 4 * GRID_W, 128)
-
-    begun, wide = pl.pallas_call(
+    begun, last = pl.pallas_call(
         join_kernel,
-        out_shape=(pltpu.VMEM((out_rows - 4, 4 * GRID_W, feat), BF16), pltpu.VMEM(wide_shape, BF16)),
+        out_shape=(pltpu.HBM(join_shape, BF16), pltpu.VMEM((4, 4 * GRID_W, feat), BF16)),
         in_specs=[VMEM] * (4 + low),
-        out_specs=(VMEM, VMEM),
+        out_specs=(ANY, VMEM),
         scratch_shapes=[
             pltpu.VMEM((tok_dev, 3 * c4), BF16),
             pltpu.VMEM((place_rows, c4), BF16),
-            pltpu.VMEM(acc_shape, F32),
+            pltpu.VMEM(((out_rows + 2) * GRID_W, 6 * c4), BF16),
+            pltpu.VMEM((8, feat // 128, 4 * GRID_W, 128), F32),
+            pltpu.VMEM((out_rows - 4, 4 * GRID_W, feat), BF16),
+            pltpu.SemaphoreType.DMA((row_count - 1,)),
         ],
         compiler_params=pltpu.CompilerParams(vmem_limit_bytes=20 << 20),
         cost_estimate=pl.CostEstimate(flops=4 << 30, bytes_accessed=4 << 20, transcendentals=0),
@@ -401,23 +450,21 @@
     joined, upsampled_two, same_scale = pl.pallas_call(
         rest_kernel,
         out_shape=(shape(join_shape, BF16), shape((2 * row_count, 2 * GRID_W, c2), BF16), shape((tok_dev, cs), BF16)),
-        in_specs=[VMEM] * (6 + len(rest)),
+        in_specs=[ANY] + [VMEM] * (4 + len(rest)),
         out_specs=(ANY, ANY, ANY),
         scratch_shapes=[
             pltpu.VMEM((tok_dev, c2 + cs), BF16),
             pltpu.VMEM((2 * row_count, c2 // 128, 2 * GRID_W, 128), F32),
             pltpu.VMEM((2 * row_count, 2 * GRID_W, c2), BF16),
             pltpu.VMEM((tok_dev, cs), BF16),
-            pltpu.VMEM(acc_shape, F32),
-            pltpu.VMEM((4, 4 * GRID_W, feat), BF16),
             pltpu.SemaphoreType.DMA((2 * row_count,)),
-            pltpu.SemaphoreType.DMA,
             pltpu.SemaphoreType.DMA((2,)),
         ],
+        input_output_aliases={0: 0},
         compiler_params=pltpu.CompilerParams(vmem_limit_bytes=12 << 20),
         cost_estimate=pl.CostEstimate(flops=2 << 30, bytes_accessed=4 << 20, transcendentals=0),
         name="rest",
-    )(begun, wide, wj, places, w2, b2, *rest)
+    )(begun, last, places, w2, b2, *rest)
     return (joined, upsampled_two, same_scale.reshape(row_count, GRID_W, cs))
 
 

time: 34 us -> 32.3 us (0.950)
  waiting for transfers between devices: 8.5 us -> 6.41 us
  Pallas kernels: 10.7 us -> 11.1 us
    ppermute x12, waiting for transfers between devices: 8.5 us -> 6.41 us  [swap(): lax.ppermute(piece, 'rows', [(i, i ^ step * unit) for i in range(shards)])]
    pallas_call x3, Pallas kernels: 2.21 us -> 4.04 us  [the longest x1 3.98 us: body(): pl.pallas_call(join_kernel, out_shape=(pltpu.HBM(join_shape, BF16), pltpu...]
    pallas_call x1, Pallas kernels: 2.72 us -> 1.44 us  [body(): pl.pallas_call(rest_kernel, out_shape=(shape(join_shape, BF16), shape((2...]
  transfers between devices with their start and end apart: 12 -> 12, of which waited for: 3 -> 3; matrix products, arithmetic and copies ran while one was open for 0% -> 0% of each run, Pallas kernels for 14% -> 21%
where the time goes in v8:
time: 32.3 us; the launch traced here: 32.1 us
  starting transfers between devices  13.9 us (43%)
  Pallas kernels  11.1 us (34%)
  waiting for transfers between devices  6.41 us (20%)
  between operations  0.72 us (2%)
    ppermute x12, starting transfers between devices, swap(): lax.ppermute(piece, 'rows', [(i, i ^ step * unit) for i in range(shards)])  13.9 us
    ppermute x12, waiting for transfers between devices, swap(): lax.ppermute(piece, 'rows', [(i, i ^ step * unit) for i in range(shards)])  6.41 us
    pallas_call x1, Pallas kernels, body(): pl.pallas_call(join_kernel, out_shape=(pltpu.HBM(join_shape, BF16), pltpu...  3.98 us
    pallas_call x1, Pallas kernels, body(): pl.pallas_call(functools.partial(project_kernel, low), out_shape=(pltpu.V...  2.93 us
    pallas_call x1, Pallas kernels, body(): pl.pallas_call(fetch_kernel, out_shape=tuple((pltpu.VMEM(w.shape, w.dtype...  2.64 us
    pallas_call x1, Pallas kernels, body(): pl.pallas_call(rest_kernel, out_shape=(shape(join_shape, BF16), shape((2...  1.44 us
  transfers between devices with their start and end apart: 12, of which 3 were waited for; matrix products, arithmetic and copies ran while one was open for 0% of the time, Pallas kernels for 21%

profile of v8, /device:TPU:0, one launch (start us, length us, event | category | flops | bytes accessed | tf_op | source)
XLA Modules:
  0.0 32.1 jit_solution(13910355852902535847)
XLA Ops:
  0.6 2.9 %project.1 = (bf16[896,128]{1,0:T(8,128)(2,1)S(1)}, bf16[48,256]{1,0:T(8,128)(2,1)S(1)}, bf16[48,256]{1,0:T(8,128)(2,1)S(1)}, bf16[48,256]{1,0:T(8,128)(2,1)S(1)...) custom-call(bf16[3,128,1024]{2,1,0:T(8,128)(2,1)} %hidden.1, ...), custom_call_target="tpu_custom_call" | custom-call | flops 469762048 | bytes 5242880 | tf_op jit(solution)/shard_map/project/pallas_call | solution.py:359
  3.6 0.6 %collective-permute-start.6 = (bf16[32,1536]{1,0:T(8,128)(2,1)S(1)}, bf16[32,1536]{1,0:T(8,128)(2,1)S(1)}, u32[]{:S(2)}, u32[]{:S(2)}) collective-permute-start(bf16[32,1536]{1,0:T(8,128)(2,1)S(1)} %get-tuple-element.47), channel_id=1, source_target_pairs={{0,1},{1,0},{2,3},{3,2},{4,5},{5,4},{6,7},{7,6},{8,9},{9,8},{10,11... | collective-permute-start | bytes 294920 | tf_op jit(solution)/shard_map/ppermute | solution.py:385
  4.1 2.6 %collective-permute-start = (bf16[48,256]{1,0:T(8,128)(2,1)S(1)}, bf16[48,256]{1,0:T(8,128)(2,1)S(1)}, u32[]{:S(2)}, u32[]{:S(2)}) collective-permute-start(bf16[48,256]{1,0:T(8,128)(2,1)S(1)} %get-tuple-element.35), channel_id=1, source_target_pairs={{0,4},{1,5},{2,6},{3,7},{4,0},{5,1},{6,2},{7,3},{8,12},{9,13},{10,... | collective-permute-start | bytes 73736 | tf_op jit(solution)/shard_map/ppermute | solution.py:385
  6.8 2.6 %collective-permute-start.1 = (bf16[48,256]{1,0:T(8,128)(2,1)S(1)}, bf16[48,256]{1,0:T(8,128)(2,1)S(1)}, u32[]{:S(2)}, u32[]{:S(2)}) collective-permute-start(bf16[48,256]{1,0:T(8,128)(2,1)S(1)} %get-tuple-element.36), channel_id=1, source_target_pairs={{0,8},{1,9},{2,10},{3,11},{4,12},{5,13},{6,14},{7,15},{8,0},{9,1},... | collective-permute-start | bytes 73736 | tf_op jit(solution)/shard_map/ppermute | solution.py:385
  9.4 0.0 collective-permute-start.2
  9.4 1.7 %collective-permute-start.7 = (bf16[32,1536]{1,0:T(8,128)(2,1)S(1)}, bf16[32,1536]{1,0:T(8,128)(2,1)S(1)}, u32[]{:S(2)}, u32[]{:S(2)}) collective-permute-start(bf16[32,1536]{1,0:T(8,128)(2,1)S(1)} %get-tuple-element.48), channel_id=1, source_target_pairs={{0,2},{1,3},{2,0},{3,1},{4,6},{5,7},{6,4},{7,5},{8,10},{9,11},{10,... | collective-permute-start | bytes 294920 | tf_op jit(solution)/shard_map/ppermute | solution.py:385
  11.1 0.0 collective-permute-done.refs_1_
  11.1 0.5 %collective-permute-done.1.refs_2_ = bf16[48,256]{1,0:T(8,128)(2,1)S(1)} collective-permute-done((bf16[48,256]{1,0:T(8,128)(2,1)S(1)}, bf16[48,256]{1,0:T(8,128)(2,1)S(1)}, u32[]{:S(2)}, u32[]{:S(2)}) %collective-permute-start.1) | collective-permute-done | bytes 24608 | tf_op jit(solution)/shard_map/ppermute | solution.py:385
  11.6 3.4 %collective-permute-done.2.refs_3_ = bf16[48,256]{1,0:T(8,128)(2,1)S(1)} collective-permute-done((bf16[48,256]{1,0:T(8,128)(2,1)S(1)}, bf16[48,256]{1,0:T(8,128)(2,1)S(1)}, u32[]{:S(2)}, u32[]{:S(2)}) %collective-permute-start.2) | collective-permute-done | bytes 24608 | tf_op jit(solution)/shard_map/ppermute | solution.py:385
  15.0 0.1 collective-permute-start.3
  15.1 1.6 %collective-permute-start.4 = (bf16[32,768]{1,0:T(8,128)(2,1)S(1)}, bf16[32,768]{1,0:T(8,128)(2,1)S(1)}, u32[]{:S(2)}, u32[]{:S(2)}) collective-permute-start(bf16[32,768]{1,0:T(8,128)(2,1)S(1)} %get-tuple-element.40), channel_id=1, source_target_pairs={{0,2},{1,3},{2,0},{3,1},{4,6},{5,7},{6,4},{7,5},{8,10},{9,11},{10,... | collective-permute-start | bytes 147464 | tf_op jit(solution)/shard_map/ppermute | solution.py:385
  16.7 0.0 collective-permute-done.6.refs_1_
  16.7 0.3 collective-permute-start.5
  17.0 2.6 %fetch.1 = (bf16[256,4096]{1,0:T(8,128)(2,1)S(1)}, f32[1,256]{1,0:T(1,128)S(1)}, bf16[3,768,256]{2,1,0:T(8,128)(2,1)S(1)}, bf16[512,2048]{1,0:T(8,128)(2,1)S(1)}, f32[1,512]{1,0:T(1,128)S(1)}) custom-call(bf16[256,4096]{1,0:T(8,128)(2,1)} %refs_0_.1, f32[1,256]{1,0:T(1,128)} %bitcast.14, bf16[3,768,256]{2,1,0:T(8,128)(2,1)} %bitcast.8, ...), custom_call_target="tpu_custom_call" | custom-call | flops 1073741824 | bytes 5242880 | tf_op jit(solution)/shard_map/fetch/pallas_call | solution.py:420
  19.6 0.0 collective-permute-done.7.refs_2_
  19.6 0.0 collective-permute-done.8.refs_3_
  19.7 0.1 collective-permute-start.9
  19.7 0.9 %collective-permute-start.10 = (bf16[32,1536]{1,0:T(8,128)(2,1)S(1)}, bf16[32,1536]{1,0:T(8,128)(2,1)S(1)}, u32[]{:S(2)}, u32[]{:S(2)}) collective-permute-start(bf16[32,1536]{1,0:T(8,128)(2,1)S(1)} %get-tuple-element.52), channel_id=1, source_target_pairs={{0,8},{1,9},{2,10},{3,11},{4,12},{5,13},{6,14},{7,15},{8,0},{9,1},... | collective-permute-start | bytes 294920 | tf_op jit(solution)/shard_map/ppermute | solution.py:385
  20.6 0.0 collective-permute-done.3.refs_1_
  20.6 3.5 %collective-permute-start.11 = (bf16[32,1536]{1,0:T(8,128)(2,1)S(1)}, bf16[32,1536]{1,0:T(8,128)(2,1)S(1)}, u32[]{:S(2)}, u32[]{:S(2)}) collective-permute-start(bf16[32,1536]{1,0:T(8,128)(2,1)S(1)} %get-tuple-element.53), channel_id=1, source_target_pairs={{0,12},{1,13},{2,14},{3,15},{4,8},{5,9},{6,10},{7,11},{8,4},{9,5},... | collective-permute-start | bytes 294920 | tf_op jit(solution)/shard_map/ppermute | solution.py:385
  24.1 0.0 collective-permute-done.4.refs_2_
  24.1 4.0 %join.1 = (bf16[8,256,256]{2,1,0:T(8,128)(2,1)}, bf16[4,256,256]{2,1,0:T(8,128)(2,1)S(1)}) custom-call(bf16[896,128]{1,0:T(8,128)(2,1)S(1)} %get-tuple-element.30.places, bf16[256,4096]{1,0:T(8,128)(2,1)S(1)} %get-tuple-element.31.w4, f32[1,256]{1,0:T(1,128)S(1)} %get-tuple-element.32.b4, bf16[3,768,256]{2,1,0:T(8,128)(2,1)S(1)} %get-tuple-element.33.wj, ...), custom_call_target="tpu_custom_call" | custom-call | flops 4294967296 | bytes 4194304 | tf_op jit(solution)/shard_map/join/pallas_call | solution.py:433
  28.1 2.5 %collective-permute-done.10.refs_2_ = bf16[32,1536]{1,0:T(8,128)(2,1)S(1)} collective-permute-done((bf16[32,1536]{1,0:T(8,128)(2,1)S(1)}, bf16[32,1536]{1,0:T(8,128)(2,1)S(1)}, u32[]{:S(2)}, u32[]{:S(2)}) %collective-permute-start.10) | collective-permute-done | bytes 98336 | tf_op jit(solution)/shard_map/ppermute | solution.py:385
  30.6 1.4 %rest.1 = (bf16[8,256,256]{2,1,0:T(8,128)(2,1)}, bf16[4,128,512]{2,1,0:T(8,128)(2,1)}, bf16[128,1024]{1,0:T(8,128)(2,1)}) custom-call(bf16[8,256,256]{2,1,0:T(8,128)(2,1)} %get-tuple-element.42.begun, bf16[4,256,256]{2,1,0:T(8,128)(2,1)S(1)} %get-tuple-element.43.last, ...), custom_call_target="tpu_custom_call", output_to_operand_aliasing={{0}: (0, {})} | custom-call | flops 2147483648 | bytes 4194304 | tf_op jit(solution)/shard_map/rest/pallas_call | solution.py:450
  (6 shorter events, 0.1 us)
Async XLA Ops:
  3.6 13.1 %collective-permute-start.6 = (bf16[32,1536]{1,0:T(8,128)(2,1)S(1)}, bf16[32,1536]{1,0:T(8,128)(2,1)S(1)}, u32[]{:S(2)}, u32[]{:S(2)}) collective-permute-start(bf16[32,1536]{1,0:T(8,128)(2,1)S(1)} %get-tuple-element.47), channel_id=1, source_target_pairs={{0,1},{1,0},{2,3},{3,2},{4,5},{5,4},{6,7},{7,6},{8,9},{9,8},{10,11... | collective-permute-start | bytes 294920 | tf_op jit(solution)/shard_map/ppermute | solution.py:385
  4.1 7.0 %collective-permute-start = (bf16[48,256]{1,0:T(8,128)(2,1)S(1)}, bf16[48,256]{1,0:T(8,128)(2,1)S(1)}, u32[]{:S(2)}, u32[]{:S(2)}) collective-permute-start(bf16[48,256]{1,0:T(8,128)(2,1)S(1)} %get-tuple-element.35), channel_id=1, source_target_pairs={{0,4},{1,5},{2,6},{3,7},{4,0},{5,1},{6,2},{7,3},{8,12},{9,13},{10,... | collective-permute-start | bytes 73736 | tf_op jit(solution)/shard_map/ppermute | solution.py:385
  6.8 4.8 %collective-permute-start.1 = (bf16[48,256]{1,0:T(8,128)(2,1)S(1)}, bf16[48,256]{1,0:T(8,128)(2,1)S(1)}, u32[]{:S(2)}, u32[]{:S(2)}) collective-permute-start(bf16[48,256]{1,0:T(8,128)(2,1)S(1)} %get-tuple-element.36), channel_id=1, source_target_pairs={{0,8},{1,9},{2,10},{3,11},{4,12},{5,13},{6,14},{7,15},{8,0},{9,1},... | collective-permute-start | bytes 73736 | tf_op jit(solution)/shard_map/ppermute | solution.py:385
  9.4 5.6 %collective-permute-start.2 = (bf16[48,256]{1,0:T(8,128)(2,1)S(1)}, bf16[48,256]{1,0:T(8,128)(2,1)S(1)}, u32[]{:S(2)}, u32[]{:S(2)}) collective-permute-start(bf16[48,256]{1,0:T(8,128)(2,1)S(1)} %get-tuple-element.37), channel_id=1, source_target_pairs={{0,12},{1,13},{2,14},{3,15},{4,8},{5,9},{6,10},{7,11},{8,4},{9,5},... | collective-permute-start | bytes 73736 | tf_op jit(solution)/shard_map/ppermute | solution.py:385
  9.4 10.2 %collective-permute-start.7 = (bf16[32,1536]{1,0:T(8,128)(2,1)S(1)}, bf16[32,1536]{1,0:T(8,128)(2,1)S(1)}, u32[]{:S(2)}, u32[]{:S(2)}) collective-permute-start(bf16[32,1536]{1,0:T(8,128)(2,1)S(1)} %get-tuple-element.48), channel_id=1, source_target_pairs={{0,2},{1,3},{2,0},{3,1},{4,6},{5,7},{6,4},{7,5},{8,10},{9,11},{10,... | collective-permute-start | bytes 294920 | tf_op jit(solution)/shard_map/ppermute | solution.py:385
  11.1 8.5 %collective-permute-start.8 = (bf16[32,1536]{1,0:T(8,128)(2,1)S(1)}, bf16[32,1536]{1,0:T(8,128)(2,1)S(1)}, u32[]{:S(2)}, u32[]{:S(2)}) collective-permute-start(bf16[32,1536]{1,0:T(8,128)(2,1)S(1)} %get-tuple-element.49), channel_id=1, source_target_pairs={{0,3},{1,2},{2,1},{3,0},{4,7},{5,6},{6,5},{7,4},{8,11},{9,10},{10,... | collective-permute-start | bytes 294920 | tf_op jit(solution)/shard_map/ppermute | solution.py:385
  15.0 5.6 %collective-permute-start.3 = (bf16[32,768]{1,0:T(8,128)(2,1)S(1)}, bf16[32,768]{1,0:T(8,128)(2,1)S(1)}, u32[]{:S(2)}, u32[]{:S(2)}) collective-permute-start(bf16[32,768]{1,0:T(8,128)(2,1)S(1)} %get-tuple-element.39), channel_id=1, source_target_pairs={{0,1},{1,0},{2,3},{3,2},{4,5},{5,4},{6,7},{7,6},{8,9},{9,8},{10,11... | collective-permute-start | bytes 147464 | tf_op jit(solution)/shard_map/ppermute | solution.py:385
  15.1 9.0 %collective-permute-start.4 = (bf16[32,768]{1,0:T(8,128)(2,1)S(1)}, bf16[32,768]{1,0:T(8,128)(2,1)S(1)}, u32[]{:S(2)}, u32[]{:S(2)}) collective-permute-start(bf16[32,768]{1,0:T(8,128)(2,1)S(1)} %get-tuple-element.40), channel_id=1, source_target_pairs={{0,2},{1,3},{2,0},{3,1},{4,6},{5,7},{6,4},{7,5},{8,10},{9,11},{10,... | collective-permute-start | bytes 147464 | tf_op jit(solution)/shard_map/ppermute | solution.py:385
  16.7 7.4 %collective-permute-start.5 = (bf16[32,768]{1,0:T(8,128)(2,1)S(1)}, bf16[32,768]{1,0:T(8,128)(2,1)S(1)}, u32[]{:S(2)}, u32[]{:S(2)}) collective-permute-start(bf16[32,768]{1,0:T(8,128)(2,1)S(1)} %get-tuple-element.41), channel_id=1, source_target_pairs={{0,3},{1,2},{2,1},{3,0},{4,7},{5,6},{6,5},{7,4},{8,11},{9,10},{10,... | collective-permute-start | bytes 147464 | tf_op jit(solution)/shard_map/ppermute | solution.py:385
  19.7 8.5 %collective-permute-start.9 = (bf16[32,1536]{1,0:T(8,128)(2,1)S(1)}, bf16[32,1536]{1,0:T(8,128)(2,1)S(1)}, u32[]{:S(2)}, u32[]{:S(2)}) collective-permute-start(bf16[32,1536]{1,0:T(8,128)(2,1)S(1)} %get-tuple-element.51), channel_id=1, source_target_pairs={{0,4},{1,5},{2,6},{3,7},{4,0},{5,1},{6,2},{7,3},{8,12},{9,13},{10,... | collective-permute-start | bytes 294920 | tf_op jit(solution)/shard_map/ppermute | solution.py:385
  19.7 10.9 %collective-permute-start.10 = (bf16[32,1536]{1,0:T(8,128)(2,1)S(1)}, bf16[32,1536]{1,0:T(8,128)(2,1)S(1)}, u32[]{:S(2)}, u32[]{:S(2)}) collective-permute-start(bf16[32,1536]{1,0:T(8,128)(2,1)S(1)} %get-tuple-element.52), channel_id=1, source_target_pairs={{0,8},{1,9},{2,10},{3,11},{4,12},{5,13},{6,14},{7,15},{8,0},{9,1},... | collective-permute-start | bytes 294920 | tf_op jit(solution)/shard_map/ppermute | solution.py:385
  20.6 10.0 %collective-permute-start.11 = (bf16[32,1536]{1,0:T(8,128)(2,1)S(1)}, bf16[32,1536]{1,0:T(8,128)(2,1)S(1)}, u32[]{:S(2)}, u32[]{:S(2)}) collective-permute-start(bf16[32,1536]{1,0:T(8,128)(2,1)S(1)} %get-tuple-element.53), channel_id=1, source_target_pairs={{0,12},{1,13},{2,14},{3,15},{4,8},{5,9},{6,10},{7,11},{8,4},{9,5},... | collective-permute-start | bytes 294920 | tf_op jit(solution)/shard_map/ppermute | solution.py:385

commit v9 on v8

--- a/solution.py
+++ b/solution.py
@@ -198,18 +198,10 @@
 
 
 def join_kernel(places, w4, b4, wj, *refs):
-    pieces, (begun, last, rows_v, tiles_v, wide_v, acc_v, out_v, sems) = refs[:-8], refs[-8:]
+    pieces, (joined, rows_v, tiles_v, wide_v, acc_v) = refs[:-5], refs[-5:]
     gather_rows(pieces, rows_v)
     widen(rows_v, places, w4, b4, tiles_v, wide_v)
-    stores = []
-    for chunk in range(out_v.shape[0] // 4):
-        rows = pl.ds(4 * chunk, 4)
-        convolve(chunk, wide_v, wj, acc_v, out_v, 4 * chunk)
-        stores.append(pltpu.make_async_copy(out_v.at[rows], begun.at[rows], sems.at[chunk]))
-        stores[-1].start()
-    convolve(out_v.shape[0] // 4, wide_v, wj, acc_v, last, 0)
-    for store in stores:
-        store.wait()
+    convolve(wide_v, wj, acc_v, joined)
 
 
 def gather_rows(pieces, rows_v):
@@ -258,32 +250,30 @@
     fill(3 * tok_dev + 3 * GRID_W, 1, 0, lambda i: 4 * row_count + 1, bottom)
 
 
-def convolve(chunk, wide_v, wj, acc_v, out_v, at):
+def convolve(wide_v, wj, acc_v, out_v):
     feat = wj.shape[2]
-    slot = chunk % 2
+    rows = out_v.shape[0]
     for b in range(4):
         total = None
         for row_tap in range(3):
-            first = (4 * chunk + row_tap) * GRID_W
-            term = matmul(wide_v[first : first + 4 * GRID_W, b * feat : (b + 3) * feat], wj[row_tap])
+            first = row_tap * GRID_W
+            term = matmul(wide_v[first : first + rows * GRID_W, b * feat : (b + 3) * feat], wj[row_tap])
             total = term if total is None else total + term
-        for r in range(4):
+        for r in range(rows):
             for block in range(feat // 128):
-                acc_v[4 * slot + r, block, pl.ds(b, GRID_W, 4), :] = total[
+                acc_v[r, block, pl.ds(b, GRID_W, 4), :] = total[
                     r * GRID_W : (r + 1) * GRID_W, block * 128 : (block + 1) * 128
                 ]
-    for r in range(4):
+    for r in range(rows):
         for block in range(feat // 128):
-            out_v[at + r, :, block * 128 : (block + 1) * 128] = acc_v[4 * slot + r, block].astype(BF16)
-
-
-def rest_kernel(begun, last, places, w2, b2, *refs):
-    del begun
+            out_v[r, :, block * 128 : (block + 1) * 128] = acc_v[r, block].astype(BF16)
+
+
+def rest_kernel(rows_joined, places, w2, b2, *refs):
     arrived, outs = refs[:-9], refs[-9:]
     joined, up_two, same, rows_v, acc_v, out_v, same_v, sems, end_sems = outs
-    tail = joined.shape[0] - last.shape[0]
     ends = [
-        pltpu.make_async_copy(last, joined.at[pl.ds(tail, last.shape[0])], end_sems.at[0]),
+        pltpu.make_async_copy(rows_joined, joined, end_sems.at[0]),
         pltpu.make_async_copy(same_v, same, end_sems.at[1]),
     ]
     ends[0].start()
@@ -430,18 +420,16 @@
 
     out_rows = 4 * row_count
     join_shape = (out_rows, 4 * GRID_W, feat)
-    begun, last = pl.pallas_call(
+    rows_joined = pl.pallas_call(
         join_kernel,
-        out_shape=(pltpu.HBM(join_shape, BF16), pltpu.VMEM((4, 4 * GRID_W, feat), BF16)),
+        out_shape=pltpu.VMEM(join_shape, BF16),
         in_specs=[VMEM] * (4 + low),
-        out_specs=(ANY, VMEM),
+        out_specs=VMEM,
         scratch_shapes=[
             pltpu.VMEM((tok_dev, 3 * c4), BF16),
             pltpu.VMEM((place_rows, c4), BF16),
             pltpu.VMEM(((out_rows + 2) * GRID_W, 6 * c4), BF16),
-            pltpu.VMEM((8, feat // 128, 4 * GRID_W, 128), F32),
-            pltpu.VMEM((out_rows - 4, 4 * GRID_W, feat), BF16),
-            pltpu.SemaphoreType.DMA((row_count - 1,)),
+            pltpu.VMEM((out_rows, feat // 128, 4 * GRID_W, 128), F32),
         ],
         compiler_params=pltpu.CompilerParams(vmem_limit_bytes=20 << 20),
         cost_estimate=pl.CostEstimate(flops=4 << 30, bytes_accessed=4 << 20, transcendentals=0),
@@ -450,7 +438,7 @@
     joined, upsampled_two, same_scale = pl.pallas_call(
         rest_kernel,
         out_shape=(shape(join_shape, BF16), shape((2 * row_count, 2 * GRID_W, c2), BF16), shape((tok_dev, cs), BF16)),
-        in_specs=[ANY] + [VMEM] * (4 + len(rest)),
+        in_specs=[VMEM] * (4 + len(rest)),
         out_specs=(ANY, ANY, ANY),
         scratch_shapes=[
             pltpu.VMEM((tok_dev, c2 + cs), BF16),
@@ -460,11 +448,10 @@
             pltpu.SemaphoreType.DMA((2 * row_count,)),
             pltpu.SemaphoreType.DMA((2,)),
         ],
-        input_output_aliases={0: 0},
         compiler_params=pltpu.CompilerParams(vmem_limit_bytes=12 << 20),
         cost_estimate=pl.CostEstimate(flops=2 << 30, bytes_accessed=4 << 20, transcendentals=0),
         name="rest",
-    )(begun, last, places, w2, b2, *rest)
+    )(rows_joined, places, w2, b2, *rest)
     return (joined, upsampled_two, same_scale.reshape(row_count, GRID_W, cs))
 
 

time: 32.3 us -> 32.3 us (level)
  Pallas kernels: 11.1 us -> 10.5 us
  waiting for transfers between devices: 6.41 us -> 6.95 us
    pallas_call x1, Pallas kernels: 3.98 us -> 3.44 us  [body(): pl.pallas_call(join_kernel, out_shape=pltpu.VMEM(join_shape, BF16), in_sp...]
    ppermute x12, waiting for transfers between devices: 6.41 us -> 6.95 us  [swap(): lax.ppermute(piece, 'rows', [(i, i ^ step * unit) for i in range(shards)])]
  transfers between devices with their start and end apart: 12 -> 12, of which waited for: 3 -> 3; matrix products, arithmetic and copies ran while one was open for 0% -> 0% of each run, Pallas kernels for 21% -> 19%
where the time goes in v9:
time: 32.3 us; the launch traced here: 32.1 us
  starting transfers between devices  13.9 us (43%)
  Pallas kernels  10.5 us (33%)
  waiting for transfers between devices  6.95 us (22%)
  between operations  0.72 us (2%)
    ppermute x12, starting transfers between devices, swap(): lax.ppermute(piece, 'rows', [(i, i ^ step * unit) for i in range(shards)])  13.9 us
    ppermute x12, waiting for transfers between devices, swap(): lax.ppermute(piece, 'rows', [(i, i ^ step * unit) for i in range(shards)])  6.95 us
    pallas_call x1, Pallas kernels, body(): pl.pallas_call(join_kernel, out_shape=pltpu.VMEM(join_shape, BF16), in_sp...  3.44 us
    pallas_call x1, Pallas kernels, body(): pl.pallas_call(functools.partial(project_kernel, low), out_shape=(pltpu.V...  2.93 us
    pallas_call x1, Pallas kernels, body(): pl.pallas_call(fetch_kernel, out_shape=tuple((pltpu.VMEM(w.shape, w.dtype...  2.64 us
    pallas_call x1, Pallas kernels, body(): pl.pallas_call(rest_kernel, out_shape=(shape(join_shape, BF16), shape((2...  1.44 us
  transfers between devices with their start and end apart: 12, of which 3 were waited for; matrix products, arithmetic and copies ran while one was open for 0% of the time, Pallas kernels for 19%

profile of v9, /device:TPU:0, one launch (start us, length us, event | category | flops | bytes accessed | tf_op | source)
XLA Modules:
  0.0 32.1 jit_solution(7870923708198545892)
XLA Ops:
  0.6 2.9 %project.1 = (bf16[896,128]{1,0:T(8,128)(2,1)S(1)}, bf16[48,256]{1,0:T(8,128)(2,1)S(1)}, bf16[48,256]{1,0:T(8,128)(2,1)S(1)}, bf16[48,256]{1,0:T(8,128)(2,1)S(1)...) custom-call(bf16[3,128,1024]{2,1,0:T(8,128)(2,1)} %hidden.1, ...), custom_call_target="tpu_custom_call" | custom-call | flops 469762048 | bytes 5242880 | tf_op jit(solution)/shard_map/project/pallas_call | solution.py:349
  3.6 0.6 %collective-permute-start.6 = (bf16[32,1536]{1,0:T(8,128)(2,1)S(1)}, bf16[32,1536]{1,0:T(8,128)(2,1)S(1)}, u32[]{:S(2)}, u32[]{:S(2)}) collective-permute-start(bf16[32,1536]{1,0:T(8,128)(2,1)S(1)} %get-tuple-element.43), channel_id=1, source_target_pairs={{0,1},{1,0},{2,3},{3,2},{4,5},{5,4},{6,7},{7,6},{8,9},{9,8},{10,11... | collective-permute-start | bytes 294920 | tf_op jit(solution)/shard_map/ppermute | solution.py:375
  4.1 2.6 %collective-permute-start = (bf16[48,256]{1,0:T(8,128)(2,1)S(1)}, bf16[48,256]{1,0:T(8,128)(2,1)S(1)}, u32[]{:S(2)}, u32[]{:S(2)}) collective-permute-start(bf16[48,256]{1,0:T(8,128)(2,1)S(1)} %get-tuple-element.33), channel_id=1, source_target_pairs={{0,4},{1,5},{2,6},{3,7},{4,0},{5,1},{6,2},{7,3},{8,12},{9,13},{10,... | collective-permute-start | bytes 73736 | tf_op jit(solution)/shard_map/ppermute | solution.py:375
  6.8 2.6 %collective-permute-start.1 = (bf16[48,256]{1,0:T(8,128)(2,1)S(1)}, bf16[48,256]{1,0:T(8,128)(2,1)S(1)}, u32[]{:S(2)}, u32[]{:S(2)}) collective-permute-start(bf16[48,256]{1,0:T(8,128)(2,1)S(1)} %get-tuple-element.34), channel_id=1, source_target_pairs={{0,8},{1,9},{2,10},{3,11},{4,12},{5,13},{6,14},{7,15},{8,0},{9,1},... | collective-permute-start | bytes 73736 | tf_op jit(solution)/shard_map/ppermute | solution.py:375
  9.4 0.0 collective-permute-start.2
  9.4 1.7 %collective-permute-start.7 = (bf16[32,1536]{1,0:T(8,128)(2,1)S(1)}, bf16[32,1536]{1,0:T(8,128)(2,1)S(1)}, u32[]{:S(2)}, u32[]{:S(2)}) collective-permute-start(bf16[32,1536]{1,0:T(8,128)(2,1)S(1)} %get-tuple-element.44), channel_id=1, source_target_pairs={{0,2},{1,3},{2,0},{3,1},{4,6},{5,7},{6,4},{7,5},{8,10},{9,11},{10,... | collective-permute-start | bytes 294920 | tf_op jit(solution)/shard_map/ppermute | solution.py:375
  11.1 0.0 collective-permute-done.refs_1_
  11.1 0.5 %collective-permute-done.1.refs_2_ = bf16[48,256]{1,0:T(8,128)(2,1)S(1)} collective-permute-done((bf16[48,256]{1,0:T(8,128)(2,1)S(1)}, bf16[48,256]{1,0:T(8,128)(2,1)S(1)}, u32[]{:S(2)}, u32[]{:S(2)}) %collective-permute-start.1) | collective-permute-done | bytes 24608 | tf_op jit(solution)/shard_map/ppermute | solution.py:375
  11.6 3.4 %collective-permute-done.2.refs_3_ = bf16[48,256]{1,0:T(8,128)(2,1)S(1)} collective-permute-done((bf16[48,256]{1,0:T(8,128)(2,1)S(1)}, bf16[48,256]{1,0:T(8,128)(2,1)S(1)}, u32[]{:S(2)}, u32[]{:S(2)}) %collective-permute-start.2) | collective-permute-done | bytes 24608 | tf_op jit(solution)/shard_map/ppermute | solution.py:375
  15.0 0.1 collective-permute-start.3
  15.1 1.6 %collective-permute-start.4 = (bf16[32,768]{1,0:T(8,128)(2,1)S(1)}, bf16[32,768]{1,0:T(8,128)(2,1)S(1)}, u32[]{:S(2)}, u32[]{:S(2)}) collective-permute-start(bf16[32,768]{1,0:T(8,128)(2,1)S(1)} %get-tuple-element.38), channel_id=1, source_target_pairs={{0,2},{1,3},{2,0},{3,1},{4,6},{5,7},{6,4},{7,5},{8,10},{9,11},{10,... | collective-permute-start | bytes 147464 | tf_op jit(solution)/shard_map/ppermute | solution.py:375
  16.7 0.0 collective-permute-done.6.refs_1_
  16.7 0.3 collective-permute-start.5
  17.0 2.6 %fetch.1 = (bf16[256,4096]{1,0:T(8,128)(2,1)S(1)}, f32[1,256]{1,0:T(1,128)S(1)}, bf16[3,768,256]{2,1,0:T(8,128)(2,1)S(1)}, bf16[512,2048]{1,0:T(8,128)(2,1)S(1)}, f32[1,512]{1,0:T(1,128)S(1)}) custom-call(bf16[256,4096]{1,0:T(8,128)(2,1)} %refs_0_.1, f32[1,256]{1,0:T(1,128)} %bitcast.14, bf16[3,768,256]{2,1,0:T(8,128)(2,1)} %bitcast.8, ...), custom_call_target="tpu_custom_call" | custom-call | flops 1073741824 | bytes 5242880 | tf_op jit(solution)/shard_map/fetch/pallas_call | solution.py:410
  19.6 0.0 collective-permute-done.7.refs_2_
  19.6 0.0 collective-permute-done.8.refs_3_
  19.7 0.1 collective-permute-start.9
  19.7 0.9 %collective-permute-start.10 = (bf16[32,1536]{1,0:T(8,128)(2,1)S(1)}, bf16[32,1536]{1,0:T(8,128)(2,1)S(1)}, u32[]{:S(2)}, u32[]{:S(2)}) collective-permute-start(bf16[32,1536]{1,0:T(8,128)(2,1)S(1)} %get-tuple-element.48), channel_id=1, source_target_pairs={{0,8},{1,9},{2,10},{3,11},{4,12},{5,13},{6,14},{7,15},{8,0},{9,1},... | collective-permute-start | bytes 294920 | tf_op jit(solution)/shard_map/ppermute | solution.py:375
  20.6 0.0 collective-permute-done.3.refs_1_
  20.6 3.5 %collective-permute-start.11 = (bf16[32,1536]{1,0:T(8,128)(2,1)S(1)}, bf16[32,1536]{1,0:T(8,128)(2,1)S(1)}, u32[]{:S(2)}, u32[]{:S(2)}) collective-permute-start(bf16[32,1536]{1,0:T(8,128)(2,1)S(1)} %get-tuple-element.49), channel_id=1, source_target_pairs={{0,12},{1,13},{2,14},{3,15},{4,8},{5,9},{6,10},{7,11},{8,4},{9,5},... | collective-permute-start | bytes 294920 | tf_op jit(solution)/shard_map/ppermute | solution.py:375
  24.1 0.0 collective-permute-done.4.refs_2_
  24.1 3.4 %join.1.rows_joined = bf16[8,256,256]{2,1,0:T(8,128)(2,1)S(1)} custom-call(bf16[896,128]{1,0:T(8,128)(2,1)S(1)} %get-tuple-element.28.places, bf16[256,4096]{1,0:T(8,128)(2,1)S(1)} %get-tuple-element.29.w4, f32[1,256]{1,0:T(1,128)S(1)} %get-tuple-element.30.b4, bf16[3,768,256]{2,1,0:T(8,128)(2,1)S(1)} %get-tuple-element.31.wj, ...), custom_call_target="tpu_custom_call" | custom-call | flops 4294967296 | bytes 4194304 | tf_op jit(solution)/shard_map/join/pallas_call | solution.py:423
  27.6 3.0 %collective-permute-done.10.refs_2_ = bf16[32,1536]{1,0:T(8,128)(2,1)S(1)} collective-permute-done((bf16[32,1536]{1,0:T(8,128)(2,1)S(1)}, bf16[32,1536]{1,0:T(8,128)(2,1)S(1)}, u32[]{:S(2)}, u32[]{:S(2)}) %collective-permute-start.10) | collective-permute-done | bytes 98336 | tf_op jit(solution)/shard_map/ppermute | solution.py:375
  30.6 1.4 %rest.1 = (bf16[8,256,256]{2,1,0:T(8,128)(2,1)}, bf16[4,128,512]{2,1,0:T(8,128)(2,1)}, bf16[128,1024]{1,0:T(8,128)(2,1)}) custom-call(bf16[8,256,256]{2,1,0:T(8,128)(2,1)S(1)} %join.1.rows_joined, bf16[896,128]{1,0:T(8,128)(2,1)S(1)} %get-tuple-element.28.places, bf16[512,2048]{1,0:T(8,128)(2,1)S(1)} %get-tuple-element.40.w2, ...), custom_call_target="tpu_custom_call" | custom-call | flops 2147483648 | bytes 4194304 | tf_op jit(solution)/shard_map/rest/pallas_call | solution.py:438
  (6 shorter events, 0.1 us)
Async XLA Ops:
  3.6 13.1 %collective-permute-start.6 = (bf16[32,1536]{1,0:T(8,128)(2,1)S(1)}, bf16[32,1536]{1,0:T(8,128)(2,1)S(1)}, u32[]{:S(2)}, u32[]{:S(2)}) collective-permute-start(bf16[32,1536]{1,0:T(8,128)(2,1)S(1)} %get-tuple-element.43), channel_id=1, source_target_pairs={{0,1},{1,0},{2,3},{3,2},{4,5},{5,4},{6,7},{7,6},{8,9},{9,8},{10,11... | collective-permute-start | bytes 294920 | tf_op jit(solution)/shard_map/ppermute | solution.py:375
  4.1 7.0 %collective-permute-start = (bf16[48,256]{1,0:T(8,128)(2,1)S(1)}, bf16[48,256]{1,0:T(8,128)(2,1)S(1)}, u32[]{:S(2)}, u32[]{:S(2)}) collective-permute-start(bf16[48,256]{1,0:T(8,128)(2,1)S(1)} %get-tuple-element.33), channel_id=1, source_target_pairs={{0,4},{1,5},{2,6},{3,7},{4,0},{5,1},{6,2},{7,3},{8,12},{9,13},{10,... | collective-permute-start | bytes 73736 | tf_op jit(solution)/shard_map/ppermute | solution.py:375
  6.8 4.8 %collective-permute-start.1 = (bf16[48,256]{1,0:T(8,128)(2,1)S(1)}, bf16[48,256]{1,0:T(8,128)(2,1)S(1)}, u32[]{:S(2)}, u32[]{:S(2)}) collective-permute-start(bf16[48,256]{1,0:T(8,128)(2,1)S(1)} %get-tuple-element.34), channel_id=1, source_target_pairs={{0,8},{1,9},{2,10},{3,11},{4,12},{5,13},{6,14},{7,15},{8,0},{9,1},... | collective-permute-start | bytes 73736 | tf_op jit(solution)/shard_map/ppermute | solution.py:375
  9.4 5.6 %collective-permute-start.2 = (bf16[48,256]{1,0:T(8,128)(2,1)S(1)}, bf16[48,256]{1,0:T(8,128)(2,1)S(1)}, u32[]{:S(2)}, u32[]{:S(2)}) collective-permute-start(bf16[48,256]{1,0:T(8,128)(2,1)S(1)} %get-tuple-element.35), channel_id=1, source_target_pairs={{0,12},{1,13},{2,14},{3,15},{4,8},{5,9},{6,10},{7,11},{8,4},{9,5},... | collective-permute-start | bytes 73736 | tf_op jit(solution)/shard_map/ppermute | solution.py:375
  9.4 10.2 %collective-permute-start.7 = (bf16[32,1536]{1,0:T(8,128)(2,1)S(1)}, bf16[32,1536]{1,0:T(8,128)(2,1)S(1)}, u32[]{:S(2)}, u32[]{:S(2)}) collective-permute-start(bf16[32,1536]{1,0:T(8,128)(2,1)S(1)} %get-tuple-element.44), channel_id=1, source_target_pairs={{0,2},{1,3},{2,0},{3,1},{4,6},{5,7},{6,4},{7,5},{8,10},{9,11},{10,... | collective-permute-start | bytes 294920 | tf_op jit(solution)/shard_map/ppermute | solution.py:375
  11.1 8.5 %collective-permute-start.8 = (bf16[32,1536]{1,0:T(8,128)(2,1)S(1)}, bf16[32,1536]{1,0:T(8,128)(2,1)S(1)}, u32[]{:S(2)}, u32[]{:S(2)}) collective-permute-start(bf16[32,1536]{1,0:T(8,128)(2,1)S(1)} %get-tuple-element.45), channel_id=1, source_target_pairs={{0,3},{1,2},{2,1},{3,0},{4,7},{5,6},{6,5},{7,4},{8,11},{9,10},{10,... | collective-permute-start | bytes 294920 | tf_op jit(solution)/shard_map/ppermute | solution.py:375
  15.0 5.6 %collective-permute-start.3 = (bf16[32,768]{1,0:T(8,128)(2,1)S(1)}, bf16[32,768]{1,0:T(8,128)(2,1)S(1)}, u32[]{:S(2)}, u32[]{:S(2)}) collective-permute-start(bf16[32,768]{1,0:T(8,128)(2,1)S(1)} %get-tuple-element.37), channel_id=1, source_target_pairs={{0,1},{1,0},{2,3},{3,2},{4,5},{5,4},{6,7},{7,6},{8,9},{9,8},{10,11... | collective-permute-start | bytes 147464 | tf_op jit(solution)/shard_map/ppermute | solution.py:375
  15.1 9.0 %collective-permute-start.4 = (bf16[32,768]{1,0:T(8,128)(2,1)S(1)}, bf16[32,768]{1,0:T(8,128)(2,1)S(1)}, u32[]{:S(2)}, u32[]{:S(2)}) collective-permute-start(bf16[32,768]{1,0:T(8,128)(2,1)S(1)} %get-tuple-element.38), channel_id=1, source_target_pairs={{0,2},{1,3},{2,0},{3,1},{4,6},{5,7},{6,4},{7,5},{8,10},{9,11},{10,... | collective-permute-start | bytes 147464 | tf_op jit(solution)/shard_map/ppermute | solution.py:375
  16.7 7.4 %collective-permute-start.5 = (bf16[32,768]{1,0:T(8,128)(2,1)S(1)}, bf16[32,768]{1,0:T(8,128)(2,1)S(1)}, u32[]{:S(2)}, u32[]{:S(2)}) collective-permute-start(bf16[32,768]{1,0:T(8,128)(2,1)S(1)} %get-tuple-element.39), channel_id=1, source_target_pairs={{0,3},{1,2},{2,1},{3,0},{4,7},{5,6},{6,5},{7,4},{8,11},{9,10},{10,... | collective-permute-start | bytes 147464 | tf_op jit(solution)/shard_map/ppermute | solution.py:375
  19.7 7.9 %collective-permute-start.9 = (bf16[32,1536]{1,0:T(8,128)(2,1)S(1)}, bf16[32,1536]{1,0:T(8,128)(2,1)S(1)}, u32[]{:S(2)}, u32[]{:S(2)}) collective-permute-start(bf16[32,1536]{1,0:T(8,128)(2,1)S(1)} %get-tuple-element.47), channel_id=1, source_target_pairs={{0,4},{1,5},{2,6},{3,7},{4,0},{5,1},{6,2},{7,3},{8,12},{9,13},{10,... | collective-permute-start | bytes 294920 | tf_op jit(solution)/shard_map/ppermute | solution.py:375
  19.7 10.9 %collective-permute-start.10 = (bf16[32,1536]{1,0:T(8,128)(2,1)S(1)}, bf16[32,1536]{1,0:T(8,128)(2,1)S(1)}, u32[]{:S(2)}, u32[]{:S(2)}) collective-permute-start(bf16[32,1536]{1,0:T(8,128)(2,1)S(1)} %get-tuple-element.48), channel_id=1, source_target_pairs={{0,8},{1,9},{2,10},{3,11},{4,12},{5,13},{6,14},{7,15},{8,0},{9,1},... | collective-permute-start | bytes 294920 | tf_op jit(solution)/shard_map/ppermute | solution.py:375
  20.6 10.0 %collective-permute-start.11 = (bf16[32,1536]{1,0:T(8,128)(2,1)S(1)}, bf16[32,1536]{1,0:T(8,128)(2,1)S(1)}, u32[]{:S(2)}, u32[]{:S(2)}) collective-permute-start(bf16[32,1536]{1,0:T(8,128)(2,1)S(1)} %get-tuple-element.49), channel_id=1, source_target_pairs={{0,12},{1,13},{2,14},{3,15},{4,8},{5,9},{6,10},{7,11},{8,4},{9,5},... | collective-permute-start | bytes 294920 | tf_op jit(solution)/shard_map/ppermute | solution.py:375

commit v10 on v9

--- a/solution.py
+++ b/solution.py
@@ -282,10 +282,11 @@
     c2 = w2.shape[0]
     row_count = tok_dev // GRID_W
     place = places[places.shape[0] - tok_dev :]
-    same_v[...] = matmul(place, rows_v[:, c2:]).astype(BF16)
+    placed = matmul(place, rows_v[...]).astype(BF16)
+    same_v[...] = placed[:, c2:]
     ends[1].start()
     stores = [*ends]
-    tile = matmul(place, rows_v[:, 0:c2]).astype(BF16)
+    tile = placed[:, 0:c2]
     bias = b2[...]
     for a in range(2):
         for b in range(2):

time: 32.3 us -> 32.2 us (level)
  no operation moved by 1% of the time
where the time goes in v10:
time: 32.2 us; the launch traced here: 32 us
  starting transfers between devices  13.9 us (43%)
  Pallas kernels  10.4 us (32%)
  waiting for transfers between devices  6.95 us (22%)
  between operations  0.72 us (2%)
    ppermute x12, starting transfers between devices, swap(): lax.ppermute(piece, 'rows', [(i, i ^ step * unit) for i in range(shards)])  13.9 us
    ppermute x12, waiting for transfers between devices, swap(): lax.ppermute(piece, 'rows', [(i, i ^ step * unit) for i in range(shards)])  6.95 us
    pallas_call x1, Pallas kernels, body(): pl.pallas_call(join_kernel, out_shape=pltpu.VMEM(join_shape, BF16), in_sp...  3.44 us
    pallas_call x1, Pallas kernels, body(): pl.pallas_call(functools.partial(project_kernel, low), out_shape=(pltpu.V...  2.93 us
    pallas_call x1, Pallas kernels, body(): pl.pallas_call(fetch_kernel, out_shape=tuple((pltpu.VMEM(w.shape, w.dtype...  2.64 us
    pallas_call x1, Pallas kernels, body(): pl.pallas_call(rest_kernel, out_shape=(shape(join_shape, BF16), shape((2...  1.34 us
  transfers between devices with their start and end apart: 12, of which 3 were waited for; matrix products, arithmetic and copies ran while one was open for 0% of the time, Pallas kernels for 19%

profile of v10, /device:TPU:0, one launch (start us, length us, event | category | flops | bytes accessed | tf_op | source)
XLA Modules:
  0.0 32.0 jit_solution(15124966819712352563)
XLA Ops:
  0.6 2.9 %project.1 = (bf16[896,128]{1,0:T(8,128)(2,1)S(1)}, bf16[48,256]{1,0:T(8,128)(2,1)S(1)}, bf16[48,256]{1,0:T(8,128)(2,1)S(1)}, bf16[48,256]{1,0:T(8,128)(2,1)S(1)...) custom-call(bf16[3,128,1024]{2,1,0:T(8,128)(2,1)} %hidden.1, ...), custom_call_target="tpu_custom_call" | custom-call | flops 469762048 | bytes 5242880 | tf_op jit(solution)/shard_map/project/pallas_call | solution.py:350
  3.6 0.6 %collective-permute-start.6 = (bf16[32,1536]{1,0:T(8,128)(2,1)S(1)}, bf16[32,1536]{1,0:T(8,128)(2,1)S(1)}, u32[]{:S(2)}, u32[]{:S(2)}) collective-permute-start(bf16[32,1536]{1,0:T(8,128)(2,1)S(1)} %get-tuple-element.43), channel_id=1, source_target_pairs={{0,1},{1,0},{2,3},{3,2},{4,5},{5,4},{6,7},{7,6},{8,9},{9,8},{10,11... | collective-permute-start | bytes 294920 | tf_op jit(solution)/shard_map/ppermute | solution.py:376
  4.1 2.6 %collective-permute-start = (bf16[48,256]{1,0:T(8,128)(2,1)S(1)}, bf16[48,256]{1,0:T(8,128)(2,1)S(1)}, u32[]{:S(2)}, u32[]{:S(2)}) collective-permute-start(bf16[48,256]{1,0:T(8,128)(2,1)S(1)} %get-tuple-element.33), channel_id=1, source_target_pairs={{0,4},{1,5},{2,6},{3,7},{4,0},{5,1},{6,2},{7,3},{8,12},{9,13},{10,... | collective-permute-start | bytes 73736 | tf_op jit(solution)/shard_map/ppermute | solution.py:376
  6.8 2.6 %collective-permute-start.1 = (bf16[48,256]{1,0:T(8,128)(2,1)S(1)}, bf16[48,256]{1,0:T(8,128)(2,1)S(1)}, u32[]{:S(2)}, u32[]{:S(2)}) collective-permute-start(bf16[48,256]{1,0:T(8,128)(2,1)S(1)} %get-tuple-element.34), channel_id=1, source_target_pairs={{0,8},{1,9},{2,10},{3,11},{4,12},{5,13},{6,14},{7,15},{8,0},{9,1},... | collective-permute-start | bytes 73736 | tf_op jit(solution)/shard_map/ppermute | solution.py:376
  9.4 0.0 collective-permute-start.2
  9.4 1.7 %collective-permute-start.7 = (bf16[32,1536]{1,0:T(8,128)(2,1)S(1)}, bf16[32,1536]{1,0:T(8,128)(2,1)S(1)}, u32[]{:S(2)}, u32[]{:S(2)}) collective-permute-start(bf16[32,1536]{1,0:T(8,128)(2,1)S(1)} %get-tuple-element.44), channel_id=1, source_target_pairs={{0,2},{1,3},{2,0},{3,1},{4,6},{5,7},{6,4},{7,5},{8,10},{9,11},{10,... | collective-permute-start | bytes 294920 | tf_op jit(solution)/shard_map/ppermute | solution.py:376
  11.1 0.0 collective-permute-done.refs_1_
  11.1 0.5 %collective-permute-done.1.refs_2_ = bf16[48,256]{1,0:T(8,128)(2,1)S(1)} collective-permute-done((bf16[48,256]{1,0:T(8,128)(2,1)S(1)}, bf16[48,256]{1,0:T(8,128)(2,1)S(1)}, u32[]{:S(2)}, u32[]{:S(2)}) %collective-permute-start.1) | collective-permute-done | bytes 24608 | tf_op jit(solution)/shard_map/ppermute | solution.py:376
  11.6 3.4 %collective-permute-done.2.refs_3_ = bf16[48,256]{1,0:T(8,128)(2,1)S(1)} collective-permute-done((bf16[48,256]{1,0:T(8,128)(2,1)S(1)}, bf16[48,256]{1,0:T(8,128)(2,1)S(1)}, u32[]{:S(2)}, u32[]{:S(2)}) %collective-permute-start.2) | collective-permute-done | bytes 24608 | tf_op jit(solution)/shard_map/ppermute | solution.py:376
  15.0 0.1 collective-permute-start.3
  15.1 1.6 %collective-permute-start.4 = (bf16[32,768]{1,0:T(8,128)(2,1)S(1)}, bf16[32,768]{1,0:T(8,128)(2,1)S(1)}, u32[]{:S(2)}, u32[]{:S(2)}) collective-permute-start(bf16[32,768]{1,0:T(8,128)(2,1)S(1)} %get-tuple-element.38), channel_id=1, source_target_pairs={{0,2},{1,3},{2,0},{3,1},{4,6},{5,7},{6,4},{7,5},{8,10},{9,11},{10,... | collective-permute-start | bytes 147464 | tf_op jit(solution)/shard_map/ppermute | solution.py:376
  16.7 0.0 collective-permute-done.6.refs_1_
  16.7 0.3 collective-permute-start.5
  17.0 2.6 %fetch.1 = (bf16[256,4096]{1,0:T(8,128)(2,1)S(1)}, f32[1,256]{1,0:T(1,128)S(1)}, bf16[3,768,256]{2,1,0:T(8,128)(2,1)S(1)}, bf16[512,2048]{1,0:T(8,128)(2,1)S(1)}, f32[1,512]{1,0:T(1,128)S(1)}) custom-call(bf16[256,4096]{1,0:T(8,128)(2,1)} %refs_0_.1, f32[1,256]{1,0:T(1,128)} %bitcast.14, bf16[3,768,256]{2,1,0:T(8,128)(2,1)} %bitcast.8, ...), custom_call_target="tpu_custom_call" | custom-call | flops 1073741824 | bytes 5242880 | tf_op jit(solution)/shard_map/fetch/pallas_call | solution.py:411
  19.6 0.0 collective-permute-done.7.refs_2_
  19.6 0.0 collective-permute-done.8.refs_3_
  19.7 0.1 collective-permute-start.9
  19.7 0.9 %collective-permute-start.10 = (bf16[32,1536]{1,0:T(8,128)(2,1)S(1)}, bf16[32,1536]{1,0:T(8,128)(2,1)S(1)}, u32[]{:S(2)}, u32[]{:S(2)}) collective-permute-start(bf16[32,1536]{1,0:T(8,128)(2,1)S(1)} %get-tuple-element.48), channel_id=1, source_target_pairs={{0,8},{1,9},{2,10},{3,11},{4,12},{5,13},{6,14},{7,15},{8,0},{9,1},... | collective-permute-start | bytes 294920 | tf_op jit(solution)/shard_map/ppermute | solution.py:376
  20.6 0.0 collective-permute-done.3.refs_1_
  20.6 3.5 %collective-permute-start.11 = (bf16[32,1536]{1,0:T(8,128)(2,1)S(1)}, bf16[32,1536]{1,0:T(8,128)(2,1)S(1)}, u32[]{:S(2)}, u32[]{:S(2)}) collective-permute-start(bf16[32,1536]{1,0:T(8,128)(2,1)S(1)} %get-tuple-element.49), channel_id=1, source_target_pairs={{0,12},{1,13},{2,14},{3,15},{4,8},{5,9},{6,10},{7,11},{8,4},{9,5},... | collective-permute-start | bytes 294920 | tf_op jit(solution)/shard_map/ppermute | solution.py:376
  24.1 0.0 collective-permute-done.4.refs_2_
  24.1 3.4 %join.1.rows_joined = bf16[8,256,256]{2,1,0:T(8,128)(2,1)S(1)} custom-call(bf16[896,128]{1,0:T(8,128)(2,1)S(1)} %get-tuple-element.28.places, bf16[256,4096]{1,0:T(8,128)(2,1)S(1)} %get-tuple-element.29.w4, f32[1,256]{1,0:T(1,128)S(1)} %get-tuple-element.30.b4, bf16[3,768,256]{2,1,0:T(8,128)(2,1)S(1)} %get-tuple-element.31.wj, ...), custom_call_target="tpu_custom_call" | custom-call | flops 4294967296 | bytes 4194304 | tf_op jit(solution)/shard_map/join/pallas_call | solution.py:424
  27.6 3.0 %collective-permute-done.10.refs_2_ = bf16[32,1536]{1,0:T(8,128)(2,1)S(1)} collective-permute-done((bf16[32,1536]{1,0:T(8,128)(2,1)S(1)}, bf16[32,1536]{1,0:T(8,128)(2,1)S(1)}, u32[]{:S(2)}, u32[]{:S(2)}) %collective-permute-start.10) | collective-permute-done | bytes 98336 | tf_op jit(solution)/shard_map/ppermute | solution.py:376
  30.6 1.3 %rest.1 = (bf16[8,256,256]{2,1,0:T(8,128)(2,1)}, bf16[4,128,512]{2,1,0:T(8,128)(2,1)}, bf16[128,1024]{1,0:T(8,128)(2,1)}) custom-call(bf16[8,256,256]{2,1,0:T(8,128)(2,1)S(1)} %join.1.rows_joined, bf16[896,128]{1,0:T(8,128)(2,1)S(1)} %get-tuple-element.28.places, bf16[512,2048]{1,0:T(8,128)(2,1)S(1)} %get-tuple-element.40.w2, ...), custom_call_target="tpu_custom_call" | custom-call | flops 2147483648 | bytes 4194304 | tf_op jit(solution)/shard_map/rest/pallas_call | solution.py:439
  (6 shorter events, 0.1 us)
Async XLA Ops:
  3.6 13.1 %collective-permute-start.6 = (bf16[32,1536]{1,0:T(8,128)(2,1)S(1)}, bf16[32,1536]{1,0:T(8,128)(2,1)S(1)}, u32[]{:S(2)}, u32[]{:S(2)}) collective-permute-start(bf16[32,1536]{1,0:T(8,128)(2,1)S(1)} %get-tuple-element.43), channel_id=1, source_target_pairs={{0,1},{1,0},{2,3},{3,2},{4,5},{5,4},{6,7},{7,6},{8,9},{9,8},{10,11... | collective-permute-start | bytes 294920 | tf_op jit(solution)/shard_map/ppermute | solution.py:376
  4.1 7.0 %collective-permute-start = (bf16[48,256]{1,0:T(8,128)(2,1)S(1)}, bf16[48,256]{1,0:T(8,128)(2,1)S(1)}, u32[]{:S(2)}, u32[]{:S(2)}) collective-permute-start(bf16[48,256]{1,0:T(8,128)(2,1)S(1)} %get-tuple-element.33), channel_id=1, source_target_pairs={{0,4},{1,5},{2,6},{3,7},{4,0},{5,1},{6,2},{7,3},{8,12},{9,13},{10,... | collective-permute-start | bytes 73736 | tf_op jit(solution)/shard_map/ppermute | solution.py:376
  6.8 4.8 %collective-permute-start.1 = (bf16[48,256]{1,0:T(8,128)(2,1)S(1)}, bf16[48,256]{1,0:T(8,128)(2,1)S(1)}, u32[]{:S(2)}, u32[]{:S(2)}) collective-permute-start(bf16[48,256]{1,0:T(8,128)(2,1)S(1)} %get-tuple-element.34), channel_id=1, source_target_pairs={{0,8},{1,9},{2,10},{3,11},{4,12},{5,13},{6,14},{7,15},{8,0},{9,1},... | collective-permute-start | bytes 73736 | tf_op jit(solution)/shard_map/ppermute | solution.py:376
  9.4 5.6 %collective-permute-start.2 = (bf16[48,256]{1,0:T(8,128)(2,1)S(1)}, bf16[48,256]{1,0:T(8,128)(2,1)S(1)}, u32[]{:S(2)}, u32[]{:S(2)}) collective-permute-start(bf16[48,256]{1,0:T(8,128)(2,1)S(1)} %get-tuple-element.35), channel_id=1, source_target_pairs={{0,12},{1,13},{2,14},{3,15},{4,8},{5,9},{6,10},{7,11},{8,4},{9,5},... | collective-permute-start | bytes 73736 | tf_op jit(solution)/shard_map/ppermute | solution.py:376
  9.4 10.2 %collective-permute-start.7 = (bf16[32,1536]{1,0:T(8,128)(2,1)S(1)}, bf16[32,1536]{1,0:T(8,128)(2,1)S(1)}, u32[]{:S(2)}, u32[]{:S(2)}) collective-permute-start(bf16[32,1536]{1,0:T(8,128)(2,1)S(1)} %get-tuple-element.44), channel_id=1, source_target_pairs={{0,2},{1,3},{2,0},{3,1},{4,6},{5,7},{6,4},{7,5},{8,10},{9,11},{10,... | collective-permute-start | bytes 294920 | tf_op jit(solution)/shard_map/ppermute | solution.py:376
  11.1 8.5 %collective-permute-start.8 = (bf16[32,1536]{1,0:T(8,128)(2,1)S(1)}, bf16[32,1536]{1,0:T(8,128)(2,1)S(1)}, u32[]{:S(2)}, u32[]{:S(2)}) collective-permute-start(bf16[32,1536]{1,0:T(8,128)(2,1)S(1)} %get-tuple-element.45), channel_id=1, source_target_pairs={{0,3},{1,2},{2,1},{3,0},{4,7},{5,6},{6,5},{7,4},{8,11},{9,10},{10,... | collective-permute-start | bytes 294920 | tf_op jit(solution)/shard_map/ppermute | solution.py:376
  15.0 5.6 %collective-permute-start.3 = (bf16[32,768]{1,0:T(8,128)(2,1)S(1)}, bf16[32,768]{1,0:T(8,128)(2,1)S(1)}, u32[]{:S(2)}, u32[]{:S(2)}) collective-permute-start(bf16[32,768]{1,0:T(8,128)(2,1)S(1)} %get-tuple-element.37), channel_id=1, source_target_pairs={{0,1},{1,0},{2,3},{3,2},{4,5},{5,4},{6,7},{7,6},{8,9},{9,8},{10,11... | collective-permute-start | bytes 147464 | tf_op jit(solution)/shard_map/ppermute | solution.py:376
  15.1 9.0 %collective-permute-start.4 = (bf16[32,768]{1,0:T(8,128)(2,1)S(1)}, bf16[32,768]{1,0:T(8,128)(2,1)S(1)}, u32[]{:S(2)}, u32[]{:S(2)}) collective-permute-start(bf16[32,768]{1,0:T(8,128)(2,1)S(1)} %get-tuple-element.38), channel_id=1, source_target_pairs={{0,2},{1,3},{2,0},{3,1},{4,6},{5,7},{6,4},{7,5},{8,10},{9,11},{10,... | collective-permute-start | bytes 147464 | tf_op jit(solution)/shard_map/ppermute | solution.py:376
  16.7 7.4 %collective-permute-start.5 = (bf16[32,768]{1,0:T(8,128)(2,1)S(1)}, bf16[32,768]{1,0:T(8,128)(2,1)S(1)}, u32[]{:S(2)}, u32[]{:S(2)}) collective-permute-start(bf16[32,768]{1,0:T(8,128)(2,1)S(1)} %get-tuple-element.39), channel_id=1, source_target_pairs={{0,3},{1,2},{2,1},{3,0},{4,7},{5,6},{6,5},{7,4},{8,11},{9,10},{10,... | collective-permute-start | bytes 147464 | tf_op jit(solution)/shard_map/ppermute | solution.py:376
  19.7 7.9 %collective-permute-start.9 = (bf16[32,1536]{1,0:T(8,128)(2,1)S(1)}, bf16[32,1536]{1,0:T(8,128)(2,1)S(1)}, u32[]{:S(2)}, u32[]{:S(2)}) collective-permute-start(bf16[32,1536]{1,0:T(8,128)(2,1)S(1)} %get-tuple-element.47), channel_id=1, source_target_pairs={{0,4},{1,5},{2,6},{3,7},{4,0},{5,1},{6,2},{7,3},{8,12},{9,13},{10,... | collective-permute-start | bytes 294920 | tf_op jit(solution)/shard_map/ppermute | solution.py:376
  19.7 10.9 %collective-permute-start.10 = (bf16[32,1536]{1,0:T(8,128)(2,1)S(1)}, bf16[32,1536]{1,0:T(8,128)(2,1)S(1)}, u32[]{:S(2)}, u32[]{:S(2)}) collective-permute-start(bf16[32,1536]{1,0:T(8,128)(2,1)S(1)} %get-tuple-element.48), channel_id=1, source_target_pairs={{0,8},{1,9},{2,10},{3,11},{4,12},{5,13},{6,14},{7,15},{8,0},{9,1},... | collective-permute-start | bytes 294920 | tf_op jit(solution)/shard_map/ppermute | solution.py:376
  20.6 10.0 %collective-permute-start.11 = (bf16[32,1536]{1,0:T(8,128)(2,1)S(1)}, bf16[32,1536]{1,0:T(8,128)(2,1)S(1)}, u32[]{:S(2)}, u32[]{:S(2)}) collective-permute-start(bf16[32,1536]{1,0:T(8,128)(2,1)S(1)} %get-tuple-element.49), channel_id=1, source_target_pairs={{0,12},{1,13},{2,14},{3,15},{4,8},{5,9},{6,10},{7,11},{8,4},{9,5},... | collective-permute-start | bytes 294920 | tf_op jit(solution)/shard_map/ppermute | solution.py:376
